TPU v7x, 32 devices: a whole 2x2x4 slice. The times are simulated.
32 devices in a mesh: dp: 8 (over y, x, core), tensor: 4 (over z).
Axes of the slice: x: 2, y: 2, z: 4, core: 2. Of those that a mesh axis runs over, the one named last changes fastest.
Arguments:
- tokens: bfloat16 [16384, 1024], P(('dp', 'tensor')), may hold values from -6 to 6
- weight_query: bfloat16 [1024, 1024], P('dp', 'tensor'), may hold values from -0.375 to 0.375
- weight_key: bfloat16 [1024, 1024], P('dp', 'tensor'), may hold values from -0.1875 to 0.1875
- weight_value: bfloat16 [1024, 1024], P('dp', 'tensor'), may hold values from -0.1875 to 0.1875
- weight_out: bfloat16 [1024, 1024], P('tensor', 'dp'), may hold values from -0.5 to 0.5
- bias_query: bfloat16 [1024], P(('tensor', 'dp')), may hold values from -1.796875 to 1.796875
- bias_value: bfloat16 [1024], P(('tensor', 'dp')), may hold values from -0.59765625 to 0.59765625
- bias_out: bfloat16 [1024], P('dp'), may hold values from -1.796875 to 1.796875
- first_scale: bfloat16 [1024], P('dp'), may hold values from 0.5 to 1.5
- first_shift: bfloat16 [1024], P('dp'), may hold values from -1.796875 to 1.796875
- weight_hidden: bfloat16 [1024, 4096], P('dp', 'tensor'), may hold values from -0.1875 to 0.1875
- bias_hidden: bfloat16 [4096], P(('tensor', 'dp')), may hold values from -1.796875 to 1.796875
- weight_down: bfloat16 [4096, 1024], P('tensor', 'dp'), may hold values from -0.125 to 0.125
- bias_down: bfloat16 [1024], P('dp'), may hold values from -1.796875 to 1.796875
- second_scale: bfloat16 [1024], P('dp'), may hold values from 0.5 to 1.5
- second_shift: bfloat16 [1024], P('dp'), may hold values from -1.796875 to 1.796875
- cotangent: bfloat16 [16384, 1024], P(('dp', 'tensor')), may hold values from -6 to 6
Outputs:
- output: bfloat16 [16384, 1024], P(('dp', 'tensor'))
- grad_tokens: bfloat16 [16384, 1024], P(('dp', 'tensor'))
- grad_weight_query: float32 [1024, 1024], P('dp', 'tensor')
- grad_weight_key: float32 [1024, 1024], P('dp', 'tensor')
- grad_weight_value: float32 [1024, 1024], P('dp', 'tensor')
- grad_weight_out: float32 [1024, 1024], P('tensor', 'dp')
- grad_bias_query: float32 [1024], P(('tensor', 'dp'))
- grad_bias_value: float32 [1024], P(('tensor', 'dp'))
- grad_bias_out: float32 [1024], P('dp')
- grad_first_scale: float32 [1024], P('dp')
- grad_first_shift: float32 [1024], P('dp')
- grad_weight_hidden: float32 [1024, 4096], P('dp', 'tensor')
- grad_bias_hidden: float32 [4096], P(('tensor', 'dp'))
- grad_weight_down: float32 [4096, 1024], P('tensor', 'dp')
- grad_bias_down: float32 [1024], P('dp')
- grad_second_scale: float32 [1024], P('dp')
- grad_second_shift: float32 [1024], P('dp')
All inputs are finite; a program needn't handle non-finite values.
Results may differ from a plain program's by a relative error of at most 0.02.
Values may be sent and summed in bfloat16 or wider, within the bound.
A program may use at most 128 MiB of HBM per device.

v0:
```python
import jax
import jax.numpy as jnp
from jax import lax
from jax.sharding import PartitionSpec as P

HD = 64
LEN = 2048
QB = 512


def layer_norm(values, scale_vec, shift_vec):
    average = jnp.mean(values, axis=-1, keepdims=True)
    centered = values - average
    spread = jnp.mean(centered * centered, axis=-1, keepdims=True)
    return centered * lax.rsqrt(spread + 1e-05) * scale_vec + shift_vec


def gelu_exact(values):
    return jax.nn.gelu(values, approximate=False)


def split_heads(matrix):
    seq_count = matrix.shape[0] // LEN
    head_count = matrix.shape[1] // HD
    shaped = matrix.reshape(seq_count, LEN, head_count, HD).transpose(0, 2, 1, 3)
    return shaped.reshape(seq_count * head_count, LEN, HD)


def join_heads(stacked, width):
    head_count = width // HD
    seq_count = stacked.shape[0] // head_count
    shaped = stacked.reshape(seq_count, head_count, LEN, HD).transpose(0, 2, 1, 3)
    return shaped.reshape(seq_count * LEN, width)


def head_forward(packed):
    query_head, key_head, value_head = packed

    def one_block(block_index):
        block = lax.dynamic_slice_in_dim(query_head, block_index * QB, QB, 0)
        scores = (
            jnp.einsum("qd,kd->qk", block, key_head, preferred_element_type=jnp.float32) * 0.125
        )
        highest = jnp.max(scores, axis=1, keepdims=True)
        expons = jnp.exp(scores - highest)
        total = jnp.sum(expons, axis=1, keepdims=True)
        probs = (expons / total).astype(jnp.bfloat16)
        result = jnp.dot(probs, value_head, preferred_element_type=jnp.float32)
        return (result, (highest + jnp.log(total))[:, 0])

    results, logsum = lax.map(one_block, jnp.arange(LEN // QB, dtype=jnp.int32))
    return (results.reshape(LEN, HD), logsum.reshape(LEN))


def head_backward(packed):
    query_head, key_head, value_head, grad_head, logsum_head = packed

    def one_block(carry, block_index):
        grad_keys, grad_values = carry
        start = block_index * QB
        block = lax.dynamic_slice_in_dim(query_head, start, QB, 0)
        grad_block = lax.dynamic_slice_in_dim(grad_head, start, QB, 0)
        logsum_block = lax.dynamic_slice_in_dim(logsum_head, start, QB, 0)
        scores = (
            jnp.einsum("qd,kd->qk", block, key_head, preferred_element_type=jnp.float32) * 0.125
        )
        probs = jnp.exp(scores - logsum_block[:, None])
        grad_values = grad_values + jnp.einsum(
            "qk,qd->kd", probs.astype(jnp.bfloat16), grad_block, preferred_element_type=jnp.float32
        )
        grad_probs = jnp.einsum(
            "qd,kd->qk", grad_block, value_head, preferred_element_type=jnp.float32
        )
        inner = jnp.sum(probs * grad_probs, axis=1, keepdims=True)
        grad_scores = (0.125 * probs * (grad_probs - inner)).astype(jnp.bfloat16)
        grad_query = jnp.dot(grad_scores, key_head, preferred_element_type=jnp.float32).astype(
            jnp.bfloat16
        )
        grad_keys = grad_keys + jnp.einsum(
            "qk,qd->kd", grad_scores, block, preferred_element_type=jnp.float32
        )
        return ((grad_keys, grad_values), grad_query)

    zeros = jnp.zeros((LEN, HD), jnp.float32)
    (grad_keys, grad_values), grad_query = lax.scan(
        one_block, (zeros, zeros), jnp.arange(LEN // QB, dtype=jnp.int32)
    )
    return (
        grad_query.reshape(LEN, HD),
        grad_keys.astype(jnp.bfloat16),
        grad_values.astype(jnp.bfloat16),
    )


def gather_attention(
    weight_query,
    weight_key,
    weight_value,
    weight_out,
    bias_query,
    bias_value,
    bias_out,
    first_scale,
    first_shift,
):
    return (
        lax.all_gather(weight_query, "dp", axis=0, tiled=True),
        lax.all_gather(weight_key, "dp", axis=0, tiled=True),
        lax.all_gather(weight_value, "dp", axis=0, tiled=True),
        lax.all_gather(weight_out, "dp", axis=1, tiled=True),
        lax.all_gather(bias_query, "dp", axis=0, tiled=True),
        lax.all_gather(bias_value, "dp", axis=0, tiled=True),
        lax.all_gather(bias_out, "dp", axis=0, tiled=True),
        lax.all_gather(first_scale, "dp", axis=0, tiled=True),
        lax.all_gather(first_shift, "dp", axis=0, tiled=True),
    )


def gather_feed(weight_hidden, bias_hidden, weight_down, bias_down, second_scale, second_shift):
    return (
        lax.all_gather(weight_hidden, "dp", axis=0, tiled=True),
        lax.all_gather(bias_hidden, "dp", axis=0, tiled=True),
        lax.all_gather(weight_down, "dp", axis=1, tiled=True),
        lax.all_gather(bias_down, "dp", axis=0, tiled=True),
        lax.all_gather(second_scale, "dp", axis=0, tiled=True),
        lax.all_gather(second_shift, "dp", axis=0, tiled=True),
    )


def attention_front(tokens, attn_set):
    rows_full = lax.all_gather(tokens, "tensor", axis=0, tiled=True)
    query_full, key_full, value_full = (attn_set[0], attn_set[1], attn_set[2])
    queries = (
        jnp.dot(rows_full, query_full, preferred_element_type=jnp.float32)
        + attn_set[4].astype(jnp.float32)
    ).astype(jnp.bfloat16)
    keys = jnp.dot(rows_full, key_full, preferred_element_type=jnp.float32).astype(jnp.bfloat16)
    values = (
        jnp.dot(rows_full, value_full, preferred_element_type=jnp.float32)
        + attn_set[5].astype(jnp.float32)
    ).astype(jnp.bfloat16)
    width = queries.shape[1]
    heads_out, logsum = lax.map(
        head_forward, (split_heads(queries), split_heads(keys), split_heads(values))
    )
    attended = join_heads(heads_out, width).astype(jnp.bfloat16)
    return (rows_full, queries, keys, values, attended, logsum)


def feed_front(first_low, feed_set):
    first_rows = lax.all_gather(first_low, "tensor", axis=0, tiled=True)
    pre = jnp.dot(first_rows, feed_set[0], preferred_element_type=jnp.float32) + feed_set[1].astype(
        jnp.float32
    )
    hidden = gelu_exact(pre).astype(jnp.bfloat16)
    return (first_rows, pre, hidden)


def on_device(
    tokens,
    weight_query,
    weight_key,
    weight_value,
    weight_out,
    bias_query,
    bias_value,
    bias_out,
    first_scale,
    first_shift,
    weight_hidden,
    bias_hidden,
    weight_down,
    bias_down,
    second_scale,
    second_shift,
    cotangent,
):
    attn_set = gather_attention(
        weight_query,
        weight_key,
        weight_value,
        weight_out,
        bias_query,
        bias_value,
        bias_out,
        first_scale,
        first_shift,
    )
    rows_full, queries, keys, values, attended, logsum = attention_front(tokens, attn_set)
    partial_out = jnp.dot(attended, attn_set[3], preferred_element_type=jnp.float32)
    branch = lax.psum_scatter(
        partial_out.astype(jnp.bfloat16), "tensor", scatter_dimension=0, tiled=True
    ).astype(jnp.float32)
    residual_one = tokens.astype(jnp.float32) + branch + attn_set[6].astype(jnp.float32)
    first, first_pull = jax.vjp(
        layer_norm, residual_one, attn_set[7].astype(jnp.float32), attn_set[8].astype(jnp.float32)
    )
    first_low = first.astype(jnp.bfloat16)
    feed_set = gather_feed(
        weight_hidden, bias_hidden, weight_down, bias_down, second_scale, second_shift
    )
    first_rows, pre, hidden = feed_front(first_low, feed_set)
    partial_down = jnp.dot(hidden, feed_set[2], preferred_element_type=jnp.float32)
    down = lax.psum_scatter(
        partial_down.astype(jnp.bfloat16), "tensor", scatter_dimension=0, tiled=True
    ).astype(jnp.float32)
    residual_two = first + down + feed_set[3].astype(jnp.float32)
    result, second_pull = jax.vjp(
        layer_norm, residual_two, feed_set[4].astype(jnp.float32), feed_set[5].astype(jnp.float32)
    )
    output = result.astype(jnp.bfloat16)
    grad_mid, grad_second_scale, grad_second_shift = second_pull(cotangent.astype(jnp.float32))
    feed_set = gather_feed(
        weight_hidden, bias_hidden, weight_down, bias_down, second_scale, second_shift
    )
    first_rows, pre, hidden = feed_front(first_low, feed_set)
    grad_down_rows = lax.all_gather(grad_mid.astype(jnp.bfloat16), "tensor", axis=0, tiled=True)
    grad_weight_down = jnp.einsum(
        "tf,td->fd", hidden, grad_down_rows, preferred_element_type=jnp.float32
    )
    grad_hidden = jnp.einsum(
        "td,fd->tf", grad_down_rows, feed_set[2], preferred_element_type=jnp.float32
    )
    unused_value, gelu_pull = jax.vjp(gelu_exact, pre)
    grad_pre = gelu_pull(grad_hidden)[0].astype(jnp.bfloat16)
    grad_bias_hidden = jnp.sum(grad_pre, axis=0, dtype=jnp.float32)
    grad_weight_hidden = jnp.einsum(
        "td,tf->df", first_rows, grad_pre, preferred_element_type=jnp.float32
    )
    grad_first_rows = jnp.einsum(
        "tf,df->td", grad_pre, feed_set[0], preferred_element_type=jnp.float32
    )
    feed_grads = (
        lax.psum_scatter(grad_weight_hidden, "dp", scatter_dimension=0, tiled=True),
        lax.psum_scatter(grad_bias_hidden, "dp", scatter_dimension=0, tiled=True),
        lax.psum_scatter(grad_weight_down, "dp", scatter_dimension=1, tiled=True),
    )
    grad_first = grad_mid + lax.psum_scatter(
        grad_first_rows, "tensor", scatter_dimension=0, tiled=True
    )
    grad_sum, grad_first_scale, grad_first_shift = first_pull(grad_first)
    attn_set = gather_attention(
        weight_query,
        weight_key,
        weight_value,
        weight_out,
        bias_query,
        bias_value,
        bias_out,
        first_scale,
        first_shift,
    )
    rows_full, queries, keys, values, attended, logsum = attention_front(tokens, attn_set)
    grad_branch_rows = lax.all_gather(grad_sum.astype(jnp.bfloat16), "tensor", axis=0, tiled=True)
    grad_weight_out = jnp.einsum(
        "te,td->ed", attended, grad_branch_rows, preferred_element_type=jnp.float32
    )
    grad_attended = jnp.einsum(
        "td,ed->te", grad_branch_rows, attn_set[3], preferred_element_type=jnp.float32
    ).astype(jnp.bfloat16)
    width = queries.shape[1]
    grad_query_heads, grad_key_heads, grad_value_heads = lax.map(
        head_backward,
        (
            split_heads(queries),
            split_heads(keys),
            split_heads(values),
            split_heads(grad_attended),
            logsum,
        ),
    )
    grad_queries = join_heads(grad_query_heads, width)
    grad_keys = join_heads(grad_key_heads, width)
    grad_values = join_heads(grad_value_heads, width)
    grad_weight_query = jnp.einsum(
        "td,te->de", rows_full, grad_queries, preferred_element_type=jnp.float32
    )
    grad_weight_key = jnp.einsum(
        "td,te->de", rows_full, grad_keys, preferred_element_type=jnp.float32
    )
    grad_weight_value = jnp.einsum(
        "td,te->de", rows_full, grad_values, preferred_element_type=jnp.float32
    )
    grad_bias_query = jnp.sum(grad_queries, axis=0, dtype=jnp.float32)
    grad_bias_value = jnp.sum(grad_values, axis=0, dtype=jnp.float32)
    grad_rows = (
        jnp.einsum("te,de->td", grad_queries, attn_set[0], preferred_element_type=jnp.float32)
        + jnp.einsum("te,de->td", grad_keys, attn_set[1], preferred_element_type=jnp.float32)
        + jnp.einsum("te,de->td", grad_values, attn_set[2], preferred_element_type=jnp.float32)
    )
    attn_grads = (
        lax.psum_scatter(grad_weight_query, "dp", scatter_dimension=0, tiled=True),
        lax.psum_scatter(grad_weight_key, "dp", scatter_dimension=0, tiled=True),
        lax.psum_scatter(grad_weight_value, "dp", scatter_dimension=0, tiled=True),
        lax.psum_scatter(grad_weight_out, "dp", scatter_dimension=1, tiled=True),
        lax.psum_scatter(grad_bias_query, "dp", scatter_dimension=0, tiled=True),
        lax.psum_scatter(grad_bias_value, "dp", scatter_dimension=0, tiled=True),
    )
    grad_tokens = (
        grad_sum
        + lax.psum_scatter(
            grad_rows.astype(jnp.bfloat16), "tensor", scatter_dimension=0, tiled=True
        ).astype(jnp.float32)
    ).astype(jnp.bfloat16)
    vectors = lax.psum(
        (
            jnp.sum(grad_sum, axis=0),
            grad_first_scale,
            grad_first_shift,
            jnp.sum(grad_mid, axis=0),
            grad_second_scale,
            grad_second_shift,
        ),
        ("dp", "tensor"),
    )
    full_width = vectors[0].shape[0]
    shard_width = full_width // lax.axis_size("dp")
    shard_start = lax.axis_index("dp") * shard_width
    shards = tuple(
        (lax.dynamic_slice_in_dim(vector, shard_start, shard_width, 0) for vector in vectors)
    )
    return (
        output,
        grad_tokens,
        attn_grads[0],
        attn_grads[1],
        attn_grads[2],
        attn_grads[3],
        attn_grads[4],
        attn_grads[5],
        shards[0],
        shards[1],
        shards[2],
        feed_grads[0],
        feed_grads[1],
        feed_grads[2],
        shards[3],
        shards[4],
        shards[5],
    )


def solution(mesh):
    placed = (
        P(("dp", "tensor"), None),
        P("dp", "tensor"),
        P("dp", "tensor"),
        P("dp", "tensor"),
        P("tensor", "dp"),
        P(("tensor", "dp")),
        P(("tensor", "dp")),
        P("dp"),
        P("dp"),
        P("dp"),
        P("dp", "tensor"),
        P(("tensor", "dp")),
        P("tensor", "dp"),
        P("dp"),
        P("dp"),
        P("dp"),
        P(("dp", "tensor"), None),
    )
    return jax.shard_map(
        on_device,
        mesh=mesh,
        in_specs=placed,
        out_specs=(
            P(("dp", "tensor"), None),
            P(("dp", "tensor"), None),
            P("dp", "tensor"),
            P("dp", "tensor"),
            P("dp", "tensor"),
            P("tensor", "dp"),
            P(("tensor", "dp")),
            P(("tensor", "dp")),
            P("dp"),
            P("dp"),
            P("dp"),
            P("dp", "tensor"),
            P(("tensor", "dp")),
            P("tensor", "dp"),
            P("dp"),
            P("dp"),
            P("dp"),
        ),
        check_vma=False,
    )
```

profile of v0, /device:TPU:0, one launch (start us, length us, event | category | flops | bytes accessed | tf_op | source)
XLA Modules:
  0.0 1485.1 jit_solution(14111954051303135237)
XLA Ops:
  66.6 27.3 %all-gather.14.cloned.1.call-done = bf16[2048,1024]{1,0:T(8,128)(2,1)} async-done(((bf16[512,1024]{1,0:T(8,128)(2,1)}), bf16[2048,1024]{1,0:T(8,128)(2,1)}) %all-gather.14.cloned.1.call-update) | async-done | bytes 4194320 | tf_op jit(solution)/shard_map/all_gather | solution.py:131
  109.9 76.2 %while.74 = (s32[]{:T(128)}, bf16[4,2048,64]{1,2,0:T(8,128)(2,1)S(1)}, bf16[4,2048,64]{2,1,0:T(8,128)(2,1)}, bf16[4,2048,64]{2,1,0:T(8,128)(2,1)}, bf16[4,2048,6...) while((s32[]{:T(128)}, ...), condition=%wide.region_5.6_spmd, body=%wide.region_0.5_spmd.sunk | while | flops 277871616 | bytes 17049992 | solution.py:143
  112.3 16.1 %while.79 = (s32[]{:T(128)}, bf16[4,512,64]{1,2,0:T(8,128)(2,1)S(1)}, s32[4]{0:T(128)S(1)}, bf16[2048,64]{1,0:T(8,128)(2,1)S(1)}, bf16[2048,64]{1,0:T(8,128)(2,1...) while((s32[]{:T(128)}, bf16[4,512,64]{1,2,0:T(8,128)(2,1)S(1)}, ...), condition=%wide.region_4.4_spmd, body=%wide.region_1.3_spmd.sunk | while | flops 277871616 | bytes 13904039 | solution.py:51
  215.4 49.3 %reduce-scatter.11.cloned.1.call-done = bf16[512,1024]{1,0:T(8,128)(2,1)} async-done(((bf16[2048,1024]{1,0:T(8,128)(2,1)}), bf16[512,1024]{1,0:T(8,128)(2,1)}) %reduce-scatter.11.cloned.1.call-update) | async-done | bytes 1048592 | tf_op jit(solution)/shard_map/reduce_scatter | solution.py:191
  279.5 71.6 %all-gather.16.cloned.1.call-done = bf16[2048,1024]{1,0:T(8,128)(2,1)} async-done(((bf16[512,1024]{1,0:T(8,128)(2,1)}), bf16[2048,1024]{1,0:T(8,128)(2,1)}) %all-gather.16.cloned.1.call-update) | async-done | bytes 4194320 | tf_op jit(solution)/shard_map/all_gather | solution.py:151
  351.1 26.2 %multiply_convert_fusion.1 = (bf16[2048,1024]{1,0:T(8,128)(2,1)}, f32[2048,1024]{1,0:T(8,128)}, f32[2048,1024]{1,0:T(8,128)}) fusion(f32[1024]{0:T(1024)S(1)} %bitcast.252, bf16[2048,1024]{1,0:T(8,128)(2,1)} %all-gather.16.cloned.1.call-done, bf16[1024,1024]{1,0:T(8,128)(2,1)} %all-gather.18.cloned.1.call-done), kind=kOutput, calls=%fused_computation.62 | convolution fusion | flops 4433379328 | bytes 27267072 | tf_op jit(solution)/shard_map/dot_general | solution.py:152
  414.6 50.9 %reduce-scatter.13.cloned.1.call-done = bf16[512,1024]{1,0:T(8,128)(2,1)} async-done(((bf16[2048,1024]{1,0:T(8,128)(2,1)}), bf16[512,1024]{1,0:T(8,128)(2,1)}) %reduce-scatter.13.cloned.1.call-update) | async-done | bytes 1048592 | tf_op jit(solution)/shard_map/reduce_scatter | solution.py:204
  475.0 81.0 %all-gather.22.cloned.1.call-done = bf16[2048,1024]{1,0:T(8,128)(2,1)} async-done(((bf16[512,1024]{1,0:T(8,128)(2,1)}), bf16[2048,1024]{1,0:T(8,128)(2,1)}) %all-gather.22.cloned.1.call-update) | async-done | bytes 4194320 | tf_op jit(solution)/shard_map/all_gather | solution.py:217
  579.0 143.2 %reduce-scatter.15.cloned.1.call-done = f32[512,1024]{1,0:T(8,128)} async-done(((f32[2048,1024]{1,0:T(8,128)}), f32[512,1024]{1,0:T(8,128)}) %reduce-scatter.15.cloned.1.call-update) | async-done | bytes 2097168 | tf_op jit(solution)/shard_map/reduce_scatter | solution.py:238
  730.7 143.7 %while.76 = (s32[]{:T(128)}, bf16[4,2048,64]{1,2,0:T(8,128)(2,1)S(1)}, f32[4,2048]{1,0:T(4,128)S(1)}, bf16[4,2048,64]{2,1,0:T(8,128)(2,1)}, bf16[4,2048,64]{2,1,...) while((s32[]{:T(128)}, ...), condition=%wide.region_22.23_spmd, body=%wide.region_17.0_spmd.sunk | while | flops 277872128 | bytes 33870276 | solution.py:143
  733.1 33.1 %while.80 = (s32[]{:T(128)}, bf16[4,512,64]{1,2,0:T(8,128)(2,1)S(1)}, f32[4,512]{1,0:T(4,128)S(1)}, s32[4]{0:T(128)S(1)}, bf16[2048,64]{1,0:T(8,128)(2,1)S(1)}, ...) while((s32[]{:T(128)}, ...), condition=%wide.region_21.21_spmd, body=%wide.region_18.20_spmd.sunk | while | flops 277872128 | bytes 30691536 | solution.py:51
  769.4 32.8 %while.80 = (s32[]{:T(128)}, bf16[4,512,64]{1,2,0:T(8,128)(2,1)S(1)}, f32[4,512]{1,0:T(4,128)S(1)}, s32[4]{0:T(128)S(1)}, bf16[2048,64]{1,0:T(8,128)(2,1)S(1)}, ...) while((s32[]{:T(128)}, ...), condition=%wide.region_21.21_spmd, body=%wide.region_18.20_spmd.sunk | while | flops 277872128 | bytes 30691536 | solution.py:51
  805.2 32.7 %while.80 = (s32[]{:T(128)}, bf16[4,512,64]{1,2,0:T(8,128)(2,1)S(1)}, f32[4,512]{1,0:T(4,128)S(1)}, s32[4]{0:T(128)S(1)}, bf16[2048,64]{1,0:T(8,128)(2,1)S(1)}, ...) while((s32[]{:T(128)}, ...), condition=%wide.region_21.21_spmd, body=%wide.region_18.20_spmd.sunk | while | flops 277872128 | bytes 30691536 | solution.py:51
  841.0 32.7 %while.80 = (s32[]{:T(128)}, bf16[4,512,64]{1,2,0:T(8,128)(2,1)S(1)}, f32[4,512]{1,0:T(4,128)S(1)}, s32[4]{0:T(128)S(1)}, bf16[2048,64]{1,0:T(8,128)(2,1)S(1)}, ...) while((s32[]{:T(128)}, ...), condition=%wide.region_21.21_spmd, body=%wide.region_18.20_spmd.sunk | while | flops 277872128 | bytes 30691536 | solution.py:51
  880.0 249.5 %while.78 = (s32[]{:T(128)}, bf16[4,2048,64]{1,2,0:T(8,128)(2,1)}, bf16[4,2048,64]{1,2,0:T(8,128)(2,1)}, bf16[4,2048,64]{1,2,0:T(8,128)(2,1)}, bf16[4,2048,64]{2...) while((s32[]{:T(128)}, bf16[4,2048,64]{1,2,0:T(8,128)(2,1)}, ...), condition=%wide.region_27.28_spmd, body=%wide.region_23.27_spmd.sunk | while | flops 681344512 | bytes 74018872 | solution.py:262
  884.3 53.4 %while.81 = (s32[]{:T(128)}, f32[2048,64]{0,1:T(8,128)}, f32[2048,64]{0,1:T(8,128)}, bf16[4,512,64]{1,2,0:T(8,128)(2,1)S(1)}, s32[4]{0:T(128)S(1)}, /*index=5*/b...) while((s32[]{:T(128)}, f32[2048,64]{0,1:T(8,128)}, ...), condition=%wide.region_26.26_spmd.clone, body=%wide.region_24.25_spmd.clone.sunk | while | flops 681082368 | bytes 68757784 | solution.py:85
  946.7 53.4 %while.81 = (s32[]{:T(128)}, f32[2048,64]{0,1:T(8,128)}, f32[2048,64]{0,1:T(8,128)}, bf16[4,512,64]{1,2,0:T(8,128)(2,1)S(1)}, s32[4]{0:T(128)S(1)}, /*index=5*/b...) while((s32[]{:T(128)}, f32[2048,64]{0,1:T(8,128)}, ...), condition=%wide.region_26.26_spmd.clone, body=%wide.region_24.25_spmd.clone.sunk | while | flops 681082368 | bytes 68757784 | solution.py:85
  1009.0 53.4 %while.81 = (s32[]{:T(128)}, f32[2048,64]{0,1:T(8,128)}, f32[2048,64]{0,1:T(8,128)}, bf16[4,512,64]{1,2,0:T(8,128)(2,1)S(1)}, s32[4]{0:T(128)S(1)}, /*index=5*/b...) while((s32[]{:T(128)}, f32[2048,64]{0,1:T(8,128)}, ...), condition=%wide.region_26.26_spmd.clone, body=%wide.region_24.25_spmd.clone.sunk | while | flops 681082368 | bytes 68757784 | solution.py:85
  1071.4 53.4 %while.81 = (s32[]{:T(128)}, f32[2048,64]{0,1:T(8,128)}, f32[2048,64]{0,1:T(8,128)}, bf16[4,512,64]{1,2,0:T(8,128)(2,1)S(1)}, s32[4]{0:T(128)S(1)}, /*index=5*/b...) while((s32[]{:T(128)}, f32[2048,64]{0,1:T(8,128)}, ...), condition=%wide.region_26.26_spmd.clone, body=%wide.region_24.25_spmd.clone.sunk | while | flops 681082368 | bytes 68757784 | solution.py:85
  1178.4 41.1 %all-reduce.5 = (f32[1024]{0:T(1024)S(1)}, f32[1024]{0:T(1024)S(1)}, f32[1024]{0:T(1024)S(1)}, f32[1024]{0:T(1024)S(1)}, f32[1024]{0:T(1024)S(1)}, /*index=5*/f32[1024]{0:T(1024)S(1)}) all-reduce(f32[1024]{0:T(1024)S(1)} %copy-done.28, f32[1024]{0:T(1024)S(1)} %copy-done.23, ...), channel_id=1, replica_groups=mesh['dp'=8,'tensor'=4] {'dp','tensor'}, use_global_device_ids=true, to_apply=%region_38.39 | all-reduce | flops 6144 | bytes 49152 | tf_op jit(solution)/shard_map/psum | solution.py:305
  1250.6 77.3 %reduce-scatter.17.cloned.1.call-done = bf16[512,1024]{1,0:T(8,128)(2,1)} async-done(((bf16[2048,1024]{1,0:T(8,128)(2,1)}), bf16[512,1024]{1,0:T(8,128)(2,1)}) %reduce-scatter.17.cloned.1.call-update) | async-done | bytes 1048592 | tf_op jit(solution)/shard_map/reduce_scatter | solution.py:301
  1330.3 52.9 %reduce-scatter.29.cloned.1.call-done = f32[1024,128]{1,0:T(8,128)} async-done(((f32[1024,1024]{1,0:T(8,128)}), f32[1024,128]{1,0:T(8,128)}) %reduce-scatter.29.cloned.1.call-update) | async-done | bytes 524304 | tf_op jit(solution)/shard_map/reduce_scatter | solution.py:236
  1383.2 54.8 %reduce-scatter.27.cloned.1.call-done = f32[128,1024]{1,0:T(8,128)} async-done(((f32[1024,1024]{1,0:T(8,128)}), f32[128,1024]{1,0:T(8,128)}) %reduce-scatter.27.cloned.1.call-update) | async-done | bytes 524304 | tf_op jit(solution)/shard_map/reduce_scatter | solution.py:234
  1438.1 39.7 %reduce-scatter.25.cloned.1.call-done = f32[256,128]{1,0:T(8,128)} async-done(((f32[256,1024]{1,0:T(8,128)}), f32[256,128]{1,0:T(8,128)}) %reduce-scatter.25.cloned.1.call-update) | async-done | bytes 131088 | tf_op jit(solution)/shard_map/reduce_scatter | solution.py:295
  (702 shorter events, 766.1 us)
Async XLA Ops:
  8.0 85.9 %all-gather.14.cloned.1.call-start = ((), (), s32[]{:S(2)}) async-start(), calls=%async_computation.10 | async-start | bytes 5242880 | tf_op jit(solution)/shard_map/all_gather | solution.py:131
  8.8 256.0 %reduce-scatter.11.cloned.1.call-start = ((), (), s32[]{:S(2)}) async-start(), calls=%async_computation.11 | async-start | bytes 5242880 | tf_op jit(solution)/shard_map/reduce_scatter | solution.py:191
  36.8 60.5 %copy-start.13 = (bf16[1024,256]{1,0:T(8,128)(2,1)}, bf16[1024,256]{1,0:T(8,128)(2,1)S(1)}, u32[]{:S(2)}) copy-start(bf16[1024,256]{1,0:T(8,128)(2,1)S(1)} %all_gather.69) | copy-start | bytes 1572868
  46.3 52.9 %copy-start.11 = (bf16[1024,256]{1,0:T(8,128)(2,1)}, bf16[1024,256]{1,0:T(8,128)(2,1)S(1)}, u32[]{:S(2)}) copy-start(bf16[1024,256]{1,0:T(8,128)(2,1)S(1)} %all_gather.72) | copy-start | bytes 1572868
  109.9 76.2 %copy-start.17 = (bf16[256,1024]{1,0:T(8,128)(2,1)S(1)}, bf16[256,1024]{1,0:T(8,128)(2,1)}, u32[]{:S(2)}) copy-start(bf16[256,1024]{1,0:T(8,128)(2,1)} %all_gather.74) | copy-start | bytes 1572868
  189.3 75.5 %copy-start.3 = (bf16[512,1024]{1,0:T(8,128)(2,1)S(1)}, bf16[512,1024]{1,0:T(8,128)(2,1)}, u32[]{:S(2)}) copy-start(bf16[512,1024]{1,0:T(8,128)(2,1)} %param.29) | copy-start | bytes 3145732
  189.3 90.2 %all-gather.18.cloned.1.call-start = ((), (), s32[]{:S(2)}) async-start(), calls=%async_computation.13 | async-start | bytes 2359296 | tf_op jit(solution)/shard_map/all_gather | solution.py:121
  189.9 161.2 %all-gather.16.cloned.1.call-start = ((), (), s32[]{:S(2)}) async-start(), calls=%async_computation.12 | async-start | bytes 5242880 | tf_op jit(solution)/shard_map/all_gather | solution.py:151
  269.9 109.5 %all-gather.20.cloned.1.call-start = ((), (), s32[]{:S(2)}) async-start(), calls=%async_computation.14 | async-start | bytes 2359296 | tf_op jit(solution)/shard_map/all_gather | solution.py:123
  270.5 195.1 %reduce-scatter.13.cloned.1.call-start = ((), (), s32[]{:S(2)}) async-start(), calls=%async_computation.15 | async-start | bytes 5242880 | tf_op jit(solution)/shard_map/reduce_scatter | solution.py:204
  388.7 79.4 %copy-start.10 = (bf16[512,1024]{1,0:T(8,128)(2,1)S(1)}, bf16[512,1024]{1,0:T(8,128)(2,1)}, u32[]{:S(2)}) copy-start(bf16[512,1024]{1,0:T(8,128)(2,1)} %param.45) | copy-start | bytes 3145732
  388.7 167.3 %all-gather.22.cloned.1.call-start = ((), (), s32[]{:S(2)}) async-start(), calls=%async_computation.16 | async-start | bytes 5242880 | tf_op jit(solution)/shard_map/all_gather | solution.py:217
  474.6 247.6 %reduce-scatter.15.cloned.1.call-start = ((), (), s32[]{:S(2)}) async-start(), calls=%async_computation.17 | async-start | bytes 10485760 | tf_op jit(solution)/shard_map/reduce_scatter | solution.py:238
  578.9 295.5 %all-gather.24.cloned.1.call-start = ((), (), s32[]{:S(2)}) async-start(), calls=%async_computation.18 | async-start | bytes 5242880 | tf_op jit(solution)/shard_map/all_gather | solution.py:254
  730.3 509.6 %reduce-scatter.19.cloned.1.call-start = ((), (), s32[]{:S(2)}) async-start(), calls=%async_computation.20 | async-start | bytes 1179648 | tf_op jit(solution)/shard_map/reduce_scatter | solution.py:292
  730.7 143.7 %copy-start.18 = (bf16[256,1024]{1,0:T(8,128)(2,1)S(1)}, bf16[256,1024]{1,0:T(8,128)(2,1)}, u32[]{:S(2)}) copy-start(bf16[256,1024]{1,0:T(8,128)(2,1)} %all_gather.74) | copy-start | bytes 1572868
  1134.4 107.2 %reduce-scatter.21.cloned.1.call-start = ((), (), s32[]{:S(2)}) async-start(), calls=%async_computation.21 | async-start | bytes 1179648 | tf_op jit(solution)/shard_map/reduce_scatter | solution.py:293
  1139.0 109.9 %reduce-scatter.23.cloned.1.call-start = ((), (), s32[]{:S(2)}) async-start(), calls=%async_computation.22 | async-start | bytes 1179648 | tf_op jit(solution)/shard_map/reduce_scatter | solution.py:294
  1143.7 184.1 %reduce-scatter.17.cloned.1.call-start = ((), (), s32[]{:S(2)}) async-start(), calls=%async_computation.19 | async-start | bytes 5242880 | tf_op jit(solution)/shard_map/reduce_scatter | solution.py:301
  1151.5 231.7 %reduce-scatter.29.cloned.1.call-start = ((), (), s32[]{:S(2)}) async-start(), calls=%async_computation.25 | async-start | bytes 4718592 | tf_op jit(solution)/shard_map/reduce_scatter | solution.py:236
  1161.6 276.5 %reduce-scatter.27.cloned.1.call-start = ((), (), s32[]{:S(2)}) async-start(), calls=%async_computation.24 | async-start | bytes 4718592 | tf_op jit(solution)/shard_map/reduce_scatter | solution.py:234
  1171.9 305.8 %reduce-scatter.25.cloned.1.call-start = ((), (), s32[]{:S(2)}) async-start(), calls=%async_computation.23 | async-start | bytes 1179648 | tf_op jit(solution)/shard_map/reduce_scatter | solution.py:295
  1172.1 155.8 %copy-start.7 = (f32[512,1024]{1,0:T(8,128)S(1)}, f32[512,1024]{1,0:T(8,128)}, u32[]{:S(2)}) copy-start(f32[512,1024]{1,0:T(8,128)} %copy-done.6) | copy-start | bytes 6291460
  1172.1 155.8 %copy-start.22 = (f32[512]{0:T(512)S(1)}, f32[512]{0:T(512)}, u32[]{:S(2)}) copy-start(f32[512]{0:T(512)} %copy-done.21) | copy-start | bytes 6148
  (76 other events, 371.6 us)
Sparse Core Ops, SparseCore 0:
  10.4 83.4 all-gather.13
  189.4 75.2 reduce-scatter.10
  474.7 81.2 all-gather.21
  579.0 143.0 reduce-scatter.14
Sparse Core Ops, SparseCore 1:
  191.7 26.1 all-gather.17
  270.0 81.1 all-gather.15
  352.9 26.4 all-gather.19
  388.8 76.7 reduce-scatter.12
  730.4 81.2 all-gather.23
  1134.5 36.4 reduce-scatter.18
  1173.9 35.9 reduce-scatter.20
  1212.9 36.0 reduce-scatter.22
  1251.1 76.7 reduce-scatter.16
  1331.8 51.4 reduce-scatter.28
  1387.0 51.0 reduce-scatter.26
  1441.8 35.9 reduce-scatter.24
where the time goes:
time: 1490 us
  waiting for transfers between devices  658 us (44%)
  matrix products  369 us (25%)
  blocking collectives  168 us (11%)
  local copies, waits for them, and re-layouts  164 us (11%)
  other arithmetic  73.1 us (5%)
  loops' own time  33.9 us (2%)
  between operations  18.1 us (1%)
    reduce_scatter x1, waiting for transfers between devices, on_device(): lax.psum_scatter(grad_first_rows, 'tensor', scatter_dimension=0, tiled=True)  143 us
    all_gather x1, waiting for transfers between devices, on_device(): lax.all_gather(grad_mid.astype(jnp.bfloat16), 'tensor', axis=0, tiled=True)  81 us
    reduce_scatter x1, waiting for transfers between devices, on_device(): lax.psum_scatter(grad_rows.astype(jnp.bfloat16), 'tensor', scatter_dimens...  77.3 us
    all_gather x1, waiting for transfers between devices, feed_front(): first_rows = lax.all_gather(first_low, 'tensor', axis=0, tiled=True)  71.6 us
    dot_general x32, matrix products, one_block(): result = jnp.dot(probs, value_head, preferred_element_type=jnp.float32)  71.3 us
    while x100, local copies, waits for them, and re-layouts  62.4 us
    dot_general x48, matrix products, one_block(): jnp.einsum('qd,kd->qk', block, key_head, preferred_element_type=jnp.float32)  59.8 us
    reduce_scatter x1, waiting for transfers between devices, on_device(): lax.psum_scatter(grad_weight_hidden, 'dp', scatter_dimension=0, tiled=True)  54.8 us
  transfers between devices with their start and end apart: 16, of which 12 were waited for; matrix products, arithmetic and copies ran while one was open for 13% of the time, Pallas kernels for 0%

commit v1 on v0

v1 whole, which is shorter than its diff:
```python
import jax
import jax.numpy as jnp
from jax import lax
from jax.experimental import pallas as pl
from jax.experimental.pallas import tpu as pltpu
from jax.sharding import PartitionSpec as P

HD = 64
LEN = 2048
QB = 256
PAIR = 2 * HD
PAD = 16
F32 = jnp.float32
BF = jnp.bfloat16
BOTH = ("dp", "tensor")


def contract(left, right, left_dim, right_dim):
    return lax.dot_general(
        left, right, (((left_dim,), (right_dim,)), ((), ())), preferred_element_type=F32
    )


def one_head(pair, head):
    lane = lax.broadcasted_iota(jnp.int32, pair.shape, 1)
    keep = lane < HD if head == 0 else lane >= HD
    return jnp.where(keep, pair, jnp.zeros_like(pair))


def attend_forward_kernel(q_ref, k_ref, v_ref, out_ref, logsum_ref):
    query = q_ref[...] * jnp.asarray(0.125, BF)
    key, value = k_ref[...], v_ref[...]
    total, columns = None, []
    for head in range(2):
        scores = contract(query, one_head(key, head), 1, 1)
        highest = jnp.max(scores, axis=1, keepdims=True)
        expons = jnp.exp(scores - highest)
        mass = jnp.sum(expons, axis=1, keepdims=True)
        part = contract(expons.astype(BF), one_head(value, head), 1, 0) / mass
        total = part if total is None else total + part
        columns.append(jnp.broadcast_to(highest + jnp.log(mass), (query.shape[0], PAIR)))
    out_ref[...] = total.astype(BF)
    logsum_ref[0] = jnp.concatenate([jnp.transpose(column)[:4] for column in columns], axis=0)


def attend_forward(qkv):
    width = qkv.shape[1] // 3
    pairs = width // PAIR
    block = pl.BlockSpec((QB, PAIR), lambda i, j: (j, i))
    key_block = pl.BlockSpec((LEN, PAIR), lambda i, j: (0, i + pairs))
    value_block = pl.BlockSpec((LEN, PAIR), lambda i, j: (0, i + 2 * pairs))
    return pl.pallas_call(
        attend_forward_kernel,
        grid=(width // PAIR, LEN // QB),
        in_specs=[block, key_block, value_block],
        out_specs=[block, pl.BlockSpec((1, 8, QB), lambda i, j: (i, 0, j))],
        out_shape=[
            jax.ShapeDtypeStruct((LEN, width), BF),
            jax.ShapeDtypeStruct((width // PAIR, 8, LEN), F32),
        ],
        cost_estimate=pl.CostEstimate(
            flops=20 * LEN * LEN * width, bytes_accessed=12 * LEN * width, transcendentals=0
        ),
        compiler_params=pltpu.CompilerParams(vmem_limit_bytes=40 << 20),
        name="attend_forward",
    )(qkv, qkv, qkv)


def attend_backward_kernel(
    q_ref, k_ref, v_ref, grad_ref, out_ref, logsum_ref, dq_ref, dk_ref, dv_ref, dk_sum, dv_sum
):
    step = pl.program_id(1)
    query = q_ref[...] * jnp.asarray(0.125, BF)
    key, value, grad = k_ref[...], v_ref[...], grad_ref[...]
    products = jnp.transpose(grad.astype(F32) * out_ref[...].astype(F32))

    @pl.when(step == 0)
    def _():
        dk_sum[...] = jnp.zeros_like(dk_sum)
        dv_sum[...] = jnp.zeros_like(dv_sum)

    grad_query = None
    for head in range(2):
        key_head, value_head = one_head(key, head), one_head(value, head)
        inner = jnp.sum(products[HD * head : HD * head + HD], axis=0, keepdims=True)
        logsum = logsum_ref[0, 4 * head : 4 * head + 1, :]
        probs = jnp.exp(contract(key_head, query, 1, 1) - logsum)
        grad_probs = contract(value_head, grad, 1, 1)
        grad_scores = (probs * (grad_probs - inner)).astype(BF)
        dv_sum[...] += contract(probs.astype(BF), one_head(grad, head), 1, 0)
        dk_sum[...] += contract(grad_scores, one_head(query, head), 1, 0)
        part = contract(grad_scores, key_head, 0, 0)
        grad_query = part if grad_query is None else grad_query + part
    dq_ref[...] = (grad_query * 0.125).astype(BF)

    @pl.when(step == pl.num_programs(1) - 1)
    def _():
        dk_ref[...] = dk_sum[...].astype(BF)
        dv_ref[...] = dv_sum[...].astype(BF)


def attend_backward(qkv, grad, out, logsum):
    width = qkv.shape[1] // 3
    pairs = width // PAIR
    block = pl.BlockSpec((QB, PAIR), lambda i, j: (j, i))
    whole = pl.BlockSpec((LEN, PAIR), lambda i, j: (0, i))
    return pl.pallas_call(
        attend_backward_kernel,
        grid=(width // PAIR, LEN // QB),
        in_specs=[
            block,
            pl.BlockSpec((LEN, PAIR), lambda i, j: (0, i + pairs)),
            pl.BlockSpec((LEN, PAIR), lambda i, j: (0, i + 2 * pairs)),
            block,
            block,
            pl.BlockSpec((1, 8, QB), lambda i, j: (i, 0, j)),
        ],
        out_specs=[block, whole, whole],
        out_shape=[jax.ShapeDtypeStruct((LEN, width), BF)] * 3,
        scratch_shapes=[pltpu.VMEM((LEN, PAIR), F32)] * 2,
        cost_estimate=pl.CostEstimate(
            flops=40 * LEN * LEN * width, bytes_accessed=18 * LEN * width, transcendentals=0
        ),
        compiler_params=pltpu.CompilerParams(vmem_limit_bytes=40 << 20),
        name="attend_backward",
    )(qkv, qkv, qkv, grad, out, logsum)


def row_mean(values):
    return jnp.mean(values, axis=1, keepdims=True)


def column_sum(values):
    return jnp.sum(values, axis=0, keepdims=True)


def middle_kernel(
    sizes,
    att_ref,
    tok_ref,
    cot_ref,
    outw_ref,
    vec_ref,
    hid_ref,
    feed_ref,
    out_ref,
    gsum_ref,
    gatt_ref,
    pack_ref,
    first_s,
    norm_s,
    down_s,
    inv_s,
    low_s,
    low_t,
    gdown_s,
    gdown_t,
    hidden_s,
    slope_s,
    stage_s,
    tail_s,
    sems,
):
    dps, tps, piece, chunks = sizes
    step = pl.program_id(0)
    model = tok_ref.shape[1]
    feed_rows = 2 * piece

    def norm_parts(values):
        centered = values - row_mean(values)
        inverse = lax.rsqrt(row_mean(centered * centered) + 1e-05)
        return centered * inverse, inverse

    def norm_back(grad, scale, normed, inverse):
        scaled = grad * scale
        return inverse * (scaled - row_mean(scaled) - normed * row_mean(scaled * normed))

    def send(slot, block):
        return pltpu.make_async_copy(
            stage_s.at[slot], pack_ref.at[:, block, pl.ds(0, feed_rows)], sems.at[slot]
        )

    @pl.when(step == 0)
    def _():
        branch = None
        for t in range(tps):
            weight = outw_ref[:, t, :piece].reshape(model, -1)
            part = contract(att_ref[t], weight, 1, 1)
            branch = part if branch is None else branch + part
        normed, inverse = norm_parts(tok_ref[...].astype(F32) + branch + vec_ref[0:1])
        first = normed * vec_ref[1:2] + vec_ref[2:3]
        norm_s[...] = normed
        inv_s[...] = jnp.broadcast_to(inverse, inv_s.shape)
        first_s[...] = first
        low = first.astype(BF)
        low_s[...] = low
        low_t[...] = jnp.transpose(low)
        down_s[...] = jnp.zeros_like(down_s)

    @pl.when(step < tps)
    def _():
        weight = feed_ref[:, 0, 0].reshape(model, -1)
        pre = contract(low_s[...], weight, 1, 0) + hid_ref[step]
        share = 0.5 + 0.5 * lax.erf(pre * 0.7071067811865476)
        hidden = (pre * share).astype(BF)
        hidden_s[step] = hidden
        slope_s[step] = (share + pre * (0.3989422804014327 * jnp.exp(-0.5 * pre * pre))).astype(BF)
        down_s[...] += contract(hidden, feed_ref[:, 0, 1].reshape(model, -1), 1, 1)

    @pl.when(step == tps)
    def _():
        normed, inverse = norm_parts(first_s[...] + down_s[...] + vec_ref[3:4])
        out_ref[...] = (normed * vec_ref[4:5] + vec_ref[5:6]).astype(BF)
        grad = cot_ref[...].astype(F32)
        tail_s[0:1] = column_sum(grad * normed)
        tail_s[1:2] = column_sum(grad)
        grad_mid = norm_back(grad, vec_ref[4:5], normed, inverse)
        gsum_ref[...] = grad_mid
        tail_s[2:3] = column_sum(grad_mid)
        grad_down = grad_mid.astype(BF)
        gdown_s[...] = grad_down
        gdown_t[...] = jnp.transpose(grad_down)
        down_s[...] = jnp.zeros_like(down_s)

    @pl.when(step >= tps)
    def _():
        block = 2 * tps - 1 - step
        slot = lax.rem(step, 2)

        @pl.when(step >= tps + 2)
        def _():
            send(slot, block + 2).wait()

        grad_hidden = contract(gdown_s[...], feed_ref[:, 0, 1].reshape(model, -1), 1, 0)
        grad_pre = grad_hidden * slope_s[block].astype(F32)
        grad_low = grad_pre.astype(BF)
        tail_s[pl.ds(8 + block, 1)] = column_sum(grad_low.astype(F32))
        down_s[...] += contract(grad_low, feed_ref[:, 0, 0].reshape(model, -1), 1, 1)
        stage_s[slot, :, :piece] = (
            contract(low_t[...], grad_low, 1, 0).astype(BF).reshape(dps, piece, -1)
        )
        stage_s[slot, :, piece:] = (
            contract(gdown_t[...], hidden_s[block], 1, 0).astype(BF).reshape(dps, piece, -1)
        )
        send(slot, block).start()

    @pl.when(step == 2 * tps - 1)
    def _():
        grad = gsum_ref[...] + down_s[...]
        normed = norm_s[...]
        grad_scale, grad_shift = column_sum(grad * normed), column_sum(grad)
        grad_sum = norm_back(grad, vec_ref[1:2], normed, inv_s[:, 0:1])
        gsum_ref[...] = grad_sum
        grad_bias = column_sum(grad_sum)
        low = grad_sum.astype(BF)
        low_t[...] = jnp.transpose(low)
        for t in range(tps):
            gatt_ref[t] = contract(low, outw_ref[:, t, :piece].reshape(model, -1), 1, 0).astype(BF)
        send(lax.rem(step + 1, 2), 1).wait()
        send(lax.rem(step, 2), 0).wait()
        part = piece // chunks
        width = att_ref.shape[2]
        six = jnp.concatenate(
            [grad_bias, grad_scale, grad_shift, tail_s[2:3], tail_s[0:1], tail_s[1:2]], axis=0
        )
        for t in range(tps):
            gout = contract(low_t[...], att_ref[t], 1, 0).reshape(dps, piece, width)
            wide = [gout[:, c * part : (c + 1) * part] for c in range(chunks)]
            if chunks * width < model:
                wide.append(jnp.zeros((dps, part, model - chunks * width), F32))
            stage_s[0, :, :part] = jnp.concatenate(wide, axis=2).astype(BF)
            rows = jnp.concatenate(
                [six, tail_s[8 + t : 9 + t], jnp.zeros((PAD - 7, model), F32)], axis=0
            ).astype(BF)
            stage_s[0, :, part : part + PAD] = jnp.broadcast_to(rows[None], (dps, PAD, model))
            copy = pltpu.make_async_copy(
                stage_s.at[0, :, pl.ds(0, part + PAD)],
                pack_ref.at[:, t, pl.ds(feed_rows, part + PAD)],
                sems.at[0],
            )
            copy.start()
            copy.wait()


def middle(att, tokens, cotangent, outw, vec, hid, feed):
    tps, rows, width = att.shape
    model = tokens.shape[1]
    dps, piece = feed.shape[0], feed.shape[3]
    chunks = min(model // width, piece // PAD)
    pack_rows = 2 * piece + piece // chunks + PAD

    def fixed(array):
        rank = len(array.shape)
        return pl.BlockSpec(
            array.shape, lambda i: (0,) * rank, pipeline_mode=pl.Buffered(buffer_count=1)
        )

    def feed_at(i):
        return (0, jnp.minimum(i, 2 * tps - 1 - i), 0, 0, 0)

    outs = [
        jax.ShapeDtypeStruct((rows, model), BF),
        jax.ShapeDtypeStruct((rows, model), F32),
        jax.ShapeDtypeStruct(att.shape, BF),
        jax.ShapeDtypeStruct((dps, tps, pack_rows, model), BF),
    ]
    return pl.pallas_call(
        lambda *refs: middle_kernel((dps, tps, piece, chunks), *refs),
        grid=(2 * tps,),
        in_specs=[fixed(a) for a in (att, tokens, cotangent, outw, vec, hid)]
        + [pl.BlockSpec((dps, 1, 2, piece, feed.shape[4]), feed_at)],
        out_specs=[fixed(a) for a in outs[:3]] + [pl.BlockSpec(memory_space=pl.ANY)],
        out_shape=outs,
        scratch_shapes=[
            pltpu.VMEM((rows, model), F32),
            pltpu.VMEM((rows, model), F32),
            pltpu.VMEM((rows, model), F32),
            pltpu.VMEM((rows, 128), F32),
            pltpu.VMEM((rows, model), BF),
            pltpu.VMEM((model, rows), BF),
            pltpu.VMEM((rows, model), BF),
            pltpu.VMEM((model, rows), BF),
            pltpu.VMEM((tps, rows, feed.shape[4]), BF),
            pltpu.VMEM((tps, rows, feed.shape[4]), BF),
            pltpu.VMEM((2, dps, 2 * piece, model), BF),
            pltpu.VMEM((16, model), F32),
            pltpu.SemaphoreType.DMA((2,)),
        ],
        cost_estimate=pl.CostEstimate(
            flops=6 * rows * model * model * (2 * tps + 1),
            bytes_accessed=60 << 20,
            transcendentals=0,
        ),
        compiler_params=pltpu.CompilerParams(vmem_limit_bytes=62 << 20),
        name="middle",
    )(att, tokens, cotangent, outw, vec, hid, feed)


def on_device(
    tokens,
    weight_query,
    weight_key,
    weight_value,
    weight_out,
    bias_query,
    bias_value,
    bias_out,
    first_scale,
    first_shift,
    weight_hidden,
    bias_hidden,
    weight_down,
    bias_down,
    second_scale,
    second_shift,
    cotangent,
):
    dps, tps = lax.axis_size("dp"), lax.axis_size("tensor")
    rows, model = tokens.shape
    piece = weight_hidden.shape[0]
    width = weight_query.shape[1]
    hidden_width = weight_hidden.shape[1]
    small = bias_query.shape[0]

    bias_row = jnp.concatenate([bias_query, bias_value])
    attn_bias = jnp.pad(bias_row[None], ((0, PAD - 1), (0, 3 * width - 2 * small)))
    attn_pack = jnp.concatenate(
        [jnp.concatenate([weight_query, weight_key, weight_value], axis=1), attn_bias], axis=0
    )
    attn_all = lax.all_gather(attn_pack, "dp", axis=0, tiled=False)
    rows_full = lax.all_gather(tokens, "tensor", axis=0, tiled=True)
    vec_row = jnp.concatenate(
        [bias_out, first_scale, first_shift, bias_down, second_scale, second_shift, bias_hidden]
    )
    vec_flat = jnp.pad(vec_row, (0, PAD * width - vec_row.shape[0])).reshape(PAD, width)
    out_all = lax.all_gather(
        jnp.concatenate([weight_out.T, vec_flat], axis=0), BOTH, axis=0, tiled=False
    ).reshape(dps, tps, piece + PAD, width)
    feed_all = lax.all_gather(
        jnp.concatenate([weight_hidden, weight_down.T], axis=0), BOTH, axis=0, tiled=False
    ).reshape(dps, tps, 2, piece, hidden_width)

    qkv_weight = attn_all[:, :piece].reshape(model, 3 * width)
    query_bias = attn_all[:, piece, :small].reshape(width).astype(F32)
    value_bias = attn_all[:, piece, small : 2 * small].reshape(width).astype(F32)
    bias_full = jnp.concatenate([query_bias, jnp.zeros_like(query_bias), value_bias])
    qkv = (contract(rows_full, qkv_weight, 1, 0) + bias_full).astype(BF)
    attended, logsum = attend_forward(qkv)
    crossed = lax.all_to_all(attended.reshape(tps, rows, width), "tensor", 0, 0, tiled=False)

    vecs = out_all[:, :, piece:].reshape(dps, tps, PAD * width)
    vec = vecs[:, 0, : 6 * piece].reshape(dps, 6, piece).transpose(1, 0, 2).reshape(6, model)
    vec = jnp.pad(vec.astype(F32), ((0, 2), (0, 0)))
    hid = vecs[:, :, 6 * piece : 6 * piece + bias_hidden.shape[0]].transpose(1, 0, 2)
    hid = hid.reshape(tps, 1, hidden_width).astype(F32)
    output, grad_sum, grad_cross, packed = middle(
        crossed, tokens, cotangent, out_all, vec, hid, feed_all
    )
    grad_attended = lax.all_to_all(grad_cross, "tensor", 0, 0, tiled=False)
    grad_attended = grad_attended.reshape(tps * rows, width)
    packed = lax.psum_scatter(packed, "dp", scatter_dimension=0, tiled=False)
    packed = lax.psum_scatter(packed, "tensor", scatter_dimension=0, tiled=False).astype(F32)

    grads = attend_backward(qkv, grad_attended, attended, logsum)
    grad_rows, weight_grads, sums = None, [], []
    for index, grad in enumerate(grads):
        weight = qkv_weight[:, index * width : (index + 1) * width]
        part = contract(grad, weight, 1, 1)
        grad_rows = part if grad_rows is None else grad_rows + part
        weight_grads.append(contract(rows_full, grad, 0, 0).astype(BF))
        sums.append(jnp.sum(grad, axis=0, dtype=F32).astype(BF))
    grad_tokens = (
        grad_sum
        + lax.psum_scatter(
            grad_rows.astype(BF), "tensor", scatter_dimension=0, tiled=True
        ).astype(F32)
    ).astype(BF)
    tail = jnp.pad(jnp.concatenate(sums)[None], ((0, PAD - 1), (0, 0)))
    attn_grads = jnp.concatenate(
        [
            jnp.concatenate(weight_grads, axis=1).reshape(dps, piece, 3 * width),
            jnp.broadcast_to(tail[None], (dps, PAD, 3 * width)),
        ],
        axis=1,
    )
    attn_grads = lax.psum_scatter(attn_grads, "dp", scatter_dimension=0, tiled=False).astype(F32)

    place = lax.axis_index("dp")

    def share(values, count):
        return lax.dynamic_slice_in_dim(values, place * count, count, 0)

    chunks = min(model // width, piece // PAD)
    part = piece // chunks
    out_grad = packed[2 * piece : 2 * piece + part, : chunks * width]
    out_grad = out_grad.reshape(part, chunks, width).transpose(2, 1, 0).reshape(width, piece)
    vec_grads = [share(packed[2 * piece + part + i], piece) for i in range(6)]
    hidden_grad = share(packed[2 * piece + part + 6], bias_hidden.shape[0])
    return (
        output,
        grad_tokens,
        attn_grads[:piece, :width],
        attn_grads[:piece, width : 2 * width],
        attn_grads[:piece, 2 * width :],
        out_grad,
        share(attn_grads[piece, :width], small),
        share(attn_grads[piece, 2 * width :], small),
        vec_grads[0],
        vec_grads[1],
        vec_grads[2],
        packed[:piece],
        hidden_grad,
        packed[piece : 2 * piece].T,
        vec_grads[3],
        vec_grads[4],
        vec_grads[5],
    )


def solution(mesh):
    placed = (
        P(("dp", "tensor"), None),
        P("dp", "tensor"),
        P("dp", "tensor"),
        P("dp", "tensor"),
        P("tensor", "dp"),
        P(("tensor", "dp")),
        P(("tensor", "dp")),
        P("dp"),
        P("dp"),
        P("dp"),
        P("dp", "tensor"),
        P(("tensor", "dp")),
        P("tensor", "dp"),
        P("dp"),
        P("dp"),
        P("dp"),
        P(("dp", "tensor"), None),
    )
    return jax.shard_map(
        on_device,
        mesh=mesh,
        in_specs=placed,
        out_specs=(
            P(("dp", "tensor"), None),
            P(("dp", "tensor"), None),
            P("dp", "tensor"),
            P("dp", "tensor"),
            P("dp", "tensor"),
            P("tensor", "dp"),
            P(("tensor", "dp")),
            P(("tensor", "dp")),
            P("dp"),
            P("dp"),
            P("dp"),
            P("dp", "tensor"),
            P(("tensor", "dp")),
            P("tensor", "dp"),
            P("dp"),
            P("dp"),
            P("dp"),
        ),
        check_vma=False,
    )
```

time: 1490 us -> 725 us (0.49)
  matrix products: 369 us -> 18.9 us
  waiting for transfers between devices: 658 us -> 460 us
  blocking collectives: 168 us -> 29.4 us
  Pallas kernels: 0 us -> 132 us
  local copies, waits for them, and re-layouts: 164 us -> 47.8 us
  other arithmetic: 73.1 us -> 16.6 us
  loops' own time: 33.9 us -> 0 us
    dot_general x162 -> x7, matrix products: 369 us -> 18.9 us  [contract(): lax.dot_general(left, right, (((left_dim,), (right_dim,)), ((), ())), pre...]
    reduce_scatter x10 -> x4, waiting for transfers between devices: 474 us -> 192 us  [the longest x1 76.8 us: on_device(): lax.psum_scatter(grad_rows.astype(BF), 'tensor', scatter_dimension=0, til...]
    pallas_call x0 -> x3, Pallas kernels: none -> 132 us  [the longest x1 53.8 us: attend_backward(): pl.pallas_call(attend_backward_kernel, grid=(width // PAIR, LEN // QB), i...]
    all_gather x11 -> x0, blocking collectives: 98.6 us -> none  [the longest x1 11.1 us: gather_attention(): lax.all_gather(weight_out, 'dp', axis=1, tiled=True)]
    all_gather x6 -> x4, waiting for transfers between devices: 182 us -> 267 us  [the longest x1 147 us: on_device(): lax.all_gather(jnp.concatenate([weight_hidden, weight_down.T], axis=0), B...]
    while x112 -> x0, local copies, waits for them, and re-layouts: 65.7 us -> none
    reduce_sum x43 -> x3, other arithmetic: 45.7 us -> 0.86 us  [on_device(): sums.append(jnp.sum(grad, axis=0, dtype=F32).astype(BF))]
    psum x1 -> x0, blocking collectives: 41.1 us -> none  [on_device(): lax.psum((jnp.sum(grad_sum, axis=0), grad_first_scale, grad_first_shift,...]
  transfers between devices with their start and end apart: 16 -> 9, of which waited for: 12 -> 8; matrix products, arithmetic and copies ran while one was open for 13% -> 10% of each run, Pallas kernels for 0% -> 12%
where the time goes in v1:
time: 725 us; the launch traced here: 723 us
  waiting for transfers between devices  460 us (63%)
  Pallas kernels  132 us (18%)
  local copies, waits for them, and re-layouts  47.8 us (7%)
  blocking collectives  29.4 us (4%)
  matrix products  18.9 us (3%)
  other arithmetic  16.6 us (2%)
  between operations  14.4 us (2%)
    all_gather x1, waiting for transfers between devices, on_device(): lax.all_gather(jnp.concatenate([weight_hidden, weight_down.T], axis=0), B...  147 us
    all_gather x1, waiting for transfers between devices, on_device(): rows_full = lax.all_gather(tokens, 'tensor', axis=0, tiled=True)  79.7 us
    reduce_scatter x1, waiting for transfers between devices, on_device(): lax.psum_scatter(grad_rows.astype(BF), 'tensor', scatter_dimension=0, til...  76.8 us
    pallas_call x1, Pallas kernels, attend_backward(): pl.pallas_call(attend_backward_kernel, grid=(width // PAIR, LEN // QB), i...  53.8 us
    reduce_scatter x1, waiting for transfers between devices, on_device(): lax.psum_scatter(packed, 'tensor', scatter_dimension=0, tiled=False)  50.5 us
    pallas_call x1, Pallas kernels, middle(): pl.pallas_call(lambda *refs: middle_kernel((dps, tps, piece, chunks), *re...  47.4 us
    reduce_scatter x1, waiting for transfers between devices, on_device(): lax.psum_scatter(attn_grads, 'dp', scatter_dimension=0, tiled=False)  42.5 us
    pallas_call x1, Pallas kernels, attend_forward(): pl.pallas_call(attend_forward_kernel, grid=(width // PAIR, LEN // QB), in...  30.6 us
  transfers between devices with their start and end apart: 9, of which 8 were waited for; matrix products, arithmetic and copies ran while one was open for 10% of the time, Pallas kernels for 12%

profile of v1, /device:TPU:0, one launch (start us, length us, event | category | flops | bytes accessed | tf_op | source)
XLA Modules:
  0.0 723.0 jit_solution(1827763571521334326)
XLA Ops:
  8.0 1.6 fusion.10
  19.0 1.8 pad_maximum_fusion.2
  20.9 18.7 %all-gather.10.cloned.1.call-done = bf16[1152,768]{1,0:T(8,128)(2,1)} async-done(((bf16[144,768]{1,0:T(8,128)(2,1)}), bf16[1152,768]{1,0:T(8,128)(2,1)}) %all-gather.10.cloned.1.call-update) | async-done | bytes 1769488 | tf_op jit(solution)/shard_map/all_gather | solution.py:370
  42.2 79.7 %all-gather.8.cloned.1.call-done = bf16[2048,1024]{1,0:T(8,128)(2,1)} async-done(((bf16[512,1024]{1,0:T(8,128)(2,1)}), bf16[2048,1024]{1,0:T(8,128)(2,1)}) %all-gather.8.cloned.1.call-update) | async-done | bytes 4194320 | tf_op jit(solution)/shard_map/all_gather | solution.py:371
  122.0 5.6 fusion.q_ref.k_ref.v_ref
  127.6 30.6 %attend_forward.1 = (bf16[2048,256]{1,0:T(8,128)(2,1)}, f32[2,8,2048]{2,1,0:T(8,128)S(1)}) custom-call(bf16[2048,768]{1,0:T(8,128)(2,1)S(1)} %fusion.q_ref.k_ref.v_ref, bf16[2048,768]{1,0:T(8,128)(2,1)S(1)} %fusion.q_ref.k_ref.v_ref, bf16[2048,768]{1,0:T(8,128)(2,1)S(1)} %fusion.q_ref.k_ref.v_ref), custom_call_target="tpu_custom_call" | custom-call | flops 21474836480 | bytes 6291456 | tf_op jit(solution)/shard_map/attend_forward/pallas_call | solution.py:52
  158.3 3.5 all-to-all-start
  161.8 21.8 %all-gather.12.cloned.1.call-done = bf16[4608,256]{1,0:T(8,128)(2,1)} async-done(((bf16[144,256]{1,0:T(8,128)(2,1)}), bf16[4608,256]{1,0:T(8,128)(2,1)}) %all-gather.12.cloned.1.call-update) | async-done | bytes 2359312 | tf_op jit(solution)/shard_map/all_gather | solution.py:376
  186.1 147.2 %all-gather.14.cloned.1.call-done = bf16[8192,1024]{0,1:T(8,128)(2,1)} async-done(((bf16[256,1024]{0,1:T(8,128)(2,1)}), bf16[8192,1024]{0,1:T(8,128)(2,1)}) %all-gather.14.cloned.1.call-update) | async-done | bytes 16777232 | tf_op jit(solution)/shard_map/all_gather | solution.py:379
  333.3 22.4 %copy.58 = bf16[8192,1024]{1,0:T(8,128)(2,1)} copy(bf16[8192,1024]{0,1:T(8,128)(2,1)} %all-gather.14.cloned.1.call-done) | data formatting | bytes 33554432 | tf_op jit(solution)/shard_map/all_gather | solution.py:379
  356.7 47.4 %middle.1 = (bf16[512,1024]{1,0:T(8,128)(2,1)}, f32[512,1024]{1,0:T(8,128)}, bf16[4,512,256]{2,1,0:T(8,128)(2,1)}, bf16[8,4,304,1024]{3,2,1,0:T(8,128)(2,1)}) custom-call(bf16[4,512,256]{2,1,0:T(8,128)(2,1)} %copy-done.5, bf16[512,1024]{1,0:T(8,128)(2,1)} %refs_1_.1, bf16[512,1024]{1,0:T(8,128)(2,1)} %refs_2_.1, bf16[8,4,144,256]{3,2,1,0:T(8,128)(2,1)} %bitcast.91, ...), custom_call_target="tpu_custom_call" | custom-call | flops 28991029248 | bytes 62914560 | tf_op jit(solution)/shard_map/middle/pallas_call | solution.py:307
  405.3 29.4 %all_to_all.10 = bf16[4,512,256]{2,1,0:T(8,128)(2,1)S(1)} all-to-all(bf16[4,512,256]{2,1,0:T(8,128)(2,1)S(1)} %copy-done.6), channel_id=1, replica_groups=mesh['dp'=8,'tensor'=4] {'tensor'}, dimensions={0} | all-to-all | bytes 2097152 | tf_op jit(solution)/shard_map/all_to_all | solution.py:399
  434.7 1.9 copy-done.1
  436.6 53.8 %attend_backward.1 = (bf16[2048,256]{1,0:T(8,128)(2,1)S(1)}, bf16[2048,256]{1,0:T(8,128)(2,1)S(1)}, bf16[2048,256]{1,0:T(8,128)(2,1)S(1)}) custom-call(bf16[2048,768]{1,0:T(8,128)(2,1)S(1)} %copy-done.1, bf16[2048,768]{1,0:T(8,128)(2,1)S(1)} %copy-done.1, bf16[2048,768]{1,0:T(8,128)(2,1)S(1)} %copy-done.1, bf16[2048,256]{1,0:T(8,128)(2,1)S(1)} %bitcast.75, ...), custom_call_target="tpu_custom_call" | custom-call | flops 42949672960 | bytes 9437184 | tf_op jit(solution)/shard_map/attend_backward/pallas_call | solution.py:107
  491.3 3.6 fusion.1
  498.8 2.6 copy.64
  501.4 2.7 pad_maximum_fusion
  504.3 2.4 fusion.5
  508.0 3.4 add_convert_fusion
  511.5 22.1 %reduce-scatter.9.cloned.1.call-done = bf16[1,4,304,1024]{3,2,1,0:T(8,128)(2,1)} async-done(((bf16[8,4,304,1024]{3,2,1,0:T(8,128)(2,1)}), bf16[1,4,304,1024]{3,2,1,0:T(8,128)(2,1)}) %reduce-scatter.9.cloned.1.call-update) | async-done | bytes 2490384 | tf_op jit(solution)/shard_map/reduce_scatter | solution.py:401
  533.6 42.5 %reduce-scatter.7.cloned.1.call-done = bf16[1,144,768]{2,1,0:T(8,128)(2,1)} async-done(((bf16[8,144,768]{2,1,0:T(8,128)(2,1)}), bf16[1,144,768]{2,1,0:T(8,128)(2,1)}) %reduce-scatter.7.cloned.1.call-update) | async-done | bytes 221200 | tf_op jit(solution)/shard_map/reduce_scatter | solution.py:426
  578.5 76.8 %reduce-scatter.5.cloned.1.call-done = bf16[512,1024]{1,0:T(8,128)(2,1)} async-done(((bf16[2048,1024]{1,0:T(8,128)(2,1)}), bf16[512,1024]{1,0:T(8,128)(2,1)}) %reduce-scatter.5.cloned.1.call-update) | async-done | bytes 1048592 | tf_op jit(solution)/shard_map/reduce_scatter | solution.py:414
  655.2 2.5 add_convert_fusion.2
  657.8 50.5 %reduce-scatter.11.cloned.1.call-done = bf16[1,304,1024]{2,1,0:T(8,128)(2,1)} async-done(((bf16[4,304,1024]{2,1,0:T(8,128)(2,1)}), bf16[1,304,1024]{2,1,0:T(8,128)(2,1)}) %reduce-scatter.11.cloned.1.call-update) | async-done | bytes 622608 | tf_op jit(solution)/shard_map/reduce_scatter | solution.py:402
  (87 shorter events, 33.8 us)
Async XLA Ops:
  7.2 32.4 %all-gather.10.cloned.1.call-start = ((), (), s32[]{:S(2)}) async-start(), calls=%async_computation.11 | async-start | bytes 1990656 | tf_op jit(solution)/shard_map/all_gather | solution.py:370
  9.6 112.3 %all-gather.8.cloned.1.call-start = ((), (), s32[]{:S(2)}) async-start(), calls=%async_computation.6 | async-start | bytes 5242880 | tf_op jit(solution)/shard_map/all_gather | solution.py:371
  10.4 173.3 %all-gather.12.cloned.1.call-start = ((), (), s32[]{:S(2)}) async-start(), calls=%async_computation.12 | async-start | bytes 2433024 | tf_op jit(solution)/shard_map/all_gather | solution.py:376
  17.9 315.4 %all-gather.14.cloned.1.call-start = ((), (), s32[]{:S(2)}) async-start(), calls=%async_computation.13 | async-start | bytes 17301504 | tf_op jit(solution)/shard_map/all_gather | solution.py:379
  41.1 86.5 %copy-start.2 = (bf16[8,128,768]{2,1,0:T(8,128)(2,1)}, bf16[8,128,768]{2,1,0:T(8,128)(2,1)S(1)}, u32[]{:S(2)}) copy-start(bf16[8,128,768]{2,1,0:T(8,128)(2,1)S(1)} %slice.112) | copy-start | bytes 4718596
  127.6 30.7 %copy-start = (bf16[2048,768]{1,0:T(8,128)(2,1)}, bf16[2048,768]{1,0:T(8,128)(2,1)S(1)}, u32[]{:S(2)}) copy-start(bf16[2048,768]{1,0:T(8,128)(2,1)S(1)} %fusion.q_ref.k_ref.v_ref) | copy-start | bytes 9437188
  158.3 197.4 %all-to-all-start = ((bf16[4,512,256]{2,1,0:T(8,128)(2,1)}), bf16[4,512,256]{2,1,0:T(8,128)(2,1)S(1)}, u32[]{:S(2)}, u32[]{:S(2)}) async-start(bf16[4,512,256]{2,1,0:T(8,128)(2,1)} %bitcast.4), calls=%async_computation | async-start | bytes 2097152 | tf_op jit(solution)/shard_map/all_to_all | solution.py:389
  161.8 371.8 %reduce-scatter.9.cloned.1.call-start = ((), (), s32[]{:S(2)}) async-start(), calls=%async_computation.9 | async-start | bytes 22413312 | tf_op jit(solution)/shard_map/reduce_scatter | solution.py:401
  355.7 1.0 copy-start.5
  404.1 1.2 copy-start.6
  404.1 172.0 %reduce-scatter.7.cloned.1.call-start = ((), (), s32[]{:S(2)}) async-start(), calls=%async_computation.8 | async-start | bytes 1990656 | tf_op jit(solution)/shard_map/reduce_scatter | solution.py:426
  434.7 1.9 copy-start.1
  491.3 3.6 copy-start.7
  504.2 151.0 %reduce-scatter.5.cloned.1.call-start = ((), (), s32[]{:S(2)}) async-start(), calls=%async_computation.7 | async-start | bytes 5242880 | tf_op jit(solution)/shard_map/reduce_scatter | solution.py:414
  504.2 2.5 copy-start.3
  511.4 143.8 %copy-start.4 = (f32[512,1024]{1,0:T(8,128)S(1)}, f32[512,1024]{1,0:T(8,128)}, u32[]{:S(2)}) copy-start(f32[512,1024]{1,0:T(8,128)} %get-tuple-element.28) | copy-start | bytes 6291460
  511.4 196.9 %reduce-scatter.11.cloned.1.call-start = ((), (), s32[]{:S(2)}) async-start(), calls=%async_computation.10 | async-start | bytes 3112960 | tf_op jit(solution)/shard_map/reduce_scatter | solution.py:402
Sparse Core Ops, SparseCore 0:
  10.5 29.1 all-gather.9
  41.2 80.7 all-gather.7
  125.3 58.2 all-gather.11
  187.0 146.2 all-gather.13
  404.3 129.3 reduce-scatter.8
  536.8 39.2 reduce-scatter.6
  578.4 76.7 reduce-scatter.4
  657.6 50.7 reduce-scatter.10

commit v2 on v1

--- a/solution.py
+++ b/solution.py
@@ -25,6 +25,420 @@
     lane = lax.broadcasted_iota(jnp.int32, pair.shape, 1)
     keep = lane < HD if head == 0 else lane >= HD
     return jnp.where(keep, pair, jnp.zeros_like(pair))
+
+
+CUTS = 4
+
+
+def flipped(index, bit):
+    size = 1 << bit
+    return index + size - 2 * size * lax.rem(index // size, 2)
+
+
+def bit_order(dps):
+    count = dps.bit_length() - 1
+    return tuple(range(1, count)) + (0,)
+
+
+def greet(dps, tps):
+    place, level = lax.axis_index("dp"), lax.axis_index("tensor")
+    barrier = pltpu.get_barrier_semaphore()
+    for bit in bit_order(dps):
+        pl.semaphore_signal(barrier, inc=1, device_id={"dp": flipped(place, bit)})
+    for step in range(1, tps):
+        pl.semaphore_signal(barrier, inc=1, device_id={"tensor": lax.rem(level + step, tps)})
+    pl.semaphore_wait(barrier, len(bit_order(dps)) + tps - 1)
+
+
+def front_kernel(
+    dps,
+    tps,
+    tok_ref,
+    pack_ref,
+    rows_ref,
+    packs_ref,
+    qkv_ref,
+    weight_s,
+    right_sem,
+    left_sem,
+    land_sem,
+    pack_send,
+    pack_land,
+    local_sem,
+):
+    place, level = lax.axis_index("dp"), lax.axis_index("tensor")
+    rows, model = tok_ref.shape
+    piece = model // dps
+    cut = rows // CUTS
+    own = pltpu.make_async_copy(tok_ref, rows_ref.at[level], local_sem.at[0])
+    own_pack = pltpu.make_async_copy(pack_ref, packs_ref.at[place], local_sem.at[1])
+    own.start()
+    own_pack.start()
+    greet(dps, tps)
+
+    def hop(block, chunk, rightward, first=False):
+        span = pl.ds(chunk * cut, cut)
+        return pltpu.make_async_remote_copy(
+            src_ref=tok_ref.at[span] if first else rows_ref.at[block, span],
+            dst_ref=rows_ref.at[block, span],
+            send_sem=(right_sem if rightward else left_sem).at[block, chunk],
+            recv_sem=land_sem.at[block, chunk],
+            device_id={"tensor": level + 1 if rightward else level - 1},
+        )
+
+    for chunk in range(CUTS):
+
+        @pl.when(level < tps - 1)
+        def _():
+            hop(level, chunk, True, True).start()
+
+        @pl.when(level > 0)
+        def _():
+            hop(level, chunk, False, True).start()
+
+    own_pack.wait()
+    held = [place]
+    for bit in bit_order(dps):
+        copies = []
+        for block in held:
+            copies.append(
+                pltpu.make_async_remote_copy(
+                    src_ref=packs_ref.at[block],
+                    dst_ref=packs_ref.at[block],
+                    send_sem=pack_send.at[block],
+                    recv_sem=pack_land.at[block],
+                    device_id={"dp": flipped(place, bit)},
+                )
+            )
+            copies[-1].start()
+        for copy in copies:
+            copy.wait_send()
+        more = [flipped(block, bit) for block in held]
+        for block in more:
+            pltpu.make_async_remote_copy(
+                src_ref=packs_ref.at[block],
+                dst_ref=packs_ref.at[block],
+                send_sem=pack_send.at[block],
+                recv_sem=pack_land.at[block],
+                device_id={"dp": flipped(place, bit)},
+            ).wait_recv()
+        held = held + more
+    weight_s[...] = packs_ref[:, :piece].reshape(weight_s.shape)
+    bias = jnp.sum(packs_ref[:, piece : piece + PAD].astype(F32), axis=0)[0:1]
+
+    def project(block):
+        qkv_ref[block] = (contract(rows_ref[block], weight_s[...], 1, 0) + bias).astype(BF)
+
+    own.wait()
+    project(level)
+    for step in range(1, tps):
+        for chunk in range(CUTS):
+
+            @pl.when(level - step >= 0)
+            def _():
+                hop(level - step, chunk, True).wait_recv()
+
+            @pl.when((level - step >= 0) & (level < tps - 1))
+            def _():
+                hop(level - step, chunk, True).start()
+
+            @pl.when(level + step < tps)
+            def _():
+                hop(level + step, chunk, False).wait_recv()
+
+            @pl.when((level + step < tps) & (level > 0))
+            def _():
+                hop(level + step, chunk, False).start()
+
+        @pl.when(level - step >= 0)
+        def _():
+            project(level - step)
+
+        @pl.when(level + step < tps)
+        def _():
+            project(level + step)
+
+    for step in range(tps):
+        for chunk in range(CUTS):
+
+            @pl.when((level - step >= 0) & (level < tps - 1))
+            def _():
+                hop(level - step, chunk, True, step == 0).wait_send()
+
+            @pl.when((level + step < tps) & (level > 0))
+            def _():
+                hop(level + step, chunk, False, step == 0).wait_send()
+
+
+def front(tokens, pack, dps, tps):
+    rows, model = tokens.shape
+    columns = pack.shape[1]
+    vmem = pl.BlockSpec(memory_space=pltpu.VMEM)
+    return pl.pallas_call(
+        lambda *refs: front_kernel(dps, tps, *refs),
+        in_specs=[vmem] * 2,
+        out_specs=[vmem] * 3,
+        out_shape=[
+            jax.ShapeDtypeStruct((tps, rows, model), BF),
+            jax.ShapeDtypeStruct((dps,) + pack.shape, BF),
+            jax.ShapeDtypeStruct((tps, rows, columns), BF),
+        ],
+        scratch_shapes=[
+            pltpu.VMEM((model, columns), BF),
+            pltpu.SemaphoreType.DMA((tps, CUTS)),
+            pltpu.SemaphoreType.DMA((tps, CUTS)),
+            pltpu.SemaphoreType.DMA((tps, CUTS)),
+            pltpu.SemaphoreType.DMA((dps,)),
+            pltpu.SemaphoreType.DMA((dps,)),
+            pltpu.SemaphoreType.DMA((2,)),
+        ],
+        cost_estimate=pl.CostEstimate(
+            flops=2 * tps * rows * model * columns, bytes_accessed=200 << 20, transcendentals=0
+        ),
+        compiler_params=pltpu.CompilerParams(
+            vmem_limit_bytes=32 << 20, collective_id=1, has_side_effects=True
+        ),
+        name="front",
+    )(tokens, pack)
+
+
+def back_kernel(
+    dps,
+    tps,
+    dq_ref,
+    dk_ref,
+    dv_ref,
+    rows_ref,
+    packs_ref,
+    gsum_ref,
+    tok_out,
+    pack_out,
+    weight_s,
+    part_s,
+    right_s,
+    left_s,
+    mine_s,
+    theirs_s,
+    right_send,
+    right_land,
+    left_send,
+    left_land,
+    pack_send,
+    pack_land,
+):
+    place, level = lax.axis_index("dp"), lax.axis_index("tensor")
+    rows, model = gsum_ref.shape
+    piece = model // dps
+    cut = rows // CUTS
+    width = dq_ref.shape[1]
+    greet(dps, tps)
+    weight_s[...] = packs_ref[:, :piece].reshape(weight_s.shape)
+
+    def rows_of(block):
+        span = pl.ds(pl.multiple_of(block * rows, rows), rows)
+        total = None
+        for index, ref in enumerate((dq_ref, dk_ref, dv_ref)):
+            weight = weight_s[:, index * width : (index + 1) * width]
+            part = contract(ref[span], weight, 1, 1)
+            total = part if total is None else total + part
+        part_s[block] = total.astype(BF)
+
+    def hop(block, chunk, rightward):
+        span = pl.ds(chunk * cut, cut)
+        land = right_s if rightward else left_s
+        return pltpu.make_async_remote_copy(
+            src_ref=part_s.at[block, span],
+            dst_ref=land.at[block, span],
+            send_sem=(right_send if rightward else left_send).at[block, chunk],
+            recv_sem=(right_land if rightward else left_land).at[block, chunk],
+            device_id={"tensor": level + 1 if rightward else level - 1},
+        )
+
+    def gather_in(block, chunk, rightward):
+        hop(block, chunk, rightward).wait_recv()
+        span = pl.ds(chunk * cut, cut)
+        land = right_s if rightward else left_s
+        part_s[block, span] = (
+            part_s[block, span].astype(F32) + land[block, span].astype(F32)
+        ).astype(BF)
+
+    for step in range(tps - 1, 0, -1):
+
+        @pl.when(level + step < tps)
+        def _():
+            rows_of(level + step)
+
+        @pl.when((level + step < tps) & (level == 0))
+        def _():
+            for chunk in range(CUTS):
+                hop(level + step, chunk, True).start()
+
+        @pl.when(level - step >= 0)
+        def _():
+            rows_of(level - step)
+
+        @pl.when((level - step >= 0) & (level == tps - 1))
+        def _():
+            for chunk in range(CUTS):
+                hop(level - step, chunk, False).start()
+
+    rows_of(level)
+    model_rows = rows_ref.reshape(tps * rows, model)
+    tail = jnp.concatenate(
+        [jnp.sum(ref[...].astype(F32), axis=0, keepdims=True) for ref in (dq_ref, dk_ref, dv_ref)],
+        axis=1,
+    )
+    for index, ref in enumerate((dq_ref, dk_ref, dv_ref)):
+        grad = contract(model_rows[...], ref[...], 0, 0).astype(BF).reshape(dps, piece, width)
+        mine_s[:, :piece, index * width : (index + 1) * width] = grad
+    mine_s[:, piece:] = jnp.broadcast_to(tail.astype(BF)[None], (dps, PAD, 3 * width))
+
+    def exchange(index, bit, other):
+        return pltpu.make_async_remote_copy(
+            src_ref=mine_s.at[other],
+            dst_ref=theirs_s.at[index],
+            send_sem=pack_send.at[index],
+            recv_sem=pack_land.at[index],
+            device_id={"dp": flipped(place, bit)},
+        )
+
+    order = bit_order(dps)[::-1]
+
+    def kept(done):
+        blocks = [place]
+        for bit in order[done:][::-1]:
+            blocks = blocks + [flipped(block, bit) for block in blocks]
+        return blocks
+
+    starts = []
+    at = 0
+    for done in range(len(order)):
+        starts.append(at)
+        at += dps >> (done + 1)
+
+    def pack_start(done):
+        for index, block in enumerate(kept(done + 1)):
+            exchange(starts[done] + index, order[done], flipped(block, order[done])).start()
+
+    def pack_finish(done):
+        for index, block in enumerate(kept(done + 1)):
+            exchange(starts[done] + index, order[done], block).wait()
+            mine_s[block] = (
+                mine_s[block].astype(F32) + theirs_s[starts[done] + index].astype(F32)
+            ).astype(BF)
+
+    pack_start(0)
+    pack_done = 0
+    for step in range(tps - 1, 0, -1):
+        for chunk in range(CUTS):
+
+            @pl.when((level > 0) & (level + step < tps))
+            def _():
+                gather_in(level + step, chunk, True)
+                hop(level + step, chunk, True).start()
+
+            @pl.when((level < tps - 1) & (level - step >= 0))
+            def _():
+                gather_in(level - step, chunk, False)
+                hop(level - step, chunk, False).start()
+
+        if pack_done < len(order):
+            pack_finish(pack_done)
+            pack_done += 1
+            if pack_done < len(order):
+                pack_start(pack_done)
+    while pack_done < len(order):
+        pack_finish(pack_done)
+        pack_done += 1
+        if pack_done < len(order):
+            pack_start(pack_done)
+    pack_out[...] = mine_s[place].astype(F32)
+    for chunk in range(CUTS):
+
+        @pl.when(level > 0)
+        def _():
+            hop(level, chunk, True).wait_recv()
+
+        @pl.when(level < tps - 1)
+        def _():
+            hop(level, chunk, False).wait_recv()
+
+    total = gsum_ref[...] + part_s[level].astype(F32)
+    total = total + jnp.where(level > 0, right_s[level].astype(F32), 0.0)
+    total = total + jnp.where(level < tps - 1, left_s[level].astype(F32), 0.0)
+    tok_out[...] = total.astype(BF)
+    for step in range(1, tps):
+        for chunk in range(CUTS):
+
+            @pl.when(level + step < tps)
+            def _():
+                hop(level + step, chunk, True).wait_send()
+
+            @pl.when(level - step >= 0)
+            def _():
+                hop(level - step, chunk, False).wait_send()
+
+
+def back(grads, rows_full, packs, grad_sum):
+    rows, model = grad_sum.shape
+    tps = rows_full.shape[0]
+    dps, pack_rows, columns = packs.shape
+    vmem = pl.BlockSpec(memory_space=pltpu.VMEM)
+    return pl.pallas_call(
+        lambda *refs: back_kernel(dps, tps, *refs),
+        in_specs=[vmem] * 6,
+        out_specs=[vmem] * 2,
+        out_shape=[
+            jax.ShapeDtypeStruct((rows, model), BF),
+            jax.ShapeDtypeStruct((pack_rows, columns), F32),
+        ],
+        scratch_shapes=[
+            pltpu.VMEM((model, columns), BF),
+            pltpu.VMEM((tps, rows, model), BF),
+            pltpu.VMEM((tps, rows, model), BF),
+            pltpu.VMEM((tps, rows, model), BF),
+            pltpu.VMEM(packs.shape, BF),
+            pltpu.VMEM(packs.shape, BF),
+        ]
+        + [pltpu.SemaphoreType.DMA((tps, CUTS))] * 4
+        + [pltpu.SemaphoreType.DMA((dps,))] * 2,
+        cost_estimate=pl.CostEstimate(
+            flops=4 * tps * rows * model * columns, bytes_accessed=200 << 20, transcendentals=0
+        ),
+        compiler_params=pltpu.CompilerParams(
+            vmem_limit_bytes=56 << 20, collective_id=2, has_side_effects=True
+        ),
+        name="back",
+    )(*grads, rows_full, packs, grad_sum)
+
+
+def pack_kernel(hidden_ref, down_ref, out_ref, vec_ref, packed_ref):
+    piece, wide = hidden_ref.shape
+    width = out_ref.shape[0]
+    chunks = min(wide // width, piece // PAD)
+    part = piece // chunks
+    packed_ref[:piece] = hidden_ref[...]
+    packed_ref[piece : 2 * piece] = jnp.transpose(down_ref[...])
+    turned = jnp.transpose(out_ref[...])
+    for chunk in range(chunks):
+        packed_ref[2 * piece : 2 * piece + part, chunk * width : (chunk + 1) * width] = turned[
+            chunk * part : (chunk + 1) * part
+        ]
+    if chunks * width < wide:
+        packed_ref[2 * piece : 2 * piece + part, chunks * width :] = jnp.zeros(
+            (part, wide - chunks * width), BF
+        )
+    packed_ref[2 * piece + part :] = vec_ref[...]
+
+
+def pack_weights(hidden, down, out, vec):
+    piece, wide = hidden.shape
+    chunks = min(wide // out.shape[0], piece // PAD)
+    return pl.pallas_call(
+        pack_kernel,
+        out_shape=jax.ShapeDtypeStruct((2 * piece + piece // chunks + PAD, wide), BF),
+        name="pack",
+    )(hidden, down, out, vec)
 
 
 def attend_forward_kernel(q_ref, k_ref, v_ref, out_ref, logsum_ref):
@@ -139,9 +553,7 @@
     att_ref,
     tok_ref,
     cot_ref,
-    outw_ref,
-    vec_ref,
-    hid_ref,
+    all_ref,
     feed_ref,
     out_ref,
     gsum_ref,
@@ -159,12 +571,18 @@
     slope_s,
     stage_s,
     tail_s,
+    extra_s,
+    wout_s,
+    vec_s,
     sems,
+    extra_sem,
 ):
     dps, tps, piece, chunks = sizes
     step = pl.program_id(0)
     model = tok_ref.shape[1]
     feed_rows = 2 * piece
+    part = piece // chunks
+    width = att_ref.shape[2]
 
     def norm_parts(values):
         centered = values - row_mean(values)
@@ -182,13 +600,31 @@
 
     @pl.when(step == 0)
     def _():
+        def fetch(t):
+            return pltpu.make_async_copy(
+                all_ref.at[:, t, pl.ds(feed_rows, part + PAD)], extra_s.at[t % 2], extra_sem.at[t % 2]
+            )
+
+        fetch(0).start()
+        for t in range(tps):
+            if t + 1 < tps:
+                fetch(t + 1).start()
+            fetch(t).wait()
+            extra = extra_s.at[t % 2]
+            placed = jnp.sum(extra[:, part:].astype(F32), axis=0)
+            if t == 0:
+                vec_s[0:8] = placed[0:8]
+            vec_s[8 + t : 9 + t] = placed[6:7]
+            turned = jnp.concatenate(
+                [extra[:, :part, c * width : (c + 1) * width] for c in range(chunks)], axis=1
+            )
+            wout_s[t] = turned.reshape(model, width)
         branch = None
         for t in range(tps):
-            weight = outw_ref[:, t, :piece].reshape(model, -1)
-            part = contract(att_ref[t], weight, 1, 1)
-            branch = part if branch is None else branch + part
-        normed, inverse = norm_parts(tok_ref[...].astype(F32) + branch + vec_ref[0:1])
-        first = normed * vec_ref[1:2] + vec_ref[2:3]
+            term = contract(att_ref[t], wout_s[t], 1, 1)
+            branch = term if branch is None else branch + term
+        normed, inverse = norm_parts(tok_ref[...].astype(F32) + branch + vec_s[0:1])
+        first = normed * vec_s[1:2] + vec_s[2:3]
         norm_s[...] = normed
         inv_s[...] = jnp.broadcast_to(inverse, inv_s.shape)
         first_s[...] = first
@@ -199,22 +635,22 @@
 
     @pl.when(step < tps)
     def _():
-        weight = feed_ref[:, 0, 0].reshape(model, -1)
-        pre = contract(low_s[...], weight, 1, 0) + hid_ref[step]
+        weight = feed_ref[:, 0, :piece].reshape(model, -1)
+        pre = contract(low_s[...], weight, 1, 0) + vec_s[pl.ds(8 + step, 1)]
         share = 0.5 + 0.5 * lax.erf(pre * 0.7071067811865476)
         hidden = (pre * share).astype(BF)
         hidden_s[step] = hidden
         slope_s[step] = (share + pre * (0.3989422804014327 * jnp.exp(-0.5 * pre * pre))).astype(BF)
-        down_s[...] += contract(hidden, feed_ref[:, 0, 1].reshape(model, -1), 1, 1)
+        down_s[...] += contract(hidden, feed_ref[:, 0, piece:].reshape(model, -1), 1, 1)
 
     @pl.when(step == tps)
     def _():
-        normed, inverse = norm_parts(first_s[...] + down_s[...] + vec_ref[3:4])
-        out_ref[...] = (normed * vec_ref[4:5] + vec_ref[5:6]).astype(BF)
+        normed, inverse = norm_parts(first_s[...] + down_s[...] + vec_s[3:4])
+        out_ref[...] = (normed * vec_s[4:5] + vec_s[5:6]).astype(BF)
         grad = cot_ref[...].astype(F32)
         tail_s[0:1] = column_sum(grad * normed)
         tail_s[1:2] = column_sum(grad)
-        grad_mid = norm_back(grad, vec_ref[4:5], normed, inverse)
+        grad_mid = norm_back(grad, vec_s[4:5], normed, inverse)
         gsum_ref[...] = grad_mid
         tail_s[2:3] = column_sum(grad_mid)
         grad_down = grad_mid.astype(BF)
@@ -231,11 +667,11 @@
         def _():
             send(slot, block + 2).wait()
 
-        grad_hidden = contract(gdown_s[...], feed_ref[:, 0, 1].reshape(model, -1), 1, 0)
+        grad_hidden = contract(gdown_s[...], feed_ref[:, 0, piece:].reshape(model, -1), 1, 0)
         grad_pre = grad_hidden * slope_s[block].astype(F32)
         grad_low = grad_pre.astype(BF)
         tail_s[pl.ds(8 + block, 1)] = column_sum(grad_low.astype(F32))
-        down_s[...] += contract(grad_low, feed_ref[:, 0, 0].reshape(model, -1), 1, 1)
+        down_s[...] += contract(grad_low, feed_ref[:, 0, :piece].reshape(model, -1), 1, 1)
         stage_s[slot, :, :piece] = (
             contract(low_t[...], grad_low, 1, 0).astype(BF).reshape(dps, piece, -1)
         )
@@ -249,17 +685,15 @@
         grad = gsum_ref[...] + down_s[...]
         normed = norm_s[...]
         grad_scale, grad_shift = column_sum(grad * normed), column_sum(grad)
-        grad_sum = norm_back(grad, vec_ref[1:2], normed, inv_s[:, 0:1])
+        grad_sum = norm_back(grad, vec_s[1:2], normed, inv_s[:, 0:1])
         gsum_ref[...] = grad_sum
         grad_bias = column_sum(grad_sum)
         low = grad_sum.astype(BF)
         low_t[...] = jnp.transpose(low)
         for t in range(tps):
-            gatt_ref[t] = contract(low, outw_ref[:, t, :piece].reshape(model, -1), 1, 0).astype(BF)
+            gatt_ref[t] = contract(low, wout_s[t], 1, 0).astype(BF)
         send(lax.rem(step + 1, 2), 1).wait()
         send(lax.rem(step, 2), 0).wait()
-        part = piece // chunks
-        width = att_ref.shape[2]
         six = jnp.concatenate(
             [grad_bias, grad_scale, grad_shift, tail_s[2:3], tail_s[0:1], tail_s[1:2]], axis=0
         )
@@ -282,10 +716,11 @@
             copy.wait()
 
 
-def middle(att, tokens, cotangent, outw, vec, hid, feed):
+def middle(att, tokens, cotangent, gathered):
     tps, rows, width = att.shape
     model = tokens.shape[1]
-    dps, piece = feed.shape[0], feed.shape[3]
+    dps, wide = gathered.shape[0], gathered.shape[3]
+    piece = model // dps
     chunks = min(model // width, piece // PAD)
     pack_rows = 2 * piece + piece // chunks + PAD
 
@@ -296,7 +731,7 @@
         )
 
     def feed_at(i):
-        return (0, jnp.minimum(i, 2 * tps - 1 - i), 0, 0, 0)
+        return (0, jnp.minimum(i, 2 * tps - 1 - i), 0, 0)
 
     outs = [
         jax.ShapeDtypeStruct((rows, model), BF),
@@ -307,8 +742,11 @@
     return pl.pallas_call(
         lambda *refs: middle_kernel((dps, tps, piece, chunks), *refs),
         grid=(2 * tps,),
-        in_specs=[fixed(a) for a in (att, tokens, cotangent, outw, vec, hid)]
-        + [pl.BlockSpec((dps, 1, 2, piece, feed.shape[4]), feed_at)],
+        in_specs=[fixed(a) for a in (att, tokens, cotangent)]
+        + [
+            pl.BlockSpec(memory_space=pl.ANY),
+            pl.BlockSpec((dps, 1, 2 * piece, wide), feed_at),
+        ],
         out_specs=[fixed(a) for a in outs[:3]] + [pl.BlockSpec(memory_space=pl.ANY)],
         out_shape=outs,
         scratch_shapes=[
@@ -320,10 +758,14 @@
             pltpu.VMEM((model, rows), BF),
             pltpu.VMEM((rows, model), BF),
             pltpu.VMEM((model, rows), BF),
-            pltpu.VMEM((tps, rows, feed.shape[4]), BF),
-            pltpu.VMEM((tps, rows, feed.shape[4]), BF),
+            pltpu.VMEM((tps, rows, wide), BF),
+            pltpu.VMEM((tps, rows, wide), BF),
             pltpu.VMEM((2, dps, 2 * piece, model), BF),
             pltpu.VMEM((16, model), F32),
+            pltpu.VMEM((2, dps, piece // chunks + PAD, wide), BF),
+            pltpu.VMEM((tps, model, width), BF),
+            pltpu.VMEM((16, model), F32),
+            pltpu.SemaphoreType.DMA((2,)),
             pltpu.SemaphoreType.DMA((2,)),
         ],
         cost_estimate=pl.CostEstimate(
@@ -333,7 +775,7 @@
         ),
         compiler_params=pltpu.CompilerParams(vmem_limit_bytes=62 << 20),
         name="middle",
-    )(att, tokens, cotangent, outw, vec, hid, feed)
+    )(att, tokens, cotangent, gathered, gathered)
 
 
 def on_device(
@@ -359,73 +801,48 @@
     rows, model = tokens.shape
     piece = weight_hidden.shape[0]
     width = weight_query.shape[1]
-    hidden_width = weight_hidden.shape[1]
     small = bias_query.shape[0]
 
-    bias_row = jnp.concatenate([bias_query, bias_value])
-    attn_bias = jnp.pad(bias_row[None], ((0, PAD - 1), (0, 3 * width - 2 * small)))
+    place = lax.axis_index("dp")
+
+    def placed(pieces, length):
+        zeros = jnp.zeros((pieces.shape[0], length), BF)
+        return lax.dynamic_update_slice_in_dim(zeros, pieces, place * pieces.shape[1], 1)
+
+    vec_rows = placed(
+        jnp.stack(
+            [bias_out, first_scale, first_shift, bias_down, second_scale, second_shift, bias_hidden]
+        ),
+        model,
+    )
+    packed_weights = pack_weights(
+        weight_hidden, weight_down, weight_out, jnp.pad(vec_rows, ((0, PAD - 7), (0, 0)))
+    )
+    gathered = lax.all_gather(packed_weights, BOTH, axis=0, tiled=False)
+    gathered = gathered.reshape((dps, tps) + packed_weights.shape)
+
+    bias_rows = placed(jnp.stack([bias_query, bias_value]), width)
+    bias_row = jnp.concatenate([bias_rows[0:1], jnp.zeros((1, width), BF), bias_rows[1:2]], axis=1)
     attn_pack = jnp.concatenate(
-        [jnp.concatenate([weight_query, weight_key, weight_value], axis=1), attn_bias], axis=0
+        [
+            jnp.concatenate([weight_query, weight_key, weight_value], axis=1),
+            jnp.pad(bias_row, ((0, PAD - 1), (0, 0))),
+        ],
+        axis=0,
     )
-    attn_all = lax.all_gather(attn_pack, "dp", axis=0, tiled=False)
-    rows_full = lax.all_gather(tokens, "tensor", axis=0, tiled=True)
-    vec_row = jnp.concatenate(
-        [bias_out, first_scale, first_shift, bias_down, second_scale, second_shift, bias_hidden]
-    )
-    vec_flat = jnp.pad(vec_row, (0, PAD * width - vec_row.shape[0])).reshape(PAD, width)
-    out_all = lax.all_gather(
-        jnp.concatenate([weight_out.T, vec_flat], axis=0), BOTH, axis=0, tiled=False
-    ).reshape(dps, tps, piece + PAD, width)
-    feed_all = lax.all_gather(
-        jnp.concatenate([weight_hidden, weight_down.T], axis=0), BOTH, axis=0, tiled=False
-    ).reshape(dps, tps, 2, piece, hidden_width)
-
-    qkv_weight = attn_all[:, :piece].reshape(model, 3 * width)
-    query_bias = attn_all[:, piece, :small].reshape(width).astype(F32)
-    value_bias = attn_all[:, piece, small : 2 * small].reshape(width).astype(F32)
-    bias_full = jnp.concatenate([query_bias, jnp.zeros_like(query_bias), value_bias])
-    qkv = (contract(rows_full, qkv_weight, 1, 0) + bias_full).astype(BF)
+    rows_full, packs, qkv = front(tokens, attn_pack, dps, tps)
+    qkv = qkv.reshape(tps * rows, 3 * width)
     attended, logsum = attend_forward(qkv)
     crossed = lax.all_to_all(attended.reshape(tps, rows, width), "tensor", 0, 0, tiled=False)
 
-    vecs = out_all[:, :, piece:].reshape(dps, tps, PAD * width)
-    vec = vecs[:, 0, : 6 * piece].reshape(dps, 6, piece).transpose(1, 0, 2).reshape(6, model)
-    vec = jnp.pad(vec.astype(F32), ((0, 2), (0, 0)))
-    hid = vecs[:, :, 6 * piece : 6 * piece + bias_hidden.shape[0]].transpose(1, 0, 2)
-    hid = hid.reshape(tps, 1, hidden_width).astype(F32)
-    output, grad_sum, grad_cross, packed = middle(
-        crossed, tokens, cotangent, out_all, vec, hid, feed_all
-    )
+    output, grad_sum, grad_cross, packed = middle(crossed, tokens, cotangent, gathered)
     grad_attended = lax.all_to_all(grad_cross, "tensor", 0, 0, tiled=False)
     grad_attended = grad_attended.reshape(tps * rows, width)
     packed = lax.psum_scatter(packed, "dp", scatter_dimension=0, tiled=False)
     packed = lax.psum_scatter(packed, "tensor", scatter_dimension=0, tiled=False).astype(F32)
 
     grads = attend_backward(qkv, grad_attended, attended, logsum)
-    grad_rows, weight_grads, sums = None, [], []
-    for index, grad in enumerate(grads):
-        weight = qkv_weight[:, index * width : (index + 1) * width]
-        part = contract(grad, weight, 1, 1)
-        grad_rows = part if grad_rows is None else grad_rows + part
-        weight_grads.append(contract(rows_full, grad, 0, 0).astype(BF))
-        sums.append(jnp.sum(grad, axis=0, dtype=F32).astype(BF))
-    grad_tokens = (
-        grad_sum
-        + lax.psum_scatter(
-            grad_rows.astype(BF), "tensor", scatter_dimension=0, tiled=True
-        ).astype(F32)
-    ).astype(BF)
-    tail = jnp.pad(jnp.concatenate(sums)[None], ((0, PAD - 1), (0, 0)))
-    attn_grads = jnp.concatenate(
-        [
-            jnp.concatenate(weight_grads, axis=1).reshape(dps, piece, 3 * width),
-            jnp.broadcast_to(tail[None], (dps, PAD, 3 * width)),
-        ],
-        axis=1,
-    )
-    attn_grads = lax.psum_scatter(attn_grads, "dp", scatter_dimension=0, tiled=False).astype(F32)
-
-    place = lax.axis_index("dp")
+    grad_tokens, attn_grads = back(grads, rows_full, packs, grad_sum)
 
     def share(values, count):
         return lax.dynamic_slice_in_dim(values, place * count, count, 0)

time: 725 us -> 577 us (0.80)
  waiting for transfers between devices: 460 us -> 127 us
  Pallas kernels: 132 us -> 374 us
  local copies, waits for them, and re-layouts: 47.8 us -> 21.5 us
  matrix products: 18.9 us -> 0 us
  other arithmetic: 16.6 us -> 2.91 us
    all_gather x4 -> x1, waiting for transfers between devices: 267 us -> 0.01 us  [on_device(): gathered = lax.all_gather(packed_weights, BOTH, axis=0, tiled=False)]
    pallas_call x0 -> x3, Pallas kernels: none -> 242 us  [the longest x1 163 us: front(): pl.pallas_call(lambda *refs: front_kernel(dps, tps, *refs), in_specs=[vme...]
    reduce_scatter x2 -> x0, waiting for transfers between devices: 119 us -> none  [the longest x1 76.8 us: on_device(): lax.psum_scatter(grad_rows.astype(BF), 'tensor', scatter_dimension=0, til...]
    reduce_scatter x1, waiting for transfers between devices: 22.1 us -> 127 us  [on_device(): packed = lax.psum_scatter(packed, 'dp', scatter_dimension=0, tiled=False)]
    reduce_scatter x1, waiting for transfers between devices: 50.5 us -> 0.01 us  [on_device(): lax.psum_scatter(packed, 'tensor', scatter_dimension=0, tiled=False)]
    all_gather x1 -> x0, local copies, waits for them, and re-layouts: 22.4 us -> none  [on_device(): lax.all_gather(jnp.concatenate([weight_hidden, weight_down.T], axis=0), B...]
    dot_general x7 -> x0, matrix products: 18.9 us -> none  [contract(): lax.dot_general(left, right, (((left_dim,), (right_dim,)), ((), ())), pre...]
  transfers between devices with their start and end apart: 9 -> 4, of which waited for: 8 -> 1; matrix products, arithmetic and copies ran while one was open for 10% -> 1% of each run, Pallas kernels for 12% -> 57%
where the time goes in v2:
time: 577 us; the launch traced here: 570 us
  Pallas kernels  374 us (65%)
  waiting for transfers between devices  127 us (22%)
  blocking collectives  26.4 us (5%)
  local copies, waits for them, and re-layouts  21.5 us (4%)
  between operations  14.4 us (2%)
    pallas_call x1, Pallas kernels, front(): pl.pallas_call(lambda *refs: front_kernel(dps, tps, *refs), in_specs=[vme...  163 us
    reduce_scatter x1, waiting for transfers between devices, on_device(): packed = lax.psum_scatter(packed, 'dp', scatter_dimension=0, tiled=False)  127 us
    pallas_call x1, Pallas kernels, back(): pl.pallas_call(lambda *refs: back_kernel(dps, tps, *refs), in_specs=[vmem...  77.8 us
    pallas_call x1, Pallas kernels, attend_backward(): pl.pallas_call(attend_backward_kernel, grid=(width // PAIR, LEN // QB), i...  51.8 us
    pallas_call x1, Pallas kernels, middle(): pl.pallas_call(lambda *refs: middle_kernel((dps, tps, piece, chunks), *re...  50.1 us
    pallas_call x1, Pallas kernels, attend_forward(): pl.pallas_call(attend_forward_kernel, grid=(width // PAIR, LEN // QB), in...  30 us
    all_to_all x1, blocking collectives, on_device(): lax.all_to_all(attended.reshape(tps, rows, width), 'tensor', 0, 0, tiled=...  26.4 us
    unnamed x21, local copies, waits for them, and re-layouts  11.9 us
  transfers between devices with their start and end apart: 4, of which 1 were waited for; matrix products, arithmetic and copies ran while one was open for 1% of the time, Pallas kernels for 57%

profile of v2, /device:TPU:0, one launch (start us, length us, event | category | flops | bytes accessed | tf_op | source)
XLA Modules:
  0.0 569.8 jit_solution(6735196493537955927)
XLA Ops:
  8.7 2.0 pack.1
  11.7 0.9 fusion.1.refs_1_
  12.6 1.2 copy-done
  13.8 162.5 %front.1 = (bf16[4,512,1024]{2,1,0:T(8,128)(2,1)S(1)}, bf16[8,144,768]{2,1,0:T(8,128)(2,1)S(1)}, bf16[4,512,768]{2,1,0:T(8,128)(2,1)S(1)}) custom-call(bf16[512,1024]{1,0:T(8,128)(2,1)S(1)} %copy-done, bf16[144,768]{1,0:T(8,128)(2,1)S(1)} %fusion.1.refs_1_), custom_call_target="tpu_custom_call" | custom-call | flops 3221225472 | bytes 209715200 | tf_op jit(solution)/shard_map/front/pallas_call | solution.py:177
  176.4 2.0 copy-done.3
  178.3 1.2 copy-done.4
  179.5 30.0 %attend_forward.1 = (bf16[2048,256]{1,0:T(8,128)(2,1)S(1)}, f32[2,8,2048]{2,1,0:T(8,128)S(1)}) custom-call(bf16[2048,768]{1,0:T(8,128)(2,1)S(1)} %bitcast.43, bf16[2048,768]{1,0:T(8,128)(2,1)S(1)} %bitcast.44, bf16[2048,768]{1,0:T(8,128)(2,1)S(1)} %bitcast.45), custom_call_target="tpu_custom_call" | custom-call | flops 21474836480 | bytes 6291456 | tf_op jit(solution)/shard_map/attend_forward/pallas_call | solution.py:466
  209.6 26.4 %all_to_all.10.refs_0_ = bf16[4,512,256]{2,1,0:T(8,128)(2,1)} all-to-all(bf16[4,512,256]{2,1,0:T(8,128)(2,1)S(1)} %bitcast.41), channel_id=1, replica_groups=mesh['dp'=8,'tensor'=4] {'tensor'}, dimensions={0} | all-to-all | bytes 2097152 | tf_op jit(solution)/shard_map/all_to_all | solution.py:836
  236.0 50.1 %middle.1 = (bf16[512,1024]{1,0:T(8,128)(2,1)}, f32[512,1024]{1,0:T(8,128)}, bf16[4,512,256]{2,1,0:T(8,128)(2,1)}, bf16[8,4,304,1024]{3,2,1,0:T(8,128)(2,1)}) custom-call(bf16[4,512,256]{2,1,0:T(8,128)(2,1)} %all_to_all.10.refs_0_, bf16[512,1024]{1,0:T(8,128)(2,1)} %refs_1_.1, bf16[512,1024]{1,0:T(8,128)(2,1)} %refs_2_.1, ...), custom_call_target="tpu_custom_call" | custom-call | flops 28991029248 | bytes 62914560 | tf_op jit(solution)/shard_map/middle/pallas_call | solution.py:742
  286.1 3.5 all-to-all-start.1
  289.7 126.6 %reduce-scatter.3.cloned.1.call-done = bf16[1,4,304,1024]{3,2,1,0:T(8,128)(2,1)} async-done(((bf16[8,4,304,1024]{3,2,1,0:T(8,128)(2,1)}), bf16[1,4,304,1024]{3,2,1,0:T(8,128)(2,1)}) %reduce-scatter.3.cloned.1.call-update) | async-done | bytes 2490384 | tf_op jit(solution)/shard_map/reduce_scatter | solution.py:841
  416.4 1.9 copy-done.2
  418.3 51.8 %attend_backward.1 = (bf16[2048,256]{1,0:T(8,128)(2,1)S(1)}, bf16[2048,256]{1,0:T(8,128)(2,1)S(1)}, bf16[2048,256]{1,0:T(8,128)(2,1)S(1)}) custom-call(bf16[2048,768]{1,0:T(8,128)(2,1)S(1)} %bitcast.46, bf16[2048,768]{1,0:T(8,128)(2,1)S(1)} %bitcast.47, bf16[2048,768]{1,0:T(8,128)(2,1)S(1)} %bitcast.48, bf16[2048,256]{1,0:T(8,128)(2,1)S(1)} %bitcast.42, ...), custom_call_target="tpu_custom_call" | custom-call | flops 42949672960 | bytes 9437184 | tf_op jit(solution)/shard_map/attend_backward/pallas_call | solution.py:521
  470.1 1.0 copy-done.5
  471.1 1.0 copy-done.6
  472.1 1.0 copy-done.7
  473.1 77.8 %back.1 = (bf16[512,1024]{1,0:T(8,128)(2,1)}, f32[144,768]{1,0:T(8,128)}) custom-call(bf16[2048,256]{1,0:T(8,128)(2,1)} %copy-done.5, bf16[2048,256]{1,0:T(8,128)(2,1)} %copy-done.6, bf16[2048,256]{1,0:T(8,128)(2,1)} %copy-done.7, bf16[4,512,1024]{2,1,0:T(8,128)(2,1)} %copy-done.3, bf16[8,144,768]{2,1,0:T(8,128)(2,1)} %copy-done.4, ...), custom_call_target="tpu_custom_call" | custom-call | flops 6442450944 | bytes 209715200 | tf_op jit(solution)/shard_map/back/pallas_call | solution.py:387
  552.1 1.8 fusion.14
  553.9 1.0 fusion.12
  555.4 0.8 slice.86
  557.1 1.3 convert_element_type.8
  558.4 0.9 slice_bitcast_fusion
  559.3 1.0 copy.38
  561.9 1.0 copy.42
  (40 shorter events, 6.7 us)
Async XLA Ops:
  7.2 228.8 %all-gather.3.cloned.1.call-start = ((), (), s32[]{:S(2)}) async-start(), calls=%async_computation.6 | async-start | bytes 20545536 | tf_op jit(solution)/shard_map/all_gather | solution.py:821
  10.7 405.7 %reduce-scatter.3.cloned.1.call-start = ((), (), s32[]{:S(2)}) async-start(), calls=%async_computation.4 | async-start | bytes 22413312 | tf_op jit(solution)/shard_map/reduce_scatter | solution.py:841
  12.6 1.2 copy-start
  176.3 2.0 copy-start.3
  178.3 1.2 copy-start.4
  179.5 30.0 %copy-start.1 = (bf16[4,512,768]{2,1,0:T(8,128)(2,1)}, bf16[4,512,768]{2,1,0:T(8,128)(2,1)S(1)}, u32[]{:S(2)}) copy-start(bf16[4,512,768]{2,1,0:T(8,128)(2,1)S(1)} %get-tuple-element.31) | copy-start | bytes 9437188
  286.1 130.3 %all-to-all-start.1 = ((bf16[4,512,256]{2,1,0:T(8,128)(2,1)}), bf16[4,512,256]{2,1,0:T(8,128)(2,1)S(1)}, u32[]{:S(2)}, u32[]{:S(2)}) async-start(bf16[4,512,256]{2,1,0:T(8,128)(2,1)} %get-tuple-element.34), calls=%async_computation.1 | async-start | bytes 2097152 | tf_op jit(solution)/shard_map/all_to_all | solution.py:839
  289.7 264.2 %reduce-scatter.5.cloned.1.call-start = ((), (), s32[]{:S(2)}) async-start(), calls=%async_computation.5 | async-start | bytes 3112960 | tf_op jit(solution)/shard_map/reduce_scatter | solution.py:842
  416.4 1.9 copy-start.2
  470.1 1.0 copy-start.5
  471.1 1.0 copy-start.6
  472.1 1.0 copy-start.7
  557.1 4.7 copy-start.8
Sparse Core Ops, SparseCore 0:
  11.4 172.7 all-gather.2
  286.2 130.0 reduce-scatter.2
  418.7 50.2 reduce-scatter.4

commit v3 on v2

--- a/solution.py
+++ b/solution.py
@@ -12,7 +12,6 @@
 PAD = 16
 F32 = jnp.float32
 BF = jnp.bfloat16
-BOTH = ("dp", "tensor")
 
 
 def contract(left, right, left_dim, right_dim):
@@ -50,14 +49,19 @@
     pl.semaphore_wait(barrier, len(bit_order(dps)) + tps - 1)
 
 
-def front_kernel(
+def forward_kernel(
     dps,
     tps,
     tok_ref,
     pack_ref,
+    mine_ref,
     rows_ref,
     packs_ref,
     qkv_ref,
+    att_ref,
+    lse_ref,
+    cross_ref,
+    gath_ref,
     weight_s,
     right_sem,
     left_sem,
@@ -65,15 +69,30 @@
     pack_send,
     pack_land,
     local_sem,
+    level_send,
+    level_land,
+    plane_send,
+    plane_land,
+    cross_send,
+    cross_land,
 ):
     place, level = lax.axis_index("dp"), lax.axis_index("tensor")
     rows, model = tok_ref.shape
     piece = model // dps
+    width = pack_ref.shape[1] // 3
+    pairs = width // PAIR
     cut = rows // CUTS
+    count = mine_ref.shape[0]
+    middle_row = count // (2 * PAD) * PAD
+    spans = (pl.ds(0, middle_row), pl.ds(middle_row, count - middle_row))
+    bits = tuple(range(1, dps.bit_length() - 1))
+    orders = (bits, bits[::-1])
     own = pltpu.make_async_copy(tok_ref, rows_ref.at[level], local_sem.at[0])
     own_pack = pltpu.make_async_copy(pack_ref, packs_ref.at[place], local_sem.at[1])
+    own_block = pltpu.make_async_copy(mine_ref, gath_ref.at[place, level], local_sem.at[2])
     own.start()
     own_pack.start()
+    own_block.start()
     greet(dps, tps)
 
     def hop(block, chunk, rightward, first=False):
@@ -86,6 +105,63 @@
             device_id={"tensor": level + 1 if rightward else level - 1},
         )
 
+    def to_level(step, half):
+        return pltpu.make_async_remote_copy(
+            src_ref=mine_ref.at[spans[half]],
+            dst_ref=gath_ref.at[place, level, spans[half]],
+            send_sem=level_send.at[step, half],
+            recv_sem=level_land.at[step, half],
+            device_id={"tensor": lax.rem(level + step, tps)},
+        )
+
+    def in_plane(block, step, half, bit, number, mine=False):
+        at = lax.rem(level + step, tps)
+        return pltpu.make_async_remote_copy(
+            src_ref=mine_ref.at[spans[half]] if mine else gath_ref.at[block, at, spans[half]],
+            dst_ref=gath_ref.at[block, at, spans[half]],
+            send_sem=plane_send.at[number, step, half],
+            recv_sem=plane_land.at[block, step, half],
+            device_id={"dp": flipped(place, bit)},
+        )
+
+    def held(half, stage):
+        blocks = [place]
+        for bit in orders[half][:stage]:
+            blocks = blocks + [flipped(block, bit) for block in blocks]
+        return blocks
+
+    def numbered(half):
+        found, at = [], 0
+        for stage in range(len(bits) + 1):
+            for block in held(half, stage)[(1 << stage) // 2 if stage else 0 :]:
+                targets = list(orders[half][stage:]) + [0]
+                found.append((stage, block, [(bit, at + i) for i, bit in enumerate(targets)]))
+                at += len(targets)
+        return found
+
+    tables = (numbered(0), numbered(1))
+
+    def pass_on(step, stage):
+        for half in range(2):
+            for came, block, targets in tables[half]:
+                if came != stage:
+                    continue
+                if stage:
+                    in_plane(block, step, half, 0, 0).wait_recv()
+                for bit, number in targets:
+                    in_plane(block, step, half, bit, number, step == 0 and stage == 0).start()
+
+    def level_in(step):
+        back = tps - step
+        for half in range(2):
+            pltpu.make_async_remote_copy(
+                src_ref=mine_ref.at[spans[half]],
+                dst_ref=gath_ref.at[place, lax.rem(level + step, tps), spans[half]],
+                send_sem=level_send.at[back, half],
+                recv_sem=level_land.at[back, half],
+                device_id={"tensor": lax.rem(level + back, tps)},
+            ).wait_recv()
+
     for chunk in range(CUTS):
 
         @pl.when(level < tps - 1)
@@ -97,10 +173,10 @@
             hop(level, chunk, False, True).start()
 
     own_pack.wait()
-    held = [place]
+    known = [place]
     for bit in bit_order(dps):
         copies = []
-        for block in held:
+        for block in known:
             copies.append(
                 pltpu.make_async_remote_copy(
                     src_ref=packs_ref.at[block],
@@ -113,7 +189,7 @@
             copies[-1].start()
         for copy in copies:
             copy.wait_send()
-        more = [flipped(block, bit) for block in held]
+        more = [flipped(block, bit) for block in known]
         for block in more:
             pltpu.make_async_remote_copy(
                 src_ref=packs_ref.at[block],
@@ -122,7 +198,8 @@
                 recv_sem=pack_land.at[block],
                 device_id={"dp": flipped(place, bit)},
             ).wait_recv()
-        held = held + more
+        known = known + more
+    pass_on(0, 0)
     weight_s[...] = packs_ref[:, :piece].reshape(weight_s.shape)
     bias = jnp.sum(packs_ref[:, piece : piece + PAD].astype(F32), axis=0)[0:1]
 
@@ -158,6 +235,95 @@
         def _():
             project(level + step)
 
+        if step == min(2, tps - 1):
+            for other in range(1, tps):
+                for half in range(2):
+                    to_level(other, half).start()
+        if step <= len(bits):
+            pass_on(0, step)
+    for stage in range(tps, len(bits) + 1):
+        pass_on(0, stage)
+
+    half_rows = rows // 2
+
+    def cross(target, half):
+        span = pl.ds(half * half_rows, half_rows)
+        return pltpu.make_async_remote_copy(
+            src_ref=att_ref.at[target, span],
+            dst_ref=cross_ref.at[level, span],
+            send_sem=cross_send.at[target, half],
+            recv_sem=cross_land.at[level, half],
+            device_id={"tensor": target},
+        )
+
+    turns = 2 * pairs * tps
+
+    def attend(turn, carry):
+        pair = lax.rem(turn, pairs)
+        half = lax.rem(turn // pairs, 2)
+        target = lax.rem(level + 1 + turn // (2 * pairs), tps)
+        span = pl.ds(pl.multiple_of(half * half_rows, half_rows), half_rows)
+        lanes = pl.ds(pl.multiple_of(pair * PAIR, PAIR), PAIR)
+        query = qkv_ref[target, span, lanes] * jnp.asarray(0.125, BF)
+        key = qkv_ref[:, :, pl.ds(pl.multiple_of(width + pair * PAIR, PAIR), PAIR)]
+        value = qkv_ref[:, :, pl.ds(pl.multiple_of(2 * width + pair * PAIR, PAIR), PAIR)]
+        key, value = key.reshape(tps * rows, PAIR), value.reshape(tps * rows, PAIR)
+        total, columns = None, []
+        for head in range(2):
+            scores = contract(query, one_head(key, head), 1, 1)
+            highest = jnp.max(scores, axis=1, keepdims=True)
+            expons = jnp.exp(scores - highest)
+            mass = jnp.sum(expons, axis=1, keepdims=True)
+            part = contract(expons.astype(BF), one_head(value, head), 1, 0) / mass
+            total = part if total is None else total + part
+            columns.append(jnp.broadcast_to(highest + jnp.log(mass), (half_rows, PAIR)))
+        att_ref[target, span, lanes] = total.astype(BF)
+        where = pl.ds(pl.multiple_of(target * rows + half * half_rows, half_rows), half_rows)
+        lse_ref[pair, :, where] = jnp.concatenate(
+            [jnp.transpose(column)[:4] for column in columns], axis=0
+        )
+
+        @pl.when((pair == pairs - 1) & (turn < 2 * pairs * (tps - 1)))
+        def _():
+            cross(target, half).start()
+
+        @pl.when(turn == turns // 2)
+        def _():
+            level_in(1)
+            pass_on(1, 0)
+
+        return carry
+
+    lax.fori_loop(0, turns, attend, 0)
+    own_cross = pltpu.make_async_copy(att_ref.at[level], cross_ref.at[level], local_sem.at[3])
+    own_cross.start()
+    for step in range(2, tps):
+        level_in(step)
+        pass_on(step, 0)
+        for stage in range(1, len(bits) + 1):
+            pass_on(step - 1, stage)
+    for stage in range(1, len(bits) + 1):
+        pass_on(tps - 1, stage)
+    for step in range(1, tps):
+        other = lax.rem(level + step, tps)
+        for half in range(2):
+            pltpu.make_async_remote_copy(
+                src_ref=att_ref.at[level, pl.ds(half * half_rows, half_rows)],
+                dst_ref=cross_ref.at[other, pl.ds(half * half_rows, half_rows)],
+                send_sem=cross_send.at[other, half],
+                recv_sem=cross_land.at[other, half],
+                device_id={"tensor": other},
+            ).wait_recv()
+            cross(other, half).wait_send()
+            to_level(step, half).wait_send()
+    for step in range(tps):
+        for half in range(2):
+            for stage, block, targets in tables[half]:
+                in_plane(flipped(block, 0), step, half, 0, 0).wait_recv()
+                for bit, number in targets:
+                    in_plane(block, step, half, bit, number).wait_send()
+    own_block.wait()
+    own_cross.wait()
     for step in range(tps):
         for chunk in range(CUTS):
 
@@ -170,36 +336,49 @@
                 hop(level + step, chunk, False, step == 0).wait_send()
 
 
-def front(tokens, pack, dps, tps):
+def forward(tokens, pack, mine, dps, tps):
     rows, model = tokens.shape
     columns = pack.shape[1]
+    width = columns // 3
     vmem = pl.BlockSpec(memory_space=pltpu.VMEM)
+    hbm = pl.BlockSpec(memory_space=pl.ANY)
+    dma = pltpu.SemaphoreType.DMA
     return pl.pallas_call(
-        lambda *refs: front_kernel(dps, tps, *refs),
-        in_specs=[vmem] * 2,
-        out_specs=[vmem] * 3,
+        lambda *refs: forward_kernel(dps, tps, *refs),
+        in_specs=[vmem, vmem, hbm],
+        out_specs=[vmem] * 5 + [hbm] * 2,
         out_shape=[
             jax.ShapeDtypeStruct((tps, rows, model), BF),
             jax.ShapeDtypeStruct((dps,) + pack.shape, BF),
             jax.ShapeDtypeStruct((tps, rows, columns), BF),
+            jax.ShapeDtypeStruct((tps, rows, width), BF),
+            jax.ShapeDtypeStruct((width // PAIR, 8, tps * rows), F32),
+            jax.ShapeDtypeStruct((tps, rows, width), BF),
+            jax.ShapeDtypeStruct((dps, tps) + mine.shape, BF),
         ],
         scratch_shapes=[
             pltpu.VMEM((model, columns), BF),
-            pltpu.SemaphoreType.DMA((tps, CUTS)),
-            pltpu.SemaphoreType.DMA((tps, CUTS)),
-            pltpu.SemaphoreType.DMA((tps, CUTS)),
-            pltpu.SemaphoreType.DMA((dps,)),
-            pltpu.SemaphoreType.DMA((dps,)),
-            pltpu.SemaphoreType.DMA((2,)),
+            dma((tps, CUTS)),
+            dma((tps, CUTS)),
+            dma((tps, CUTS)),
+            dma((dps,)),
+            dma((dps,)),
+            dma((4,)),
+            dma((tps, 2)),
+            dma((tps, 2)),
+            dma((dps - 1, tps, 2)),
+            dma((dps, tps, 2)),
+            dma((tps, 2)),
+            dma((tps, 2)),
         ],
         cost_estimate=pl.CostEstimate(
             flops=2 * tps * rows * model * columns, bytes_accessed=200 << 20, transcendentals=0
         ),
         compiler_params=pltpu.CompilerParams(
-            vmem_limit_bytes=32 << 20, collective_id=1, has_side_effects=True
+            vmem_limit_bytes=50 << 20, collective_id=1, has_side_effects=True
         ),
-        name="front",
-    )(tokens, pack)
+        name="forward",
+    )(tokens, pack, mine)
 
 
 def back_kernel(
@@ -439,45 +618,6 @@
         out_shape=jax.ShapeDtypeStruct((2 * piece + piece // chunks + PAD, wide), BF),
         name="pack",
     )(hidden, down, out, vec)
-
-
-def attend_forward_kernel(q_ref, k_ref, v_ref, out_ref, logsum_ref):
-    query = q_ref[...] * jnp.asarray(0.125, BF)
-    key, value = k_ref[...], v_ref[...]
-    total, columns = None, []
-    for head in range(2):
-        scores = contract(query, one_head(key, head), 1, 1)
-        highest = jnp.max(scores, axis=1, keepdims=True)
-        expons = jnp.exp(scores - highest)
-        mass = jnp.sum(expons, axis=1, keepdims=True)
-        part = contract(expons.astype(BF), one_head(value, head), 1, 0) / mass
-        total = part if total is None else total + part
-        columns.append(jnp.broadcast_to(highest + jnp.log(mass), (query.shape[0], PAIR)))
-    out_ref[...] = total.astype(BF)
-    logsum_ref[0] = jnp.concatenate([jnp.transpose(column)[:4] for column in columns], axis=0)
-
-
-def attend_forward(qkv):
-    width = qkv.shape[1] // 3
-    pairs = width // PAIR
-    block = pl.BlockSpec((QB, PAIR), lambda i, j: (j, i))
-    key_block = pl.BlockSpec((LEN, PAIR), lambda i, j: (0, i + pairs))
-    value_block = pl.BlockSpec((LEN, PAIR), lambda i, j: (0, i + 2 * pairs))
-    return pl.pallas_call(
-        attend_forward_kernel,
-        grid=(width // PAIR, LEN // QB),
-        in_specs=[block, key_block, value_block],
-        out_specs=[block, pl.BlockSpec((1, 8, QB), lambda i, j: (i, 0, j))],
-        out_shape=[
-            jax.ShapeDtypeStruct((LEN, width), BF),
-            jax.ShapeDtypeStruct((width // PAIR, 8, LEN), F32),
-        ],
-        cost_estimate=pl.CostEstimate(
-            flops=20 * LEN * LEN * width, bytes_accessed=12 * LEN * width, transcendentals=0
-        ),
-        compiler_params=pltpu.CompilerParams(vmem_limit_bytes=40 << 20),
-        name="attend_forward",
-    )(qkv, qkv, qkv)
 
 
 def attend_backward_kernel(
@@ -818,9 +958,6 @@
     packed_weights = pack_weights(
         weight_hidden, weight_down, weight_out, jnp.pad(vec_rows, ((0, PAD - 7), (0, 0)))
     )
-    gathered = lax.all_gather(packed_weights, BOTH, axis=0, tiled=False)
-    gathered = gathered.reshape((dps, tps) + packed_weights.shape)
-
     bias_rows = placed(jnp.stack([bias_query, bias_value]), width)
     bias_row = jnp.concatenate([bias_rows[0:1], jnp.zeros((1, width), BF), bias_rows[1:2]], axis=1)
     attn_pack = jnp.concatenate(
@@ -830,18 +967,18 @@
         ],
         axis=0,
     )
-    rows_full, packs, qkv = front(tokens, attn_pack, dps, tps)
+    rows_full, packs, qkv, attended, logsum, crossed, gathered = forward(
+        tokens, attn_pack, packed_weights, dps, tps
+    )
     qkv = qkv.reshape(tps * rows, 3 * width)
-    attended, logsum = attend_forward(qkv)
-    crossed = lax.all_to_all(attended.reshape(tps, rows, width), "tensor", 0, 0, tiled=False)
-
+    attended = attended.reshape(tps * rows, width)
     output, grad_sum, grad_cross, packed = middle(crossed, tokens, cotangent, gathered)
     grad_attended = lax.all_to_all(grad_cross, "tensor", 0, 0, tiled=False)
     grad_attended = grad_attended.reshape(tps * rows, width)
     packed = lax.psum_scatter(packed, "dp", scatter_dimension=0, tiled=False)
+    grads = attend_backward(qkv, grad_attended, attended, logsum)
+    packed, grads = lax.optimization_barrier((packed, grads))
     packed = lax.psum_scatter(packed, "tensor", scatter_dimension=0, tiled=False).astype(F32)
-
-    grads = attend_backward(qkv, grad_attended, attended, logsum)
     grad_tokens, attn_grads = back(grads, rows_full, packs, grad_sum)
 
     def share(values, count):

time: 577 us -> 537 us (0.931)
  waiting for transfers between devices: 127 us -> 41.8 us
  Pallas kernels: 374 us -> 419 us
    reduce_scatter x1, waiting for transfers between devices: 127 us -> 41.7 us  [on_device(): packed = lax.psum_scatter(packed, 'dp', scatter_dimension=0, tiled=False)]
    pallas_call x1, Pallas kernels: 77.8 us -> 117 us  [back(): pl.pallas_call(lambda *refs: back_kernel(dps, tps, *refs), in_specs=[vmem...]
    pallas_call x2 -> x1, Pallas kernels: 193 us -> 198 us  [forward(): pl.pallas_call(lambda *refs: forward_kernel(dps, tps, *refs), in_specs=[v...]
    unnamed x21 -> x23, local copies, waits for them, and re-layouts: 11.9 us -> 11.1 us
  transfers between devices with their start and end apart: 4 -> 2, of which waited for: 1 -> 1; matrix products, arithmetic and copies ran while one was open for 1% -> 1% of each run, Pallas kernels for 57% -> 32%
where the time goes in v3:
time: 537 us; the launch traced here: 529 us
  Pallas kernels  419 us (78%)
  waiting for transfers between devices  41.8 us (8%)
  blocking collectives  30.3 us (6%)
  local copies, waits for them, and re-layouts  20.7 us (4%)
  between operations  14.6 us (3%)
    pallas_call x1, Pallas kernels, forward(): pl.pallas_call(lambda *refs: forward_kernel(dps, tps, *refs), in_specs=[v...  198 us
    pallas_call x1, Pallas kernels, back(): pl.pallas_call(lambda *refs: back_kernel(dps, tps, *refs), in_specs=[vmem...  117 us
    pallas_call x1, Pallas kernels, attend_backward(): pl.pallas_call(attend_backward_kernel, grid=(width // PAIR, LEN // QB), i...  51.8 us
    pallas_call x1, Pallas kernels, middle(): pl.pallas_call(lambda *refs: middle_kernel((dps, tps, piece, chunks), *re...  50.1 us
    reduce_scatter x1, waiting for transfers between devices, on_device(): packed = lax.psum_scatter(packed, 'dp', scatter_dimension=0, tiled=False)  41.7 us
    all_to_all x1, blocking collectives, on_device(): grad_attended = lax.all_to_all(grad_cross, 'tensor', 0, 0, tiled=False)  30.3 us
    unnamed x23, local copies, waits for them, and re-layouts  11.1 us
  transfers between devices with their start and end apart: 2, of which 1 were waited for; matrix products, arithmetic and copies ran while one was open for 1% of the time, Pallas kernels for 32%

profile of v3, /device:TPU:0, one launch (start us, length us, event | category | flops | bytes accessed | tf_op | source)
XLA Modules:
  0.0 529.3 jit_solution(536265059500456883)
XLA Ops:
  8.1 0.8 stack.43
  9.6 0.9 fusion.1.refs_1_
  10.5 2.0 pack.1.refs_2_
  12.5 1.1 copy-done
  13.6 1.2 copy-done.1
  14.8 197.6 %forward.1 = (bf16[4,512,1024]{2,1,0:T(8,128)(2,1)}, bf16[8,144,768]{2,1,0:T(8,128)(2,1)}, bf16[4,512,768]{2,1,0:T(8,128)(2,1)}, bf16[4,512,256]{2,1,0:T(8,128)(...) custom-call(bf16[512,1024]{1,0:T(8,128)(2,1)S(1)} %copy-done.1, ...), custom_call_target="tpu_custom_call" | custom-call | flops 3221225472 | bytes 209715200 | tf_op jit(solution)/shard_map/forward/pallas_call | solution.py:346
  212.4 1.0 copy-done.3
  213.4 1.0 copy-done.5
  214.4 50.1 %middle.1 = (bf16[512,1024]{1,0:T(8,128)(2,1)}, f32[512,1024]{1,0:T(8,128)}, bf16[4,512,256]{2,1,0:T(8,128)(2,1)}, bf16[8,4,304,1024]{3,2,1,0:T(8,128)(2,1)}) custom-call(bf16[4,512,256]{2,1,0:T(8,128)(2,1)} %copy-done.5, bf16[512,1024]{1,0:T(8,128)(2,1)} %refs_1_.1, bf16[512,1024]{1,0:T(8,128)(2,1)} %refs_2_.1, ...), custom_call_target="tpu_custom_call" | custom-call | flops 28991029248 | bytes 62914560 | tf_op jit(solution)/shard_map/middle/pallas_call | solution.py:882
  264.6 30.3 %all_to_all.5 = bf16[4,512,256]{2,1,0:T(8,128)(2,1)S(1)} all-to-all(bf16[4,512,256]{2,1,0:T(8,128)(2,1)} %get-tuple-element.42), channel_id=1, replica_groups=mesh['dp'=8,'tensor'=4] {'tensor'}, dimensions={0} | all-to-all | bytes 2097152 | tf_op jit(solution)/shard_map/all_to_all | solution.py:976
  294.9 1.2 copy-done.4
  296.1 51.8 %attend_backward.1 = (bf16[2048,256]{1,0:T(8,128)(2,1)S(1)}, bf16[2048,256]{1,0:T(8,128)(2,1)S(1)}, bf16[2048,256]{1,0:T(8,128)(2,1)S(1)}) custom-call(bf16[2048,768]{1,0:T(8,128)(2,1)S(1)} %bitcast.41, bf16[2048,768]{1,0:T(8,128)(2,1)S(1)} %bitcast.42, bf16[2048,768]{1,0:T(8,128)(2,1)S(1)} %bitcast.43, bf16[2048,256]{1,0:T(8,128)(2,1)S(1)} %bitcast.40, ...), custom_call_target="tpu_custom_call" | custom-call | flops 42949672960 | bytes 9437184 | tf_op jit(solution)/shard_map/attend_backward/pallas_call | solution.py:661
  347.9 1.0 copy-done.6
  348.9 1.0 copy-done.7
  349.8 1.0 copy-done.8
  350.8 41.7 %reduce-scatter.3.cloned.1.call-done = bf16[1,4,304,1024]{3,2,1,0:T(8,128)(2,1)} async-done(((bf16[8,4,304,1024]{3,2,1,0:T(8,128)(2,1)}), bf16[1,4,304,1024]{3,2,1,0:T(8,128)(2,1)}) %reduce-scatter.3.cloned.1.call-update) | async-done | bytes 2490384 | tf_op jit(solution)/shard_map/reduce_scatter | solution.py:978
  392.6 117.4 %back.1 = (bf16[512,1024]{1,0:T(8,128)(2,1)}, f32[144,768]{1,0:T(8,128)}) custom-call(bf16[2048,256]{1,0:T(8,128)(2,1)} %copy-done.6, bf16[2048,256]{1,0:T(8,128)(2,1)} %copy-done.7, bf16[2048,256]{1,0:T(8,128)(2,1)} %copy-done.8, bf16[4,512,1024]{2,1,0:T(8,128)(2,1)} %get-tuple-element.51.refs_3_, bf16[8,144,768]{2,1,0:T(8,128)(2,1)} %get-tuple-element.52.refs_4_, ...), custom_call_target="tpu_custom_call" | custom-call | flops 6442450944 | bytes 209715200 | tf_op jit(solution)/shard_map/back/pallas_call | solution.py:566
  511.3 1.8 fusion.14
  513.1 1.0 fusion.12
  514.6 0.8 slice.86
  516.3 1.3 convert_element_type.8
  517.6 0.9 slice_bitcast_fusion
  518.5 1.0 copy.38
  521.1 1.0 copy.42
  (36 shorter events, 5.9 us)
Async XLA Ops:
  7.2 385.4 %reduce-scatter.3.cloned.1.call-start = ((), (), s32[]{:S(2)}) async-start(), calls=%async_computation.3 | async-start | bytes 22413312 | tf_op jit(solution)/shard_map/reduce_scatter | solution.py:978
  12.5 1.1 copy-start
  13.6 1.2 copy-start.1
  212.4 1.0 copy-start.3
  213.4 1.0 copy-start.5
  264.5 30.4 %copy-start.2 = (bf16[4,512,768]{2,1,0:T(8,128)(2,1)S(1)}, bf16[4,512,768]{2,1,0:T(8,128)(2,1)}, u32[]{:S(2)}) copy-start(bf16[4,512,768]{2,1,0:T(8,128)(2,1)} %get-tuple-element.41) | copy-start | bytes 9437188
  264.5 248.6 %reduce-scatter.5.cloned.1.call-start = ((), (), s32[]{:S(2)}) async-start(), calls=%async_computation.4 | async-start | bytes 3112960 | tf_op jit(solution)/shard_map/reduce_scatter | solution.py:981
  294.9 1.2 copy-start.4
  347.9 1.0 copy-start.6
  348.9 1.0 copy-start.7
  349.8 1.0 copy-start.8
  516.3 4.7 copy-start.9
Sparse Core Ops, SparseCore 0:
  264.6 127.8 reduce-scatter.2
  394.9 87.8 reduce-scatter.4

commit v4 on v3

--- a/solution.py
+++ b/solution.py
@@ -6,8 +6,6 @@
 from jax.sharding import PartitionSpec as P
 
 HD = 64
-LEN = 2048
-QB = 256
 PAIR = 2 * HD
 PAD = 16
 F32 = jnp.float32
@@ -381,95 +379,322 @@
     )(tokens, pack, mine)
 
 
-def back_kernel(
+def backward_kernel(
     dps,
     tps,
-    dq_ref,
-    dk_ref,
-    dv_ref,
+    scatter,
+    cross_ref,
+    packed_ref,
+    qkv_ref,
+    att_ref,
+    lse_ref,
     rows_ref,
     packs_ref,
     gsum_ref,
     tok_out,
     pack_out,
+    feed_out,
+    grad_s,
     weight_s,
-    part_s,
-    right_s,
-    left_s,
+    dq_s,
+    dk_s,
+    dv_s,
+    land_s,
     mine_s,
     theirs_s,
-    right_send,
-    right_land,
-    left_send,
-    left_land,
+    gsum_s,
+    kept_s,
+    stage_s,
+    one_a,
+    one_b,
+    two_a,
+    two_b,
+    level_s,
+    local_sem,
+    grad_send,
+    grad_land,
+    hop_send,
+    hop_land,
     pack_send,
     pack_land,
+    chip_send,
+    chip_land,
+    stage_sem,
+    one_send,
+    one_land,
+    two_send,
+    two_land,
+    level_send,
+    level_land,
 ):
     place, level = lax.axis_index("dp"), lax.axis_index("tensor")
     rows, model = gsum_ref.shape
     piece = model // dps
+    width = att_ref.shape[2]
+    pairs = width // PAIR
     cut = rows // CUTS
-    width = dq_ref.shape[1]
+    half_rows = rows // 2
+    count = packed_ref.shape[2]
+    middle_row = count // (2 * PAD) * PAD
+    spans = (pl.ds(0, middle_row), pl.ds(middle_row, count - middle_row))
+
+    load_weight = pltpu.make_async_copy(
+        packs_ref.at[:, pl.ds(0, piece)], weight_s, local_sem.at[0]
+    )
+    load_sum = pltpu.make_async_copy(gsum_ref, gsum_s, local_sem.at[1])
+    own_grad = pltpu.make_async_copy(cross_ref.at[level], grad_s.at[level], local_sem.at[2])
+    load_weight.start()
+    load_sum.start()
+    own_grad.start()
     greet(dps, tps)
-    weight_s[...] = packs_ref[:, :piece].reshape(weight_s.shape)
+
+    def cross(step):
+        other = lax.rem(level + step, tps)
+        return pltpu.make_async_remote_copy(
+            src_ref=cross_ref.at[other],
+            dst_ref=grad_s.at[level],
+            send_sem=grad_send.at[other],
+            recv_sem=grad_land.at[level],
+            device_id={"tensor": other},
+        )
+
+    def crossed(other):
+        return pltpu.make_async_remote_copy(
+            src_ref=cross_ref.at[other],
+            dst_ref=grad_s.at[other],
+            send_sem=grad_send.at[other],
+            recv_sem=grad_land.at[other],
+            device_id={"tensor": other},
+        )
+
+    for step in range(1, tps):
+        cross(step).start()
+
+    def block_of(kind):
+        block = place
+        if kind in (0, 2):
+            block = flipped(block, 1)
+        if kind in (0, 1):
+            block = flipped(block, 2)
+        return block
+
+    def level_of(turn):
+        return lax.rem(level + 1 + turn, tps)
+
+    def chip(kind, turn):
+        return pltpu.make_async_remote_copy(
+            src_ref=packed_ref.at[flipped(block_of(kind), 0), level_of(turn)],
+            dst_ref=kept_s.at[turn * 4 + kind],
+            send_sem=chip_send.at[turn * 4 + kind],
+            recv_sem=chip_land.at[turn * 4 + kind],
+            device_id={"dp": flipped(place, 0)},
+        )
+
+    def load(kind, turn, slot):
+        return pltpu.make_async_copy(
+            packed_ref.at[block_of(kind), level_of(turn)], stage_s.at[slot], stage_sem.at[slot]
+        )
+
+    def plane_one(kind, turn, half):
+        bit = 2 - half
+        target = one_b if half else one_a
+        at = turn * 2 + (0 if kind == 0 else 1)
+        return pltpu.make_async_remote_copy(
+            src_ref=kept_s.at[turn * 4 + kind, spans[half]],
+            dst_ref=target.at[at],
+            send_sem=one_send.at[at, half],
+            recv_sem=one_land.at[at, half],
+            device_id={"dp": flipped(place, bit)},
+        )
+
+    def plane_two(turn, half):
+        bit = 1 + half
+        target = two_b if half else two_a
+        return pltpu.make_async_remote_copy(
+            src_ref=kept_s.at[turn * 4 + 2 - half, spans[half]],
+            dst_ref=target.at[turn],
+            send_sem=two_send.at[turn, half],
+            recv_sem=two_land.at[turn, half],
+            device_id={"dp": flipped(place, bit)},
+        )
+
+    def over_z(turn):
+        return pltpu.make_async_remote_copy(
+            src_ref=kept_s.at[turn * 4 + 3],
+            dst_ref=level_s.at[turn],
+            send_sem=level_send.at[turn],
+            recv_sem=level_land.at[turn],
+            device_id={"tensor": level_of(turn)},
+        )
+
+    def add_to(slot, half, source):
+        kept_s[slot, spans[half]] = (
+            kept_s[slot, spans[half]].astype(F32) + source.astype(F32)
+        ).astype(BF)
+
+    def chip_in(kind, turn):
+        slot = kind % 2
+        load(kind, turn, slot).wait()
+        chip(kind, turn).wait_recv()
+        at = turn * 4 + kind
+        kept_s[at] = (kept_s[at].astype(F32) + stage_s[slot].astype(F32)).astype(BF)
+        if kind in (0, 1):
+            plane_one(kind, turn, 0).start()
+        if kind in (0, 2):
+            plane_one(kind, turn, 1).start()
+
+    def one_in(turn):
+        plane_one(0, turn, 0).wait_recv()
+        add_to(turn * 4 + 2, 0, one_a[turn * 2])
+        plane_two(turn, 0).start()
+        plane_one(0, turn, 1).wait_recv()
+        add_to(turn * 4 + 1, 1, one_b[turn * 2])
+        plane_two(turn, 1).start()
+        plane_one(1, turn, 0).wait_recv()
+        add_to(turn * 4 + 3, 0, one_a[turn * 2 + 1])
+        plane_one(2, turn, 1).wait_recv()
+        add_to(turn * 4 + 3, 1, one_b[turn * 2 + 1])
+
+    def two_in(turn):
+        plane_two(turn, 0).wait_recv()
+        add_to(turn * 4 + 3, 0, two_a[turn])
+        plane_two(turn, 1).wait_recv()
+        add_to(turn * 4 + 3, 1, two_b[turn])
+        if turn < tps - 1:
+            over_z(turn).start()
+
+    if scatter:
+        load(0, 0, 0).start()
+        for turn in range(tps):
+            for kind in range(4):
+                chip(kind, turn).start()
+
+    dk_s[...] = jnp.zeros_like(dk_s)
+    dv_s[...] = jnp.zeros_like(dv_s)
+    own_grad.wait()
+
+    def attend(turn, carry):
+        pair = lax.rem(turn, pairs)
+        half = lax.rem(turn // pairs, 2)
+        step = turn // (2 * pairs)
+        target = lax.rem(level + step, tps)
+
+        @pl.when((lax.rem(turn, 2 * pairs) == 0) & (step > 0))
+        def _():
+            crossed(target).wait_recv()
+
+        span = pl.ds(pl.multiple_of(half * half_rows, half_rows), half_rows)
+        lanes = pl.ds(pl.multiple_of(pair * PAIR, PAIR), PAIR)
+        query = qkv_ref[target, span, lanes] * jnp.asarray(0.125, BF)
+        key = qkv_ref[:, :, pl.ds(pl.multiple_of(width + pair * PAIR, PAIR), PAIR)]
+        value = qkv_ref[:, :, pl.ds(pl.multiple_of(2 * width + pair * PAIR, PAIR), PAIR)]
+        key, value = key.reshape(tps * rows, PAIR), value.reshape(tps * rows, PAIR)
+        grad = grad_s[target, span, lanes]
+        products = jnp.transpose(grad.astype(F32) * att_ref[target, span, lanes].astype(F32))
+        where = pl.ds(pl.multiple_of(target * rows + half * half_rows, half_rows), half_rows)
+        logsums = lse_ref[pair, :, where]
+        grad_query = None
+        for head in range(2):
+            key_head, value_head = one_head(key, head), one_head(value, head)
+            inner = jnp.sum(products[HD * head : HD * head + HD], axis=0, keepdims=True)
+            logsum = logsums[4 * head : 4 * head + 1]
+            probs = jnp.exp(contract(key_head, query, 1, 1) - logsum)
+            grad_probs = contract(value_head, grad, 1, 1)
+            grad_scores = (probs * (grad_probs - inner)).astype(BF)
+            dv_s[:, lanes] += contract(probs.astype(BF), one_head(grad, head), 1, 0)
+            dk_s[:, lanes] += contract(grad_scores, one_head(query, head), 1, 0)
+            part = contract(grad_scores, key_head, 0, 0)
+            grad_query = part if grad_query is None else grad_query + part
+        dq_s[where, lanes] = (grad_query * 0.125).astype(BF)
+
+        if scatter:
+            for kind in range(4):
+
+                @pl.when(lax.rem(turn, 4) == kind)
+                def _():
+                    if kind < 3:
+                        load(kind + 1, turn // 4, (kind + 1) % 2).start()
+                    else:
+
+                        @pl.when(turn // 4 < tps - 1)
+                        def _():
+                            load(0, turn // 4 + 1, 0).start()
+
+                    chip_in(kind, turn // 4)
+
+            @pl.when(turn == 9)
+            def _():
+                one_in(0)
+
+            @pl.when(turn == 13)
+            def _():
+                two_in(0)
+
+            @pl.when(turn == 15)
+            def _():
+                one_in(1)
+
+        return carry
+
+    lax.fori_loop(0, 2 * pairs * tps, attend, 0)
+    load_weight.wait()
+    refs = (dq_s, dk_s, dv_s)
 
     def rows_of(block):
         span = pl.ds(pl.multiple_of(block * rows, rows), rows)
         total = None
-        for index, ref in enumerate((dq_ref, dk_ref, dv_ref)):
-            weight = weight_s[:, index * width : (index + 1) * width]
-            part = contract(ref[span], weight, 1, 1)
+        for index, ref in enumerate(refs):
+            weight = weight_s[:, :, index * width : (index + 1) * width].reshape(model, width)
+            part = contract(ref[span].astype(BF), weight, 1, 1)
             total = part if total is None else total + part
-        part_s[block] = total.astype(BF)
+        return total
 
     def hop(block, chunk, rightward):
+        slot = block + 1 if rightward else block
         span = pl.ds(chunk * cut, cut)
-        land = right_s if rightward else left_s
         return pltpu.make_async_remote_copy(
-            src_ref=part_s.at[block, span],
-            dst_ref=land.at[block, span],
-            send_sem=(right_send if rightward else left_send).at[block, chunk],
-            recv_sem=(right_land if rightward else left_land).at[block, chunk],
+            src_ref=land_s.at[slot, span],
+            dst_ref=land_s.at[slot, span],
+            send_sem=hop_send.at[slot, chunk],
+            recv_sem=hop_land.at[slot, chunk],
             device_id={"tensor": level + 1 if rightward else level - 1},
         )
 
-    def gather_in(block, chunk, rightward):
-        hop(block, chunk, rightward).wait_recv()
-        span = pl.ds(chunk * cut, cut)
-        land = right_s if rightward else left_s
-        part_s[block, span] = (
-            part_s[block, span].astype(F32) + land[block, span].astype(F32)
-        ).astype(BF)
+    def begin(block, rightward):
+        land_s[block + 1 if rightward else block] = rows_of(block).astype(BF)
+        for chunk in range(CUTS):
+            hop(block, chunk, rightward).start()
+
+    def carry_on(block, rightward):
+        slot = block + 1 if rightward else block
+        own = rows_of(block)
+        for chunk in range(CUTS):
+            span = pl.ds(chunk * cut, cut)
+            hop(block, chunk, rightward).wait_recv()
+            land_s[slot, span] = (
+                land_s[slot, span].astype(F32) + own[chunk * cut : (chunk + 1) * cut]
+            ).astype(BF)
+            hop(block, chunk, rightward).start()
 
     for step in range(tps - 1, 0, -1):
-
-        @pl.when(level + step < tps)
-        def _():
-            rows_of(level + step)
 
         @pl.when((level + step < tps) & (level == 0))
         def _():
-            for chunk in range(CUTS):
-                hop(level + step, chunk, True).start()
-
-        @pl.when(level - step >= 0)
-        def _():
-            rows_of(level - step)
+            begin(level + step, True)
 
         @pl.when((level - step >= 0) & (level == tps - 1))
         def _():
-            for chunk in range(CUTS):
-                hop(level - step, chunk, False).start()
-
-    rows_of(level)
-    model_rows = rows_ref.reshape(tps * rows, model)
+            begin(level - step, False)
+
+    if scatter:
+        two_in(1)
     tail = jnp.concatenate(
-        [jnp.sum(ref[...].astype(F32), axis=0, keepdims=True) for ref in (dq_ref, dk_ref, dv_ref)],
-        axis=1,
+        [jnp.sum(ref[...].astype(BF).astype(F32), axis=0, keepdims=True) for ref in refs], axis=1
     )
-    for index, ref in enumerate((dq_ref, dk_ref, dv_ref)):
-        grad = contract(model_rows[...], ref[...], 0, 0).astype(BF).reshape(dps, piece, width)
-        mine_s[:, :piece, index * width : (index + 1) * width] = grad
+    tokens = rows_ref.reshape(tps * rows, model)
+    for index, ref in enumerate(refs):
+        grad = contract(tokens[...], ref[...].astype(BF), 0, 0).astype(BF)
+        mine_s[:, :piece, index * width : (index + 1) * width] = grad.reshape(dps, piece, width)
     mine_s[:, piece:] = jnp.broadcast_to(tail.astype(BF)[None], (dps, PAD, 3 * width))
 
     def exchange(index, bit, other):
@@ -489,8 +714,7 @@
             blocks = blocks + [flipped(block, bit) for block in blocks]
         return blocks
 
-    starts = []
-    at = 0
+    starts, at = [], 0
     for done in range(len(order)):
         starts.append(at)
         at += dps >> (done + 1)
@@ -507,31 +731,38 @@
             ).astype(BF)
 
     pack_start(0)
-    pack_done = 0
-    for step in range(tps - 1, 0, -1):
-        for chunk in range(CUTS):
+    for turn in range(max(tps - 1, len(order))):
+        step = tps - 1 - turn
+        if scatter and turn == 0:
+            one_in(2)
+        if step > 0:
 
             @pl.when((level > 0) & (level + step < tps))
             def _():
-                gather_in(level + step, chunk, True)
-                hop(level + step, chunk, True).start()
+                carry_on(level + step, True)
 
             @pl.when((level < tps - 1) & (level - step >= 0))
             def _():
-                gather_in(level - step, chunk, False)
-                hop(level - step, chunk, False).start()
-
-        if pack_done < len(order):
-            pack_finish(pack_done)
-            pack_done += 1
-            if pack_done < len(order):
-                pack_start(pack_done)
-    while pack_done < len(order):
-        pack_finish(pack_done)
-        pack_done += 1
-        if pack_done < len(order):
-            pack_start(pack_done)
+                carry_on(level - step, False)
+
+        if turn < len(order):
+            pack_finish(turn)
+            if turn + 1 < len(order):
+                pack_start(turn + 1)
+        if scatter and turn == 0:
+            two_in(2)
+            one_in(3)
+        if scatter and turn == 1:
+            two_in(3)
     pack_out[...] = mine_s[place].astype(F32)
+    own = rows_of(level)
+    load_sum.wait()
+    if scatter:
+        total = kept_s[(tps - 1) * 4 + 3].astype(F32)
+        for turn in range(tps - 1):
+            over_z(turn).wait_recv()
+            total = total + level_s[turn].astype(F32)
+        feed_out[...] = total
     for chunk in range(CUTS):
 
         @pl.when(level > 0)
@@ -542,11 +773,12 @@
         def _():
             hop(level, chunk, False).wait_recv()
 
-    total = gsum_ref[...] + part_s[level].astype(F32)
-    total = total + jnp.where(level > 0, right_s[level].astype(F32), 0.0)
-    total = total + jnp.where(level < tps - 1, left_s[level].astype(F32), 0.0)
+    total = gsum_s[...] + own
+    total = total + jnp.where(level > 0, land_s[level + 1].astype(F32), 0.0)
+    total = total + jnp.where(level < tps - 1, land_s[level].astype(F32), 0.0)
     tok_out[...] = total.astype(BF)
     for step in range(1, tps):
+        cross(step).wait_send()
         for chunk in range(CUTS):
 
             @pl.when(level + step < tps)
@@ -557,38 +789,88 @@
             def _():
                 hop(level - step, chunk, False).wait_send()
 
-
-def back(grads, rows_full, packs, grad_sum):
+    if scatter:
+        for turn in range(tps):
+            for kind in range(4):
+                chip(kind, turn).wait_send()
+            plane_one(0, turn, 0).wait_send()
+            plane_one(1, turn, 0).wait_send()
+            plane_one(0, turn, 1).wait_send()
+            plane_one(2, turn, 1).wait_send()
+            plane_two(turn, 0).wait_send()
+            plane_two(turn, 1).wait_send()
+            if turn < tps - 1:
+                over_z(turn).wait_send()
+    else:
+        feed_out[...] = jnp.zeros_like(feed_out)
+
+
+def backward(grad_cross, packed, qkv, attended, logsum, rows_full, packs, grad_sum, scatter):
     rows, model = grad_sum.shape
     tps = rows_full.shape[0]
     dps, pack_rows, columns = packs.shape
+    width = columns // 3
+    count = packed.shape[2]
+    middle_row = count // (2 * PAD) * PAD
     vmem = pl.BlockSpec(memory_space=pltpu.VMEM)
+    hbm = pl.BlockSpec(memory_space=pl.ANY)
+    dma = pltpu.SemaphoreType.DMA
+    slots = 4 * tps if scatter else 1
+
+    def buffer(*shape):
+        return pltpu.VMEM(shape if scatter else (1, 16, model), BF)
+
     return pl.pallas_call(
-        lambda *refs: back_kernel(dps, tps, *refs),
-        in_specs=[vmem] * 6,
-        out_specs=[vmem] * 2,
+        lambda *refs: backward_kernel(dps, tps, scatter, *refs),
+        in_specs=[hbm, hbm, vmem, vmem, vmem, vmem, hbm, hbm],
+        out_specs=[vmem] * 3,
         out_shape=[
             jax.ShapeDtypeStruct((rows, model), BF),
             jax.ShapeDtypeStruct((pack_rows, columns), F32),
+            jax.ShapeDtypeStruct((count, model), F32),
         ],
         scratch_shapes=[
-            pltpu.VMEM((model, columns), BF),
-            pltpu.VMEM((tps, rows, model), BF),
-            pltpu.VMEM((tps, rows, model), BF),
-            pltpu.VMEM((tps, rows, model), BF),
+            pltpu.VMEM((tps, rows, width), BF),
+            pltpu.VMEM((dps, model // dps, columns), BF),
+            pltpu.VMEM((tps * rows, width), BF),
+            pltpu.VMEM((tps * rows, width), F32),
+            pltpu.VMEM((tps * rows, width), F32),
+            pltpu.VMEM((tps + 1, rows, model), BF),
             pltpu.VMEM(packs.shape, BF),
             pltpu.VMEM(packs.shape, BF),
-        ]
-        + [pltpu.SemaphoreType.DMA((tps, CUTS))] * 4
-        + [pltpu.SemaphoreType.DMA((dps,))] * 2,
+            pltpu.VMEM((rows, model), F32),
+            buffer(slots, count, model),
+            buffer(2, count, model),
+            buffer(2 * tps, middle_row, model),
+            buffer(2 * tps, count - middle_row, model),
+            buffer(tps, middle_row, model),
+            buffer(tps, count - middle_row, model),
+            buffer(tps - 1, count, model),
+            dma((3,)),
+            dma((tps,)),
+            dma((tps,)),
+            dma((tps + 1, CUTS)),
+            dma((tps + 1, CUTS)),
+            dma((dps,)),
+            dma((dps,)),
+            dma((slots,)),
+            dma((slots,)),
+            dma((2,)),
+            dma((2 * tps, 2)),
+            dma((2 * tps, 2)),
+            dma((tps, 2)),
+            dma((tps, 2)),
+            dma((tps - 1,)),
+            dma((tps - 1,)),
+        ],
         cost_estimate=pl.CostEstimate(
             flops=4 * tps * rows * model * columns, bytes_accessed=200 << 20, transcendentals=0
         ),
         compiler_params=pltpu.CompilerParams(
-            vmem_limit_bytes=56 << 20, collective_id=2, has_side_effects=True
+            vmem_limit_bytes=63 << 20, collective_id=2, has_side_effects=True
         ),
-        name="back",
-    )(*grads, rows_full, packs, grad_sum)
+        name="backward",
+    )(grad_cross, packed, qkv, attended, logsum, rows_full, packs, grad_sum)
 
 
 def pack_kernel(hidden_ref, down_ref, out_ref, vec_ref, packed_ref):
@@ -618,66 +900,6 @@
         out_shape=jax.ShapeDtypeStruct((2 * piece + piece // chunks + PAD, wide), BF),
         name="pack",
     )(hidden, down, out, vec)
-
-
-def attend_backward_kernel(
-    q_ref, k_ref, v_ref, grad_ref, out_ref, logsum_ref, dq_ref, dk_ref, dv_ref, dk_sum, dv_sum
-):
-    step = pl.program_id(1)
-    query = q_ref[...] * jnp.asarray(0.125, BF)
-    key, value, grad = k_ref[...], v_ref[...], grad_ref[...]
-    products = jnp.transpose(grad.astype(F32) * out_ref[...].astype(F32))
-
-    @pl.when(step == 0)
-    def _():
-        dk_sum[...] = jnp.zeros_like(dk_sum)
-        dv_sum[...] = jnp.zeros_like(dv_sum)
-
-    grad_query = None
-    for head in range(2):
-        key_head, value_head = one_head(key, head), one_head(value, head)
-        inner = jnp.sum(products[HD * head : HD * head + HD], axis=0, keepdims=True)
-        logsum = logsum_ref[0, 4 * head : 4 * head + 1, :]
-        probs = jnp.exp(contract(key_head, query, 1, 1) - logsum)
-        grad_probs = contract(value_head, grad, 1, 1)
-        grad_scores = (probs * (grad_probs - inner)).astype(BF)
-        dv_sum[...] += contract(probs.astype(BF), one_head(grad, head), 1, 0)
-        dk_sum[...] += contract(grad_scores, one_head(query, head), 1, 0)
-        part = contract(grad_scores, key_head, 0, 0)
-        grad_query = part if grad_query is None else grad_query + part
-    dq_ref[...] = (grad_query * 0.125).astype(BF)
-
-    @pl.when(step == pl.num_programs(1) - 1)
-    def _():
-        dk_ref[...] = dk_sum[...].astype(BF)
-        dv_ref[...] = dv_sum[...].astype(BF)
-
-
-def attend_backward(qkv, grad, out, logsum):
-    width = qkv.shape[1] // 3
-    pairs = width // PAIR
-    block = pl.BlockSpec((QB, PAIR), lambda i, j: (j, i))
-    whole = pl.BlockSpec((LEN, PAIR), lambda i, j: (0, i))
-    return pl.pallas_call(
-        attend_backward_kernel,
-        grid=(width // PAIR, LEN // QB),
-        in_specs=[
-            block,
-            pl.BlockSpec((LEN, PAIR), lambda i, j: (0, i + pairs)),
-            pl.BlockSpec((LEN, PAIR), lambda i, j: (0, i + 2 * pairs)),
-            block,
-            block,
-            pl.BlockSpec((1, 8, QB), lambda i, j: (i, 0, j)),
-        ],
-        out_specs=[block, whole, whole],
-        out_shape=[jax.ShapeDtypeStruct((LEN, width), BF)] * 3,
-        scratch_shapes=[pltpu.VMEM((LEN, PAIR), F32)] * 2,
-        cost_estimate=pl.CostEstimate(
-            flops=40 * LEN * LEN * width, bytes_accessed=18 * LEN * width, transcendentals=0
-        ),
-        compiler_params=pltpu.CompilerParams(vmem_limit_bytes=40 << 20),
-        name="attend_backward",
-    )(qkv, qkv, qkv, grad, out, logsum)
 
 
 def row_mean(values):
@@ -970,16 +1192,16 @@
     rows_full, packs, qkv, attended, logsum, crossed, gathered = forward(
         tokens, attn_pack, packed_weights, dps, tps
     )
-    qkv = qkv.reshape(tps * rows, 3 * width)
-    attended = attended.reshape(tps * rows, width)
     output, grad_sum, grad_cross, packed = middle(crossed, tokens, cotangent, gathered)
-    grad_attended = lax.all_to_all(grad_cross, "tensor", 0, 0, tiled=False)
-    grad_attended = grad_attended.reshape(tps * rows, width)
-    packed = lax.psum_scatter(packed, "dp", scatter_dimension=0, tiled=False)
-    grads = attend_backward(qkv, grad_attended, attended, logsum)
-    packed, grads = lax.optimization_barrier((packed, grads))
-    packed = lax.psum_scatter(packed, "tensor", scatter_dimension=0, tiled=False).astype(F32)
-    grad_tokens, attn_grads = back(grads, rows_full, packs, grad_sum)
+    scatter = dps == 8 and tps == 4 and width == 2 * PAIR
+    grad_tokens, attn_grads, summed = backward(
+        grad_cross, packed, qkv, attended, logsum, rows_full, packs, grad_sum, scatter
+    )
+    if scatter:
+        packed = summed
+    else:
+        packed = lax.psum_scatter(packed, "dp", scatter_dimension=0, tiled=False)
+        packed = lax.psum_scatter(packed, "tensor", scatter_dimension=0, tiled=False).astype(F32)
 
     def share(values, count):
         return lax.dynamic_slice_in_dim(values, place * count, count, 0)

time: 537 us -> 454 us (0.85)
  the two profiles are of different devices: /device:TPU:0 before, /device:TPU:18 now
where the time goes in v4:
time: 454 us; the launch traced here: 447 us
  Pallas kernels  425 us (94%)
  local copies, waits for them, and re-layouts  18.5 us (4%)
    pallas_call x1, Pallas kernels, backward(): pl.pallas_call(lambda *refs: backward_kernel(dps, tps, scatter, *refs), i...  211 us
    pallas_call x1, Pallas kernels, forward(): pl.pallas_call(lambda *refs: forward_kernel(dps, tps, *refs), in_specs=[v...  162 us
    pallas_call x1, Pallas kernels, middle(): pl.pallas_call(lambda *refs: middle_kernel((dps, tps, piece, chunks), *re...  50 us

profile of v4, /device:TPU:18, one launch (start us, length us, event | category | flops | bytes accessed | tf_op | source)
XLA Modules:
  0.0 446.8 jit_solution(9901700120565143245)
XLA Ops:
  0.7 0.7 pad_maximum_fusion
  1.7 0.8 stack.43
  2.5 0.6 pad.9.vec_ref
  3.1 0.9 fusion.1.refs_1_
  4.0 2.0 pack.1.refs_2_
  6.0 1.1 copy-done.1
  7.1 1.2 copy-done.3
  8.3 161.9 %forward.1 = (bf16[4,512,1024]{2,1,0:T(8,128)(2,1)}, bf16[8,144,768]{2,1,0:T(8,128)(2,1)}, bf16[4,512,768]{2,1,0:T(8,128)(2,1)}, bf16[4,512,256]{2,1,0:T(8,128)(...) custom-call(bf16[512,1024]{1,0:T(8,128)(2,1)S(1)} %copy-done.3, ...), custom_call_target="tpu_custom_call" | custom-call | flops 3221225472 | bytes 209715200 | tf_op jit(solution)/shard_map/forward/pallas_call | solution.py:344
  170.2 1.0 copy-done
  171.2 0.7 copy-done.2
  171.9 1.0 copy-done.4
  172.8 50.0 %middle.1 = (bf16[512,1024]{1,0:T(8,128)(2,1)}, f32[512,1024]{1,0:T(8,128)}, bf16[4,512,256]{2,1,0:T(8,128)(2,1)}, bf16[8,4,304,1024]{3,2,1,0:T(8,128)(2,1)}) custom-call(bf16[4,512,256]{2,1,0:T(8,128)(2,1)} %copy-done.4, bf16[512,1024]{1,0:T(8,128)(2,1)} %refs_1_.1, bf16[512,1024]{1,0:T(8,128)(2,1)} %refs_2_.1, ...), custom_call_target="tpu_custom_call" | custom-call | flops 28991029248 | bytes 62914560 | tf_op jit(solution)/shard_map/middle/pallas_call | solution.py:1104
  222.9 211.4 %backward.1 = (bf16[512,1024]{1,0:T(8,128)(2,1)}, f32[144,768]{1,0:T(8,128)}, f32[304,1024]{1,0:T(8,128)}) custom-call(bf16[4,512,256]{2,1,0:T(8,128)(2,1)} %get-tuple-element.34.refs_0_, bf16[8,4,304,1024]{3,2,1,0:T(8,128)(2,1)} %get-tuple-element.35.refs_1_, bf16[4,512,768]{2,1,0:T(8,128)(2,1)} %get-tuple-element.36.refs_2_, bf16[4,512,256]{2,1,0:T(8,128)(2,1)} %copy-done, ...), custom_call_target="tpu_custom_call" | custom-call | flops 6442450944 | bytes 209715200 | tf_op jit(solution)/shard_map/backward/pallas_call | solution.py:823
  434.3 0.7 fusion.13
  435.1 1.8 fusion.14
  436.8 0.6 fusion.3
  437.4 1.0 fusion.12
  438.5 0.5 fusion.11
  439.0 0.5 fusion.9
  440.5 0.9 slice.56
  441.5 2.1 slice_bitcast_fusion
  443.5 1.0 copy.38
  444.5 0.8 copy.37
  445.3 1.0 copy.45
  (18 shorter events, 1.4 us)
Async XLA Ops:
  6.0 1.1 copy-start.1
  7.1 1.2 copy-start.3
  170.2 1.0 copy-start
  171.2 0.7 copy-start.2
  171.9 1.0 copy-start.4
  436.8 8.5 %copy-start.5 = (bf16[512,1024]{1,0:T(8,128)(2,1)S(1)}, bf16[512,1024]{1,0:T(8,128)(2,1)}, u32[]{:S(2)}) copy-start(bf16[512,1024]{1,0:T(8,128)(2,1)} %get-tuple-element.121) | copy-start | bytes 3145732

commit v5 on v4

--- a/solution.py
+++ b/solution.py
@@ -32,19 +32,35 @@
     return index + size - 2 * size * lax.rem(index // size, 2)
 
 
-def bit_order(dps):
-    count = dps.bit_length() - 1
-    return tuple(range(1, count)) + (0,)
-
-
 def greet(dps, tps):
     place, level = lax.axis_index("dp"), lax.axis_index("tensor")
     barrier = pltpu.get_barrier_semaphore()
-    for bit in bit_order(dps):
+    bits = range(1, dps.bit_length() - 1)
+    for bit in bits:
         pl.semaphore_signal(barrier, inc=1, device_id={"dp": flipped(place, bit)})
+    pl.semaphore_signal(barrier, inc=1, device_id={"dp": flipped(place, 0)})
     for step in range(1, tps):
-        pl.semaphore_signal(barrier, inc=1, device_id={"tensor": lax.rem(level + step, tps)})
-    pl.semaphore_wait(barrier, len(bit_order(dps)) + tps - 1)
+        other = lax.rem(level + step, tps)
+        pl.semaphore_signal(barrier, inc=1, device_id={"tensor": other})
+        pl.semaphore_signal(barrier, inc=1, device_id={"dp": flipped(place, 0), "tensor": other})
+    pl.semaphore_wait(barrier, len(bits) + 2 * tps - 1)
+
+
+def seat(place, level):
+    core = lax.rem(place, 2)
+    group = level // 2
+    gate = lax.rem((level + 1) // 2, 2)
+    mate = level + 1 - 2 * lax.rem(level, 2)
+    near, far = 2 - group, 3 - 3 * group
+    heads = lax.rem(level + 2 * core, 4)
+    return core, group, gate, mate, near, far, heads
+
+
+def ordered(level, step):
+    group = level // 2
+    gate = lax.rem((level + 1) // 2, 2)
+    turned = step + gate * (step // 2) * (5 - 2 * step)
+    return (1 - group) * (3 - turned) + group * turned
 
 
 def forward_kernel(
@@ -61,8 +77,9 @@
     cross_ref,
     gath_ref,
     weight_s,
-    right_sem,
-    left_sem,
+    away_sem,
+    mate_sem,
+    core_sem,
     land_sem,
     pack_send,
     pack_land,
@@ -85,22 +102,52 @@
     spans = (pl.ds(0, middle_row), pl.ds(middle_row, count - middle_row))
     bits = tuple(range(1, dps.bit_length() - 1))
     orders = (bits, bits[::-1])
+    core, group, gate, mate, near, far, heads = seat(place, level)
+    lead = core == group
+    partner = flipped(place, 0)
     own = pltpu.make_async_copy(tok_ref, rows_ref.at[level], local_sem.at[0])
     own_pack = pltpu.make_async_copy(pack_ref, packs_ref.at[place], local_sem.at[1])
     own_block = pltpu.make_async_copy(mine_ref, gath_ref.at[place, level], local_sem.at[2])
-    own.start()
-    own_pack.start()
     own_block.start()
+
+    @pl.when(lead)
+    def _():
+        own.start()
+
+    @pl.when(core == 0)
+    def _():
+        own_pack.start()
+
     greet(dps, tps)
 
-    def hop(block, chunk, rightward, first=False):
+    def away(chunk):
+        span = pl.ds(chunk * cut, cut)
+        return pltpu.make_async_remote_copy(
+            src_ref=tok_ref.at[span],
+            dst_ref=rows_ref.at[level, span],
+            send_sem=away_sem.at[chunk],
+            recv_sem=land_sem.at[level, chunk],
+            device_id={"tensor": near},
+        )
+
+    def to_mate(block, chunk, first=False):
         span = pl.ds(chunk * cut, cut)
         return pltpu.make_async_remote_copy(
             src_ref=tok_ref.at[span] if first else rows_ref.at[block, span],
             dst_ref=rows_ref.at[block, span],
-            send_sem=(right_sem if rightward else left_sem).at[block, chunk],
+            send_sem=mate_sem.at[block, chunk],
             recv_sem=land_sem.at[block, chunk],
-            device_id={"tensor": level + 1 if rightward else level - 1},
+            device_id={"tensor": mate},
+        )
+
+    def to_core(block, chunk, first=False):
+        span = pl.ds(chunk * cut, cut)
+        return pltpu.make_async_remote_copy(
+            src_ref=tok_ref.at[span] if first else rows_ref.at[block, span],
+            dst_ref=rows_ref.at[block, span],
+            send_sem=core_sem.at[block, chunk],
+            recv_sem=land_sem.at[block, chunk],
+            device_id={"dp": partner},
         )
 
     def to_level(step, half):
@@ -160,86 +207,113 @@
                 device_id={"tensor": lax.rem(level + back, tps)},
             ).wait_recv()
 
+    even = place - core
+    opposite = lax.rem(level + 2, tps)
+
+    def pack_to(index, block, device):
+        return pltpu.make_async_remote_copy(
+            src_ref=pack_ref,
+            dst_ref=packs_ref.at[block],
+            send_sem=pack_send.at[index],
+            recv_sem=pack_land.at[block],
+            device_id=device,
+        )
+
+    pack_to(0, place, {"dp": even + 1, "tensor": opposite}).start()
+    for half in range(2):
+        to_level(1, half).start()
+    for half in range(2):
+        to_level(3, half).start()
     for chunk in range(CUTS):
 
-        @pl.when(level < tps - 1)
+        @pl.when(lead)
         def _():
-            hop(level, chunk, True, True).start()
-
-        @pl.when(level > 0)
+            to_mate(level, chunk, True).start()
+            to_core(level, chunk, True).start()
+
+        @pl.when(core != group)
         def _():
-            hop(level, chunk, False, True).start()
-
-    own_pack.wait()
-    known = [place]
-    for bit in bit_order(dps):
-        copies = []
+            away(chunk).start()
+
+    pass_on(0, 0)
+
+    @pl.when(core == 1)
+    def _():
+        pack_to(1, place, {"dp": even}).start()
+        pack_to(0, even, {"dp": even}).wait_recv()
+
+    @pl.when(core == 0)
+    def _():
+        own_pack.wait()
+
+    pack_to(0, even + 1, {"dp": even}).wait_recv()
+
+    def pack_on(block, index, bit):
+        return pltpu.make_async_remote_copy(
+            src_ref=packs_ref.at[block],
+            dst_ref=packs_ref.at[block],
+            send_sem=pack_send.at[index],
+            recv_sem=pack_land.at[block],
+            device_id={"dp": flipped(place, bit)},
+        )
+
+    known = [even, even + 1]
+    sent = 2
+    pack_sends = []
+    for bit in bits:
         for block in known:
-            copies.append(
-                pltpu.make_async_remote_copy(
-                    src_ref=packs_ref.at[block],
-                    dst_ref=packs_ref.at[block],
-                    send_sem=pack_send.at[block],
-                    recv_sem=pack_land.at[block],
-                    device_id={"dp": flipped(place, bit)},
-                )
-            )
-            copies[-1].start()
-        for copy in copies:
-            copy.wait_send()
+            pack_on(block, sent, bit).start()
+            pack_sends.append((block, sent, bit))
+            sent += 1
         more = [flipped(block, bit) for block in known]
         for block in more:
-            pltpu.make_async_remote_copy(
-                src_ref=packs_ref.at[block],
-                dst_ref=packs_ref.at[block],
-                send_sem=pack_send.at[block],
-                recv_sem=pack_land.at[block],
-                device_id={"dp": flipped(place, bit)},
-            ).wait_recv()
+            pack_on(block, 0, bit).wait_recv()
         known = known + more
-    pass_on(0, 0)
     weight_s[...] = packs_ref[:, :piece].reshape(weight_s.shape)
     bias = jnp.sum(packs_ref[:, piece : piece + PAD].astype(F32), axis=0)[0:1]
 
     def project(block):
         qkv_ref[block] = (contract(rows_ref[block], weight_s[...], 1, 0) + bias).astype(BF)
 
-    own.wait()
-    project(level)
-    for step in range(1, tps):
+    def advance(step, stage):
+        if step and stage == 0:
+            level_in(step)
+        pass_on(step, stage)
+
+    @pl.when(lead)
+    def _():
+        own.wait()
+
+    for index, block in enumerate((level, mate, near, far)):
         for chunk in range(CUTS):
-
-            @pl.when(level - step >= 0)
+            if index:
+
+                @pl.when(lead)
+                def _():
+                    to_core(block, chunk).wait_recv()
+
+                if index > 1:
+
+                    @pl.when(lead & (gate == 1))
+                    def _():
+                        to_mate(block, chunk).start()
+
+                @pl.when(lead)
+                def _():
+                    to_core(block, chunk).start()
+
+            @pl.when(core != group)
             def _():
-                hop(level - step, chunk, True).wait_recv()
-
-            @pl.when((level - step >= 0) & (level < tps - 1))
-            def _():
-                hop(level - step, chunk, True).start()
-
-            @pl.when(level + step < tps)
-            def _():
-                hop(level + step, chunk, False).wait_recv()
-
-            @pl.when((level + step < tps) & (level > 0))
-            def _():
-                hop(level + step, chunk, False).start()
-
-        @pl.when(level - step >= 0)
-        def _():
-            project(level - step)
-
-        @pl.when(level + step < tps)
-        def _():
-            project(level + step)
-
-        if step == min(2, tps - 1):
-            for other in range(1, tps):
+                to_core(block, chunk).wait_recv()
+
+        project(block)
+        for other, when in ((2, 1),):
+            if when == index:
                 for half in range(2):
                     to_level(other, half).start()
-        if step <= len(bits):
-            pass_on(0, step)
-    for stage in range(tps, len(bits) + 1):
+        for step, stage in (((0, 1),), ((1, 0),), ((0, 2), (3, 0)), ((1, 1),))[index]:
+            advance(step, stage)
+    for stage in range(3, len(bits) + 1):
         pass_on(0, stage)
 
     half_rows = rows // 2
@@ -248,10 +322,10 @@
         span = pl.ds(half * half_rows, half_rows)
         return pltpu.make_async_remote_copy(
             src_ref=att_ref.at[target, span],
-            dst_ref=cross_ref.at[level, span],
+            dst_ref=cross_ref.at[heads, span],
             send_sem=cross_send.at[target, half],
-            recv_sem=cross_land.at[level, half],
-            device_id={"tensor": target},
+            recv_sem=cross_land.at[heads, half],
+            device_id={"dp": even + group, "tensor": target},
         )
 
     turns = 2 * pairs * tps
@@ -259,7 +333,7 @@
     def attend(turn, carry):
         pair = lax.rem(turn, pairs)
         half = lax.rem(turn // pairs, 2)
-        target = lax.rem(level + 1 + turn // (2 * pairs), tps)
+        target = ordered(level, turn // (2 * pairs))
         span = pl.ds(pl.multiple_of(half * half_rows, half_rows), half_rows)
         lanes = pl.ds(pl.multiple_of(pair * PAIR, PAIR), PAIR)
         query = qkv_ref[target, span, lanes] * jnp.asarray(0.125, BF)
@@ -281,39 +355,56 @@
             [jnp.transpose(column)[:4] for column in columns], axis=0
         )
 
-        @pl.when((pair == pairs - 1) & (turn < 2 * pairs * (tps - 1)))
+        @pl.when((pair == pairs - 1) & ((turn < 2 * pairs * (tps - 1)) | (core != group)))
         def _():
             cross(target, half).start()
 
-        @pl.when(turn == turns // 2)
-        def _():
-            level_in(1)
-            pass_on(1, 0)
+        for at, batch in events.items():
+
+            @pl.when(turn == at)
+            def _():
+                for step, stage in batch:
+                    advance(step, stage)
 
         return carry
 
+    events = {1: [(3, 1)], turns // 4: [(1, 2), (2, 0)], turns // 2: [(3, 2)], turns - 4: [(2, 1)], turns - 1: [(2, 2)]}
+    early = [item for batch in events.values() for item in batch]
+    early = early + [item for batch in (((0, 1),), ((1, 0),), ((0, 2), (3, 0)), ((1, 1),)) for item in batch]
+    late = [
+        (step, stage)
+        for step in range(1, tps)
+        for stage in range(len(bits) + 1)
+        if (step, stage) not in early
+    ]
     lax.fori_loop(0, turns, attend, 0)
-    own_cross = pltpu.make_async_copy(att_ref.at[level], cross_ref.at[level], local_sem.at[3])
-    own_cross.start()
-    for step in range(2, tps):
-        level_in(step)
-        pass_on(step, 0)
-        for stage in range(1, len(bits) + 1):
-            pass_on(step - 1, stage)
-    for stage in range(1, len(bits) + 1):
-        pass_on(tps - 1, stage)
-    for step in range(1, tps):
-        other = lax.rem(level + step, tps)
+    own_cross = pltpu.make_async_copy(att_ref.at[level], cross_ref.at[heads], local_sem.at[3])
+
+    @pl.when(lead)
+    def _():
+        own_cross.start()
+
+    for step, stage in sorted(late, key=lambda item: (item[0] + item[1], item[0])):
+        advance(step, stage)
+    for index in range(tps):
         for half in range(2):
-            pltpu.make_async_remote_copy(
-                src_ref=att_ref.at[level, pl.ds(half * half_rows, half_rows)],
-                dst_ref=cross_ref.at[other, pl.ds(half * half_rows, half_rows)],
-                send_sem=cross_send.at[other, half],
-                recv_sem=cross_land.at[other, half],
-                device_id={"tensor": other},
-            ).wait_recv()
-            cross(other, half).wait_send()
-            to_level(step, half).wait_send()
+
+            @pl.when((core != group) | (index != heads))
+            def _():
+                pltpu.make_async_remote_copy(
+                    src_ref=att_ref.at[level, pl.ds(half * half_rows, half_rows)],
+                    dst_ref=cross_ref.at[index, pl.ds(half * half_rows, half_rows)],
+                    send_sem=cross_send.at[index, half],
+                    recv_sem=cross_land.at[index, half],
+                    device_id={"tensor": mate},
+                ).wait_recv()
+
+            @pl.when((core != group) | (index != level))
+            def _():
+                cross(index, half).wait_send()
+
+            if index:
+                to_level(index, half).wait_send()
     for step in range(tps):
         for half in range(2):
             for stage, block, targets in tables[half]:
@@ -321,17 +412,42 @@
                 for bit, number in targets:
                     in_plane(block, step, half, bit, number).wait_send()
     own_block.wait()
-    own_cross.wait()
-    for step in range(tps):
-        for chunk in range(CUTS):
-
-            @pl.when((level - step >= 0) & (level < tps - 1))
+    pack_to(0, place, {"dp": even + 1, "tensor": opposite}).wait_send()
+
+    @pl.when(core == 1)
+    def _():
+        pack_to(1, place, {"dp": even}).wait_send()
+
+    for block, index, bit in pack_sends:
+        pack_on(block, index, bit).wait_send()
+
+    @pl.when(lead)
+    def _():
+        own_cross.wait()
+
+    for chunk in range(CUTS):
+
+        @pl.when(core != group)
+        def _():
+            away(chunk).wait_send()
+
+        for index, block in enumerate((level, mate, near, far)):
+
+            @pl.when(lead)
             def _():
-                hop(level - step, chunk, True, step == 0).wait_send()
-
-            @pl.when((level + step < tps) & (level > 0))
-            def _():
-                hop(level + step, chunk, False, step == 0).wait_send()
+                to_core(block, chunk).wait_send()
+
+            if index == 0:
+
+                @pl.when(lead)
+                def _():
+                    to_mate(block, chunk).wait_send()
+
+            if index > 1:
+
+                @pl.when(lead & (gate == 1))
+                def _():
+                    to_mate(block, chunk).wait_send()
 
 
 def forward(tokens, pack, mine, dps, tps):
@@ -356,6 +472,7 @@
         ],
         scratch_shapes=[
             pltpu.VMEM((model, columns), BF),
+            dma((CUTS,)),
             dma((tps, CUTS)),
             dma((tps, CUTS)),
             dma((tps, CUTS)),
@@ -400,6 +517,7 @@
     dk_s,
     dv_s,
     land_s,
+    other_s,
     mine_s,
     theirs_s,
     gsum_s,
@@ -413,6 +531,8 @@
     local_sem,
     grad_send,
     grad_land,
+    core_send,
+    core_land,
     hop_send,
     hop_land,
     pack_send,
@@ -442,33 +562,44 @@
         packs_ref.at[:, pl.ds(0, piece)], weight_s, local_sem.at[0]
     )
     load_sum = pltpu.make_async_copy(gsum_ref, gsum_s, local_sem.at[1])
-    own_grad = pltpu.make_async_copy(cross_ref.at[level], grad_s.at[level], local_sem.at[2])
+    core, group, gate, mate, near, far, heads = seat(place, level)
+    lead = core == group
+    even = place - core
+    opposite = lax.rem(level + 2, tps)
+    own_grad = pltpu.make_async_copy(cross_ref.at[heads], grad_s.at[level], local_sem.at[2])
     load_weight.start()
     load_sum.start()
-    own_grad.start()
+
+    @pl.when(lead)
+    def _():
+        own_grad.start()
+
     greet(dps, tps)
 
-    def cross(step):
-        other = lax.rem(level + step, tps)
-        return pltpu.make_async_remote_copy(
-            src_ref=cross_ref.at[other],
+    def cross(index):
+        other = lax.rem(index // 2 + core, 2)
+        return pltpu.make_async_remote_copy(
+            src_ref=cross_ref.at[index],
             dst_ref=grad_s.at[level],
-            send_sem=grad_send.at[other],
+            send_sem=grad_send.at[index],
             recv_sem=grad_land.at[level],
-            device_id={"tensor": other},
-        )
-
-    def crossed(other):
-        return pltpu.make_async_remote_copy(
-            src_ref=cross_ref.at[other],
-            dst_ref=grad_s.at[other],
-            send_sem=grad_send.at[other],
-            recv_sem=grad_land.at[other],
-            device_id={"tensor": other},
-        )
-
-    for step in range(1, tps):
-        cross(step).start()
+            device_id={"dp": even + other, "tensor": lax.rem(index + 2 * other, tps)},
+        )
+
+    def crossed(block):
+        return pltpu.make_async_remote_copy(
+            src_ref=cross_ref.at[block],
+            dst_ref=grad_s.at[block],
+            send_sem=grad_send.at[block],
+            recv_sem=grad_land.at[block],
+            device_id={"tensor": mate},
+        )
+
+    for index in range(tps):
+
+        @pl.when((core != group) | (index != heads))
+        def _():
+            cross(index).start()
 
     def block_of(kind):
         block = place
@@ -571,15 +702,18 @@
 
     dk_s[...] = jnp.zeros_like(dk_s)
     dv_s[...] = jnp.zeros_like(dv_s)
-    own_grad.wait()
+
+    @pl.when(lead)
+    def _():
+        own_grad.wait()
 
     def attend(turn, carry):
         pair = lax.rem(turn, pairs)
         half = lax.rem(turn // pairs, 2)
         step = turn // (2 * pairs)
-        target = lax.rem(level + step, tps)
-
-        @pl.when((lax.rem(turn, 2 * pairs) == 0) & (step > 0))
+        target = ordered(level, tps - 1 - step)
+
+        @pl.when((lax.rem(turn, 2 * pairs) == 0) & ((step > 0) | (core != group)))
         def _():
             crossed(target).wait_recv()
 
@@ -649,45 +783,79 @@
             total = part if total is None else total + part
         return total
 
-    def hop(block, chunk, rightward):
-        slot = block + 1 if rightward else block
+    def to_core(block, chunk):
         span = pl.ds(chunk * cut, cut)
         return pltpu.make_async_remote_copy(
-            src_ref=land_s.at[slot, span],
-            dst_ref=land_s.at[slot, span],
-            send_sem=hop_send.at[slot, chunk],
+            src_ref=land_s.at[block, span],
+            dst_ref=land_s.at[block, span],
+            send_sem=core_send.at[block, chunk],
+            recv_sem=core_land.at[block, chunk],
+            device_id={"dp": flipped(place, 0)},
+        )
+
+    def onward(block, chunk, slot, device):
+        span = pl.ds(chunk * cut, cut)
+        return pltpu.make_async_remote_copy(
+            src_ref=land_s.at[block, span],
+            dst_ref=other_s.at[slot, span],
+            send_sem=hop_send.at[block, chunk],
             recv_sem=hop_land.at[slot, chunk],
-            device_id={"tensor": level + 1 if rightward else level - 1},
-        )
-
-    def begin(block, rightward):
-        land_s[block + 1 if rightward else block] = rows_of(block).astype(BF)
+            device_id={"tensor": device},
+        )
+
+    order_of = (far, near, mate, level)
+
+    def part_out(index):
+        block = order_of[index]
+        land_s[block] = rows_of(block).astype(BF)
         for chunk in range(CUTS):
-            hop(block, chunk, rightward).start()
-
-    def carry_on(block, rightward):
-        slot = block + 1 if rightward else block
+            to_core(block, chunk).start()
+
+    def chip_total(block, chunk, own):
+        to_core(block, chunk).wait_recv()
+        span = pl.ds(chunk * cut, cut)
+        return land_s[block, span].astype(F32) + own[chunk * cut : (chunk + 1) * cut]
+
+    def part_on(index):
+        block = order_of[index]
+        own = rows_of(block)
+        for chunk in range(CUTS):
+            land_s[block, pl.ds(chunk * cut, cut)] = chip_total(block, chunk, own).astype(BF)
+            onward(block, chunk, index, mate).start()
+
+    def part_through(index):
+        block = order_of[index]
         own = rows_of(block)
         for chunk in range(CUTS):
             span = pl.ds(chunk * cut, cut)
-            hop(block, chunk, rightward).wait_recv()
-            land_s[slot, span] = (
-                land_s[slot, span].astype(F32) + own[chunk * cut : (chunk + 1) * cut]
-            ).astype(BF)
-            hop(block, chunk, rightward).start()
-
-    for step in range(tps - 1, 0, -1):
-
-        @pl.when((level + step < tps) & (level == 0))
+            total = chip_total(block, chunk, own)
+            onward(block, chunk, index, block).wait_recv()
+            land_s[block, span] = (total + other_s[index, span].astype(F32)).astype(BF)
+            onward(block, chunk, 2, block).start()
+
+    def part_own():
+        own = rows_of(level)
+        for chunk in range(CUTS):
+            land_s[level, pl.ds(chunk * cut, cut)] = chip_total(level, chunk, own).astype(BF)
+
+    for index in range(tps):
+
+        @pl.when(core != group)
         def _():
-            begin(level + step, True)
-
-        @pl.when((level - step >= 0) & (level == tps - 1))
+            part_out(index)
+
+    outer = lead & (gate == 0)
+    inner = lead & (gate == 1)
+    for index in (0, 1):
+
+        @pl.when(outer)
         def _():
-            begin(level - step, False)
-
-    if scatter:
-        two_in(1)
+            part_on(index)
+
+    @pl.when(lead)
+    def _():
+        part_on(2)
+
     tail = jnp.concatenate(
         [jnp.sum(ref[...].astype(BF).astype(F32), axis=0, keepdims=True) for ref in refs], axis=1
     )
@@ -706,56 +874,89 @@
             device_id={"dp": flipped(place, bit)},
         )
 
-    order = bit_order(dps)[::-1]
+    plane = tuple(range(1, dps.bit_length() - 1))[::-1]
 
     def kept(done):
-        blocks = [place]
-        for bit in order[done:][::-1]:
+        blocks = [even, even + 1]
+        for bit in plane[done:][::-1]:
             blocks = blocks + [flipped(block, bit) for block in blocks]
         return blocks
 
     starts, at = [], 0
-    for done in range(len(order)):
+    for done in range(len(plane)):
         starts.append(at)
         at += dps >> (done + 1)
 
     def pack_start(done):
         for index, block in enumerate(kept(done + 1)):
-            exchange(starts[done] + index, order[done], flipped(block, order[done])).start()
+            exchange(starts[done] + index, plane[done], flipped(block, plane[done])).start()
 
     def pack_finish(done):
         for index, block in enumerate(kept(done + 1)):
-            exchange(starts[done] + index, order[done], block).wait()
+            exchange(starts[done] + index, plane[done], block).wait()
             mine_s[block] = (
                 mine_s[block].astype(F32) + theirs_s[starts[done] + index].astype(F32)
             ).astype(BF)
 
+    def pack_home(block, slot, device):
+        return pltpu.make_async_remote_copy(
+            src_ref=mine_s.at[block],
+            dst_ref=theirs_s.at[slot],
+            send_sem=pack_send.at[lax.rem(block, 2) + dps - 2],
+            recv_sem=pack_land.at[slot],
+            device_id=device,
+        )
+
+    def homeward():
+        @pl.when(core == 0)
+        def _():
+            pack_home(even + 1, dps - 1, {"dp": even + 1}).start()
+
+        @pl.when(core == 1)
+        def _():
+            pack_home(even, dps - 2, {"dp": even, "tensor": opposite}).start()
+            pack_home(even + 1, dps - 2, {"tensor": opposite}).start()
+
     pack_start(0)
-    for turn in range(max(tps - 1, len(order))):
-        step = tps - 1 - turn
+    if scatter:
+        two_in(1)
+        one_in(2)
+    for index in (0, 1):
+
+        @pl.when(inner)
+        def _():
+            part_through(index)
+
+    @pl.when(lead)
+    def _():
+        part_own()
+
+    stages = len(plane)
+    for turn in range(stages):
+        pack_finish(turn)
+        if turn + 1 < stages:
+            pack_start(turn + 1)
+        else:
+            homeward()
         if scatter and turn == 0:
-            one_in(2)
-        if step > 0:
-
-            @pl.when((level > 0) & (level + step < tps))
-            def _():
-                carry_on(level + step, True)
-
-            @pl.when((level < tps - 1) & (level - step >= 0))
-            def _():
-                carry_on(level - step, False)
-
-        if turn < len(order):
-            pack_finish(turn)
-            if turn + 1 < len(order):
-                pack_start(turn + 1)
-        if scatter and turn == 0:
+            one_in(3)
             two_in(2)
-            one_in(3)
-        if scatter and turn == 1:
-            two_in(3)
-    pack_out[...] = mine_s[place].astype(F32)
-    own = rows_of(level)
+    if scatter:
+        two_in(3)
+    pack_home(even, dps - 2, {"dp": even}).wait_recv()
+
+    @pl.when(core == 0)
+    def _():
+        pack_out[...] = mine_s[even].astype(F32) + theirs_s[dps - 2].astype(F32)
+        pack_home(even + 1, dps - 1, {"dp": even + 1}).wait_send()
+
+    @pl.when(core == 1)
+    def _():
+        pack_home(even, dps - 1, {"dp": even}).wait_recv()
+        pack_out[...] = theirs_s[dps - 1].astype(F32) + theirs_s[dps - 2].astype(F32)
+        pack_home(even, dps - 2, {"dp": even, "tensor": opposite}).wait_send()
+        pack_home(even + 1, dps - 2, {"tensor": opposite}).wait_send()
+
     load_sum.wait()
     if scatter:
         total = kept_s[(tps - 1) * 4 + 3].astype(F32)
@@ -764,30 +965,26 @@
             total = total + level_s[turn].astype(F32)
         feed_out[...] = total
     for chunk in range(CUTS):
-
-        @pl.when(level > 0)
+        onward(level, chunk, 2, mate).wait_recv()
+    total = gsum_s[...] + other_s[2].astype(F32)
+    tok_out[...] = (total + jnp.where(lead, land_s[level].astype(F32), 0.0)).astype(BF)
+    for index, block in enumerate(order_of):
+
+        @pl.when((core != group) | (index != heads))
         def _():
-            hop(level, chunk, True).wait_recv()
-
-        @pl.when(level < tps - 1)
-        def _():
-            hop(level, chunk, False).wait_recv()
-
-    total = gsum_s[...] + own
-    total = total + jnp.where(level > 0, land_s[level + 1].astype(F32), 0.0)
-    total = total + jnp.where(level < tps - 1, land_s[level].astype(F32), 0.0)
-    tok_out[...] = total.astype(BF)
-    for step in range(1, tps):
-        cross(step).wait_send()
+            cross(index).wait_send()
+
         for chunk in range(CUTS):
 
-            @pl.when(level + step < tps)
+            @pl.when(core != group)
             def _():
-                hop(level + step, chunk, True).wait_send()
-
-            @pl.when(level - step >= 0)
-            def _():
-                hop(level - step, chunk, False).wait_send()
+                to_core(block, chunk).wait_send()
+
+            if index < 3:
+
+                @pl.when(lead)
+                def _():
+                    onward(block, chunk, 2, mate).wait_send()
 
     if scatter:
         for turn in range(tps):
@@ -835,7 +1032,8 @@
             pltpu.VMEM((tps * rows, width), BF),
             pltpu.VMEM((tps * rows, width), F32),
             pltpu.VMEM((tps * rows, width), F32),
-            pltpu.VMEM((tps + 1, rows, model), BF),
+            pltpu.VMEM((tps, rows, model), BF),
+            pltpu.VMEM((3, rows, model), BF),
             pltpu.VMEM(packs.shape, BF),
             pltpu.VMEM(packs.shape, BF),
             pltpu.VMEM((rows, model), F32),
@@ -849,8 +1047,10 @@
             dma((3,)),
             dma((tps,)),
             dma((tps,)),
-            dma((tps + 1, CUTS)),
-            dma((tps + 1, CUTS)),
+            dma((tps, CUTS)),
+            dma((tps, CUTS)),
+            dma((tps, CUTS)),
+            dma((3, CUTS)),
             dma((dps,)),
             dma((dps,)),
             dma((slots,)),

time: 454 us -> 395 us (0.87)
  the two profiles are of different devices: /device:TPU:18 before, /device:TPU:0 now
where the time goes in v5:
time: 395 us; the launch traced here: 388 us
  Pallas kernels  366 us (93%)
  local copies, waits for them, and re-layouts  18.4 us (5%)
    pallas_call x1, Pallas kernels, forward(): pl.pallas_call(lambda *refs: forward_kernel(dps, tps, *refs), in_specs=[v...  160 us
    pallas_call x1, Pallas kernels, backward(): pl.pallas_call(lambda *refs: backward_kernel(dps, tps, scatter, *refs), i...  154 us
    pallas_call x1, Pallas kernels, middle(): pl.pallas_call(lambda *refs: middle_kernel((dps, tps, piece, chunks), *re...  50.1 us

profile of v5, /device:TPU:0, one launch (start us, length us, event | category | flops | bytes accessed | tf_op | source)
XLA Modules:
  0.0 387.6 jit_solution(8887159734777823291)
XLA Ops:
  0.7 0.7 pad_maximum_fusion
  1.6 0.8 stack.43
  2.4 0.6 pad.9.vec_ref
  3.0 0.9 fusion.1.refs_1_
  3.9 2.0 pack.1.refs_2_
  5.9 1.1 copy-done.1
  7.0 1.2 copy-done.3
  8.2 160.3 %forward.1 = (bf16[4,512,1024]{2,1,0:T(8,128)(2,1)}, bf16[8,144,768]{2,1,0:T(8,128)(2,1)}, bf16[4,512,768]{2,1,0:T(8,128)(2,1)}, bf16[4,512,256]{2,1,0:T(8,128)(...) custom-call(bf16[512,1024]{1,0:T(8,128)(2,1)S(1)} %copy-done.3, ...), custom_call_target="tpu_custom_call" | custom-call | flops 3221225472 | bytes 209715200 | tf_op jit(solution)/shard_map/forward/pallas_call | solution.py:460
  168.5 1.0 copy-done
  169.5 0.7 copy-done.2
  170.1 1.0 copy-done.4
  171.1 50.1 %middle.1 = (bf16[512,1024]{1,0:T(8,128)(2,1)}, f32[512,1024]{1,0:T(8,128)}, bf16[4,512,256]{2,1,0:T(8,128)(2,1)}, bf16[8,4,304,1024]{3,2,1,0:T(8,128)(2,1)}) custom-call(bf16[4,512,256]{2,1,0:T(8,128)(2,1)} %copy-done.4, bf16[512,1024]{1,0:T(8,128)(2,1)} %refs_1_.1, bf16[512,1024]{1,0:T(8,128)(2,1)} %refs_2_.1, ...), custom_call_target="tpu_custom_call" | custom-call | flops 28991029248 | bytes 62914560 | tf_op jit(solution)/shard_map/middle/pallas_call | solution.py:1304
  221.2 154.0 %backward.1 = (bf16[512,1024]{1,0:T(8,128)(2,1)}, f32[144,768]{1,0:T(8,128)}, f32[304,1024]{1,0:T(8,128)}) custom-call(bf16[4,512,256]{2,1,0:T(8,128)(2,1)} %get-tuple-element.34.refs_0_, bf16[8,4,304,1024]{3,2,1,0:T(8,128)(2,1)} %get-tuple-element.35.refs_1_, bf16[4,512,768]{2,1,0:T(8,128)(2,1)} %get-tuple-element.36.refs_2_, bf16[4,512,256]{2,1,0:T(8,128)(2,1)} %copy-done, ...), custom_call_target="tpu_custom_call" | custom-call | flops 6442450944 | bytes 209715200 | tf_op jit(solution)/shard_map/backward/pallas_call | solution.py:1020
  375.2 0.7 fusion.13
  375.9 1.8 fusion.14
  377.7 0.6 fusion.3
  378.3 1.0 fusion.12
  379.3 0.5 fusion.11
  379.8 0.5 fusion.9
  381.4 0.9 slice.56
  382.3 2.1 slice_bitcast_fusion
  384.4 1.0 copy.38
  385.4 0.8 copy.37
  386.1 1.0 copy.45
  (18 shorter events, 1.3 us)
Async XLA Ops:
  5.9 1.1 copy-start.1
  7.0 1.2 copy-start.3
  168.5 1.0 copy-start
  169.5 0.7 copy-start.2
  170.1 1.0 copy-start.4
  377.7 8.5 %copy-start.5 = (bf16[512,1024]{1,0:T(8,128)(2,1)S(1)}, bf16[512,1024]{1,0:T(8,128)(2,1)}, u32[]{:S(2)}) copy-start(bf16[512,1024]{1,0:T(8,128)(2,1)} %get-tuple-element.121) | copy-start | bytes 3145732
